TPU v7x, 512 devices: a whole 4x4x16 slice. The times are simulated.
512 devices in a mesh: seg: 128 (over y, z, core), sp: 4 (over x).
Axes of the slice: x: 4, y: 4, z: 16, core: 2. Of those that a mesh axis runs over, the one named last changes fastest.
Arguments:
- coeffs: float32 [8, 2048, 680], P('sp', 'seg'), may hold values from -0.6 to 0.6
- points: float32 [3, 2048, 768], P(None, 'seg'), may hold values from -1 to 1
- owner_leaf: int32 [2048, 6], P('seg'), may hold values from 0 to 2047, as said below
- reaction: float32 [8, 8], replicated, may hold values from -2 to 2
- fit_matrix: float32 [768, 680], replicated, may hold values from -0.21875 to 0.21875
- new_seg: int32 [2048], replicated, may hold values from 0 to 127, as said below
- near_src: int32 [2048, 16], replicated, may hold values from -1 to 2047, as said below
- near_op: int32 [2048, 16], replicated, may hold values from 0 to 1
- near_mat: bfloat16 [2, 680, 680], replicated, may hold values from -0.0546875 to 0.0546875
- up_mat: bfloat16 [680, 152], replicated, may hold values from -0.21875 to 0.21875
- far_src: int32 [2048, 8], replicated, may hold values from -1 to 2047, as said below
- trans_mat: bfloat16 [8, 152, 152], replicated, may hold values from -0.15625 to 0.15625
- down_mat: bfloat16 [152, 680], replicated, may hold values from -0.5 to 0.5
Outputs:
- updated: float32 [8, 3072, 680], P('sp', 'seg')
Inputs may be any that keep to these rules, and one draw needn't show every extreme that they name: `owner_leaf`: of the 96 blocks of one segment's leaves, at most 2 have their owner among the 16 leaves of any one segment. `new_seg`: never falls along the leaves; leaf t goes to segment t // 16, or to the one before only if t % 16 < 4, or to the one after only if t % 16 >= 12. `near_src`: -1 marks an unused entry; any other entry differs from its row's leaf index by at most 4. `far_src`: -1 marks an absent interaction.
All inputs are finite; a program needn't handle non-finite values.
Results may differ from a plain program's by a relative error of at most 0.0035.
Values may be sent and summed in bfloat16 or wider, within the bound.
No kernel may reach another device: no remote copies, remote signals or barrier semaphores. Data moves between devices by JAX's collectives and lax.ppermute only.
A program may use at most 64 MiB of HBM per device.

v0:
```python
import jax
import jax.numpy as jnp
import numpy as np
from jax import lax
from jax.sharding import Mesh
from jax.sharding import PartitionSpec as P

ORDER = 14
NODES = 768
PB = 128
BLOCKS = 6
MOVE = 4
REACH = 4
SEG = ("seg_0", "seg_1", "seg_2")


precise = lax.Precision.HIGHEST


def split_up(value, dim, length):
    before, after = (value.shape[:dim], value.shape[dim + 1 :])
    return jnp.moveaxis(value.reshape(*before, length, -1, *after), dim, 0)


def joined_along(pieces, dim):
    lengths = list(pieces.shape[1:])
    lengths[dim] *= pieces.shape[0]
    return jnp.moveaxis(pieces, 0, dim).reshape(lengths)


def moved_by_axis(pieces, axes, turns):
    inside = pieces.shape[1:]
    filled = pieces.reshape(*(lax.axis_size(a) for a in axes), *inside)
    for k in turns:
        filled = lax.all_to_all(filled, axes[k], k, k, tiled=True)
    return filled.reshape(-1, *inside)


def core_and_chips(value, groups, turns, split_dim, concat_dim):
    length = lax.axis_size(groups[0]) * lax.axis_size(groups[1])
    pieces = split_up(value, split_dim, length)
    return joined_along(moved_by_axis(pieces, groups, turns), concat_dim)


def extended(value, sides, width):
    for axis, dim in sides:
        size, length = (lax.axis_size(axis), value.shape[dim])
        up = [(i, (i + 1) % size) for i in range(size - 1)]
        down = [(j, i) for i, j in up]
        last = lax.slice_in_dim(value, length - width, length, axis=dim)
        first = lax.slice_in_dim(value, 0, width, axis=dim)
        before = lax.ppermute(last, axis, up)
        after = lax.ppermute(first, axis, down)
        value = jnp.concatenate([before, value, after], axis=dim)
    return value


def gather_in_order(value, axes, turns):
    pieces = value
    for k in turns:
        pieces = lax.all_gather(pieces, axes[k])
    done = turns[::-1]
    back = [done.index(k) for k in range(len(axes))]
    pieces = pieces.transpose(*back, *range(len(axes), pieces.ndim))
    return pieces.reshape(-1, *value.shape)


def gathered_by_axis(value, axes, turns, dim):
    return joined_along(gather_in_order(value, axes, turns), dim)


def basis_tables(order):
    pair_list = [(deg_x, deg_y) for deg_x in range(order + 1) for deg_y in range(order + 1 - deg_x)]
    total_width = (order + 1) * (order + 2) * (order + 3) // 6
    lookup = np.full((len(pair_list), order + 1), total_width, np.int32)
    x_select = np.zeros((len(pair_list), order + 1), np.float32)
    y_select = np.zeros((len(pair_list), order + 1), np.float32)
    counter = 0
    for row_number, (deg_x, deg_y) in enumerate(pair_list):
        x_select[row_number, deg_x] = 1.0
        y_select[row_number, deg_y] = 1.0
        for deg_z in range(order + 1 - deg_x - deg_y):
            lookup[row_number, deg_z] = counter
            counter += 1
    return (lookup, x_select, y_select)


def chebyshev(position_values, order):
    polynomials = [jnp.ones_like(position_values), position_values]
    for degree in range(2, order + 1):
        polynomials.append(2.0 * position_values * polynomials[-1] - polynomials[-2])
    return jnp.stack(polynomials[: order + 1], axis=-2)


def evaluate(coefficient, coords):
    lookup, x_select, y_select = basis_tables(ORDER)
    padded = jnp.concatenate(
        [coefficient, jnp.zeros(coefficient.shape[:-1] + (1,), coefficient.dtype)], axis=-1
    )
    dense_coef = jnp.take(padded, jnp.asarray(lookup), axis=-1)
    along_x = chebyshev(coords[0], ORDER)
    along_y = chebyshev(coords[1], ORDER)
    along_z = chebyshev(coords[2], ORDER)
    inner_sum = jnp.einsum("sqk,kp->sqp", dense_coef, along_z, precision=precise)
    y_rows = jnp.einsum("qk,kp->qp", jnp.asarray(y_select), along_y, precision=precise)
    folded = jnp.einsum(
        "sqp,qk->skp", inner_sum * y_rows[None], jnp.asarray(x_select), precision=precise
    )
    return jnp.sum(folded * along_x[None], axis=1)


def evaluate_many(coef_rows, coords):
    return lax.map(
        lambda block_args: evaluate(block_args[0], block_args[1]),
        (coef_rows, coords),
        batch_size=16,
    )


def shards(
    coeffs,
    points,
    owner_leaf,
    reaction,
    fit_matrix,
    new_seg,
    near_src,
    near_op,
    near_mat,
    up_mat,
    far_src,
    trans_mat,
    down_mat,
):
    local_species, leaf_dev, coef_width = coeffs.shape
    segments = lax.axis_size(SEG)
    segment = lax.axis_index(SEG)
    block_count = leaf_dev * BLOCKS
    capacity = max(2, 2 * block_count // segments)
    coords = points.reshape(3, block_count, PB).transpose(1, 0, 2)
    flat_owner = owner_leaf.reshape(-1)
    target_dev = flat_owner // leaf_dev
    owned_leaf = flat_owner % leaf_dev
    onehot = (target_dev[:, None] == jnp.arange(segments, dtype=jnp.int32)[None, :]).astype(
        jnp.int32
    )
    earlier = jnp.sum((jnp.cumsum(onehot, axis=0) - onehot) * onehot, axis=1)
    position = target_dev * capacity + earlier
    by_leaf = jnp.transpose(coeffs, (1, 0, 2))
    slot_leaf = jnp.full((segments * capacity,), -1, jnp.int32).at[position].set(owned_leaf)
    received = core_and_chips(
        slot_leaf.reshape(segments, capacity), (("seg_0", "seg_1"), "seg_2"), (1, 0), 0, 0
    )
    sources, item_count = received.shape
    wanted = received.reshape(-1)
    picked = jnp.take(by_leaf, jnp.clip(wanted, 0, leaf_dev - 1), axis=0)
    picked = jnp.where((wanted >= 0)[:, None, None], picked, jnp.zeros_like(picked))
    fetched = lax.all_to_all(
        picked.reshape(sources, item_count, local_species, coef_width),
        SEG,
        split_axis=0,
        concat_axis=0,
        tiled=True,
    )
    values = evaluate_many(
        fetched.reshape(segments * capacity, local_species, coef_width)[position], coords
    )
    values = (
        values.reshape(leaf_dev, BLOCKS, local_species, PB)
        .transpose(2, 0, 1, 3)
        .reshape(local_species, leaf_dev, NODES)
    )
    gathered = lax.all_gather(values, "sp", axis=0, tiled=True)
    species_start = lax.axis_index("sp") * local_species
    my_rows = lax.dynamic_slice_in_dim(reaction, species_start, local_species, 0)
    mixing = jnp.einsum("sr,rln->sln", my_rows, gathered, precision=precise)
    reacted = values + jnp.tanh(mixing)
    refitted = jnp.einsum("sln,nc->slc", reacted, fit_matrix, precision=precise)
    ghosts = refitted.astype(jnp.bfloat16)
    equivalent = jnp.einsum(
        "slc,cq->slq", ghosts, up_mat, preferred_element_type=jnp.float32
    ).astype(jnp.bfloat16)
    margin = MOVE + REACH
    padded = extended(ghosts, ((SEG, 1),), margin)
    slot_total = leaf_dev + 2 * MOVE
    leaf_total = new_seg.shape[0]
    target = segment * leaf_dev - MOVE + jnp.arange(slot_total, dtype=jnp.int32)
    inside = (target >= 0) & (target < leaf_total)
    clipped = jnp.clip(target, 0, leaf_total - 1)
    live_slot = inside & (new_seg[clipped] == segment)
    own_term = padded[:, margin - MOVE : margin - MOVE + slot_total].astype(jnp.float32)
    near_from = near_src[clipped]
    near_kind = near_op[clipped]
    near_ok = live_slot[:, None] & (near_from >= 0)
    near_count = near_from.shape[1]
    offset_rows = jnp.clip(near_from - (segment * leaf_dev - margin), 0, leaf_dev + 2 * margin - 1)
    picked = jnp.take(padded, offset_rows.reshape(-1), axis=1).reshape(
        local_species, slot_total, near_count, coef_width
    )
    operators = jnp.arange(near_mat.shape[0], dtype=jnp.int32)
    choose = ((near_kind[None, :, :] == operators[:, None, None]) & near_ok[None, :, :]).astype(
        jnp.bfloat16
    )
    grouped = jnp.einsum("ojq,sjqc->osjc", choose, picked, preferred_element_type=jnp.float32)
    near_term = jnp.einsum(
        "osjc,ocd->sjd", grouped, near_mat.astype(jnp.float32), precision=precise
    )
    far_from = far_src[clipped]
    far_ok = live_slot[:, None] & (far_from >= 0)
    empty_rows = jnp.zeros(
        (local_species, slot_total, far_from.shape[1], up_mat.shape[1]), jnp.bfloat16
    )
    block_piece = gathered_by_axis(equivalent, SEG, (0, 1, 2), 1)
    piece_rows = block_piece.shape[1]
    in_piece = far_ok & (far_from >= 0) & (far_from < piece_rows)
    taken_rows = jnp.take(block_piece, jnp.clip(far_from, 0, piece_rows - 1).reshape(-1), axis=1)
    taken_rows = taken_rows.reshape(empty_rows.shape)
    far_rows = empty_rows + jnp.where(
        in_piece[None, :, :, None], taken_rows, jnp.zeros_like(taken_rows)
    )
    local_expansion = jnp.einsum(
        "sjoq,oqr->sjr", far_rows, trans_mat, preferred_element_type=jnp.float32
    ).astype(jnp.bfloat16)
    far_term = jnp.einsum(
        "sjq,qc->sjc", local_expansion, down_mat, preferred_element_type=jnp.float32
    )
    total = own_term + near_term + far_term
    return jnp.where(live_slot[None, :, None], total, jnp.zeros_like(total))


def solution(mesh):
    torus = Mesh(
        mesh.devices.reshape(4, 16, 2, mesh.shape["sp"]), ("seg_0", "seg_1", "seg_2", "sp")
    )
    return jax.shard_map(
        shards,
        mesh=torus,
        in_specs=(
            P("sp", SEG, None),
            P(None, SEG, None),
            P(SEG, None),
            P(),
            P(),
            P(),
            P(),
            P(),
            P(),
            P(),
            P(),
            P(),
            P(),
        ),
        out_specs=P("sp", SEG, None),
        check_vma=False,
    )
```

profile of v0, /device:TPU:1, one launch (start us, length us, event | category | flops | bytes accessed | tf_op | source)
XLA Modules:
  0.0 371.4 jit_solution(11442974668432837675)
XLA Ops:
  9.3 10.2 %all_to_all.15 = s32[2,1,128]{2,1,0:T(1,128)S(1)} all-to-all(s32[2,1,128]{2,1,0:T(1,128)S(1)} %reshape.454), channel_id=1, replica_groups=mesh['seg_0'=4,'seg_1'=16,'seg_2'=2,'sp'=4] {'seg_2'}, dimensions={0} | all-to-all | bytes 2048 | tf_op jit(solution)/shard_map/all_to_all | solution.py:35
  21.5 13.1 %all-to-all-start.1 = ((s32[64,2,1,2]{3,1,2,0:T(2,128)}), s32[64,2,1,2]{3,1,2,0:T(2,128)S(1)}, u32[]{:S(2)}, u32[]{:S(2)}) async-start(s32[64,2,1,2]{3,1,2,0:T(2,128)} %copy.129), calls=%async_computation.1 | async-start | bytes 131072 | tf_op jit(solution)/shard_map/all_to_all | solution.py:35
  35.6 12.5 %all-to-all-done.1 = s32[64,2,1,2]{3,1,2,0:T(2,128)S(1)} async-done(((s32[64,2,1,2]{3,1,2,0:T(2,128)}), s32[64,2,1,2]{3,1,2,0:T(2,128)S(1)}, u32[]{:S(2)}, u32[]{:S(2)}) %all-to-all-start.1) | async-done | bytes 1056 | tf_op jit(solution)/shard_map/all_to_all | solution.py:35
  48.5 3.4 gather_fusion.2
  51.9 3.1 select_select_fusion
  55.0 8.3 %all-to-all-start.2 = ((f32[128,2,2,680]{3,2,1,0:T(2,128)}), f32[128,2,2,680]{3,2,1,0:T(2,128)}, u32[]{:S(2)}, u32[]{:S(2)}) async-start(f32[128,2,2,680]{3,2,1,0:T(2,128)} %select_select_fusion), calls=%async_computation.2 | async-start | bytes 3145728 | tf_op jit(solution)/shard_map/all_to_all | solution.py:158
  65.5 1.2 copy.143
  67.6 72.3 %all-to-all-done.2 = f32[128,2,2,680]{3,2,1,0:T(2,128)} async-done(((f32[128,2,2,680]{3,2,1,0:T(2,128)}), f32[128,2,2,680]{3,2,1,0:T(2,128)}, u32[]{:S(2)}, u32[]{:S(2)}) %all-to-all-start.2) | async-done | bytes 1392672 | tf_op jit(solution)/shard_map/all_to_all | solution.py:158
  139.8 2.7 gather_fusion.3
  142.5 118.4 %while.14 = (s32[]{:T(128)}, f32[6,16,2,128]{3,2,1,0:T(2,128)}, f32[6,16,2,680]{3,2,1,0:T(2,128)S(1)}, f32[6,16,3,128]{3,1,0,2:T(8,128)S(1)}, s32[]{:T(128)}, /*...) while((s32[]{:T(128)}, f32[6,16,2,128]{3,2,1,0:T(2,128)}, ...), condition=%wide.region_5.6_spmd.clone, body=%wide.region_3.5_spmd.sunk.clone.sunk | while | flops 222994432 | bytes 17342592 | solution.py:113
  145.1 6.4 %gather_fusion = f32[1800,16,2]{1,2,0:T(2,128)} fusion(f32[16,2,681]{0,1,2:T(2,128)S(1)} %concatenate.10, s32[2048]{0:T(1024)S(1)} %pad_clamp_fusion.7), kind=kCustom, calls=%fused_computation.clone.1 | custom fusion | bytes 468000 | tf_op jit(solution)/shard_map/while/body/eval_jaxpr/vmap(jit(_take))/gather | solution.py:100
  151.6 4.4 %copy.201 = f32[120,15,16,2]{1,0,3,2:T(8,128)} copy(f32[120,15,16,2]{2,3,1,0:T(2,128)} %bitcast.140) | data formatting | bytes 460800 | tf_op jit(solution)/shard_map/while/body/eval_jaxpr/vmap(jit(_take))/gather | solution.py:100
  155.9 3.4 fusion.97
  160.4 1.2 fusion.98
  164.8 6.4 %gather_fusion = f32[1800,16,2]{1,2,0:T(2,128)} fusion(f32[16,2,681]{0,1,2:T(2,128)S(1)} %concatenate.10, s32[2048]{0:T(1024)S(1)} %pad_clamp_fusion.7), kind=kCustom, calls=%fused_computation.clone.1 | custom fusion | bytes 468000 | tf_op jit(solution)/shard_map/while/body/eval_jaxpr/vmap(jit(_take))/gather | solution.py:100
  171.3 4.4 %copy.201 = f32[120,15,16,2]{1,0,3,2:T(8,128)} copy(f32[120,15,16,2]{2,3,1,0:T(2,128)} %bitcast.140) | data formatting | bytes 460800 | tf_op jit(solution)/shard_map/while/body/eval_jaxpr/vmap(jit(_take))/gather | solution.py:100
  175.7 3.4 fusion.97
  180.2 1.2 fusion.98
  184.6 6.4 %gather_fusion = f32[1800,16,2]{1,2,0:T(2,128)} fusion(f32[16,2,681]{0,1,2:T(2,128)S(1)} %concatenate.10, s32[2048]{0:T(1024)S(1)} %pad_clamp_fusion.7), kind=kCustom, calls=%fused_computation.clone.1 | custom fusion | bytes 468000 | tf_op jit(solution)/shard_map/while/body/eval_jaxpr/vmap(jit(_take))/gather | solution.py:100
  191.0 4.4 %copy.201 = f32[120,15,16,2]{1,0,3,2:T(8,128)} copy(f32[120,15,16,2]{2,3,1,0:T(2,128)} %bitcast.140) | data formatting | bytes 460800 | tf_op jit(solution)/shard_map/while/body/eval_jaxpr/vmap(jit(_take))/gather | solution.py:100
  195.4 3.4 fusion.97
  199.9 1.2 fusion.98
  204.3 6.4 %gather_fusion = f32[1800,16,2]{1,2,0:T(2,128)} fusion(f32[16,2,681]{0,1,2:T(2,128)S(1)} %concatenate.10, s32[2048]{0:T(1024)S(1)} %pad_clamp_fusion.7), kind=kCustom, calls=%fused_computation.clone.1 | custom fusion | bytes 468000 | tf_op jit(solution)/shard_map/while/body/eval_jaxpr/vmap(jit(_take))/gather | solution.py:100
  210.7 4.4 %copy.201 = f32[120,15,16,2]{1,0,3,2:T(8,128)} copy(f32[120,15,16,2]{2,3,1,0:T(2,128)} %bitcast.140) | data formatting | bytes 460800 | tf_op jit(solution)/shard_map/while/body/eval_jaxpr/vmap(jit(_take))/gather | solution.py:100
  215.1 3.4 fusion.97
  219.6 1.2 fusion.98
  224.0 6.4 %gather_fusion = f32[1800,16,2]{1,2,0:T(2,128)} fusion(f32[16,2,681]{0,1,2:T(2,128)S(1)} %concatenate.10, s32[2048]{0:T(1024)S(1)} %pad_clamp_fusion.7), kind=kCustom, calls=%fused_computation.clone.1 | custom fusion | bytes 468000 | tf_op jit(solution)/shard_map/while/body/eval_jaxpr/vmap(jit(_take))/gather | solution.py:100
  230.4 4.4 %copy.201 = f32[120,15,16,2]{1,0,3,2:T(8,128)} copy(f32[120,15,16,2]{2,3,1,0:T(2,128)} %bitcast.140) | data formatting | bytes 460800 | tf_op jit(solution)/shard_map/while/body/eval_jaxpr/vmap(jit(_take))/gather | solution.py:100
  234.8 3.4 fusion.97
  239.3 1.2 fusion.98
  243.7 6.4 %gather_fusion = f32[1800,16,2]{1,2,0:T(2,128)} fusion(f32[16,2,681]{0,1,2:T(2,128)S(1)} %concatenate.10, s32[2048]{0:T(1024)S(1)} %pad_clamp_fusion.7), kind=kCustom, calls=%fused_computation.clone.1 | custom fusion | bytes 468000 | tf_op jit(solution)/shard_map/while/body/eval_jaxpr/vmap(jit(_take))/gather | solution.py:100
  250.2 4.4 %copy.201 = f32[120,15,16,2]{1,0,3,2:T(8,128)} copy(f32[120,15,16,2]{2,3,1,0:T(2,128)} %bitcast.140) | data formatting | bytes 460800 | tf_op jit(solution)/shard_map/while/body/eval_jaxpr/vmap(jit(_take))/gather | solution.py:100
  254.5 3.4 fusion.97
  259.0 1.2 fusion.98
  261.9 11.1 %all_gather.21 = f32[8,16,768]{2,1,0:T(8,128)S(1)} all-gather(f32[2,16,768]{2,1,0:T(8,128)S(1)} %reshape.349), channel_id=1, replica_groups=mesh['seg_0'=4,'seg_1'=16,'seg_2'=2,'sp'=4] {'sp'}, dimensions={0}, use_global_device_ids=true | all-gather | bytes 491520 | tf_op jit(solution)/shard_map/all_gather | solution.py:173
  273.0 1.3 fusion.34
  274.3 3.5 fusion.26
  278.0 9.5 %all-gather = bf16[8,16,152]{2,1,0:T(8,128)(2,1)S(1)} all-gather(bf16[2,16,152]{2,1,0:T(8,128)(2,1)S(1)} %convolution_convert_fusion), channel_id=2, replica_groups=mesh['seg_0'=4,'seg_1'=16,'seg_2'=2,'sp'=4] {'seg_0'}, dimensions={0}, use_global_device_ids=true | all-gather | bytes 48640 | tf_op jit(solution)/shard_map/all_gather | solution.py:61
  287.5 27.9 %all-gather.1 = bf16[64,2,16,152]{3,2,1,0:T(8,128)(2,1)} all-gather(bf16[4,2,16,152]{3,2,1,0:T(8,128)(2,1)S(1)} %bitcast.154), channel_id=3, replica_groups=mesh['seg_0'=4,'seg_1'=16,'seg_2'=2,'sp'=4] {'seg_1'}, dimensions={0}, use_global_device_ids=true | all-gather | bytes 661504 | tf_op jit(solution)/shard_map/all_gather | solution.py:61
  315.5 17.0 %collective-permute-start = (bf16[2,8,680]{2,1,0:T(8,128)(2,1)S(1)}, bf16[2,8,680]{2,1,0:T(8,128)(2,1)S(1)}, u32[]{:S(2)}, u32[]{:S(2)}) collective-permute-start(bf16[2,8,680]{2,1,0:T(8,128)(2,1)S(1)} %get-tuple-element.198), channel_id=1, source_target_pairs={{0,4},{4,8},{8,12},{12,16},{16,20},{20,24},{24,28},{28,32},{32,36}... | collective-permute-start | bytes 65288 | tf_op jit(solution)/shard_map/ppermute | solution.py:52
  332.5 2.1 collective-permute-start.1
  335.6 2.1 collective-permute-done.1
  337.8 4.5 %gather_fusion.5 = bf16[384,2,680]{2,1,0:T(2,128)(2,1)S(1)} fusion(bf16[2,32,680]{2,0,1:T(2,128)(2,1)S(1)} %copy.139, s32[1024]{0:T(1024)S(1)} %pad_clamp_fusion.2), kind=kCustom, calls=%fused_computation.5 | custom fusion | bytes 2090496 | tf_op jit(solution)/shard_map/jit(_take)/gather | solution.py:197
  342.7 1.1 fusion.23
  344.6 1.8 copy.147
  346.6 14.0 %copy.150 = bf16[2,2048,152]{2,0,1:T(2,128)(2,1)} copy(bf16[2,2048,152]{2,1,0:T(8,128)(2,1)S(1)} %bitcast.144) | data formatting | bytes 2490368 | tf_op jit(solution)/shard_map/reshape | solution.py:28
  360.6 2.6 gather_fusion.8
  363.3 1.2 add_select_fusion
  (411 shorter events, 36.5 us)
Async XLA Ops:
  6.5 336.1 %copy-start = (bf16[2,680,680]{2,1,0:T(8,128)(2,1)S(1)}, bf16[2,680,680]{2,1,0:T(8,128)(2,1)}, u32[]{:S(2)}) copy-start(bf16[2,680,680]{2,1,0:T(8,128)(2,1)} %param.26) | copy-start | bytes 5548804
  21.5 26.6 %all-to-all-start.1 = ((s32[64,2,1,2]{3,1,2,0:T(2,128)}), s32[64,2,1,2]{3,1,2,0:T(2,128)S(1)}, u32[]{:S(2)}, u32[]{:S(2)}) async-start(s32[64,2,1,2]{3,1,2,0:T(2,128)} %copy.129), calls=%async_computation.1 | async-start | bytes 131072 | tf_op jit(solution)/shard_map/all_to_all | solution.py:35
  55.0 8.6 %copy-start.16 = (f32[3,16,768]{2,1,0:T(8,128)S(1)}, f32[3,16,768]{2,1,0:T(8,128)}, u32[]{:S(2)}) copy-start(f32[3,16,768]{2,1,0:T(8,128)} %param.19) | copy-start | bytes 442372
  55.0 8.6 %copy-start.17 = (s32[2048,16]{0,1:T(8,128)S(1)}, s32[2048,16]{0,1:T(8,128)}, u32[]{:S(2)}) copy-start(s32[2048,16]{0,1:T(8,128)} %param.24) | copy-start | bytes 393220
  55.0 9.1 %copy-start.1 = (s32[2048]{0:T(1024)S(1)}, s32[2048]{0:T(1024)}, u32[]{:S(2)}) copy-start(s32[2048]{0:T(1024)} %param.23) | copy-start | bytes 24580
  55.0 84.8 %all-to-all-start.2 = ((f32[128,2,2,680]{3,2,1,0:T(2,128)}), f32[128,2,2,680]{3,2,1,0:T(2,128)}, u32[]{:S(2)}, u32[]{:S(2)}) async-start(f32[128,2,2,680]{3,2,1,0:T(2,128)} %select_select_fusion), calls=%async_computation.2 | async-start | bytes 3145728 | tf_op jit(solution)/shard_map/all_to_all | solution.py:158
  63.4 281.3 %all-gather.5.cloned.1.call-start = ((), (), s32[]{:S(2)}) async-start(), calls=%async_computation.3 | async-start | bytes 3145728 | tf_op jit(solution)/shard_map/all_gather | solution.py:61
  63.7 78.8 %copy-start.13 = (f32[120,15,1,1]{0,1,3,2:T(8,128)S(1)}, f32[120,15,1,1]{0,1,3,2:T(8,128)}, u32[]{:S(2)}) copy-start(f32[120,15,1,1]{0,1,3,2:T(8,128)} %constant.614) | copy-start | bytes 21604
  63.7 78.8 %copy-start.14 = (f32[120,15,1]{0,1,2:T(8,128)S(1)}, f32[120,15,1]{0,1,2:T(8,128)}, u32[]{:S(2)}) copy-start(f32[120,15,1]{0,1,2:T(8,128)} %constant.616) | copy-start | bytes 21604
  63.7 78.8 %copy-start.15 = (s32[1800]{0:T(1024)S(1)}, s32[1800]{0:T(1024)}, u32[]{:S(2)}) copy-start(s32[1800]{0:T(1024)} %constant.615) | copy-start | bytes 21604
  142.5 2.3 copy-start.8
  151.6 4.4 %copy-start.3 = (f32[16,15,128]{2,0,1:T(8,128)S(1)}, f32[16,15,128]{2,0,1:T(8,128)}, u32[]{:S(2)}) copy-start(f32[16,15,128]{2,0,1:T(8,128)} %copy-done.2) | copy-start | bytes 368644 | tf_op jit(solution)/shard_map/while
  155.9 3.4 copy-start.5
  155.9 4.4 %copy-start.7 = (f32[16,15,128]{2,0,1:T(8,128)S(1)}, f32[16,15,128]{2,0,1:T(8,128)}, u32[]{:S(2)}) copy-start(f32[16,15,128]{2,0,1:T(8,128)} %copy-done.6) | copy-start | bytes 368644 | tf_op jit(solution)/shard_map/while
  160.3 1.9 copy-start.9
  160.4 1.9 copy-start.11
  162.3 2.3 copy-start.8
  171.3 4.4 %copy-start.3 = (f32[16,15,128]{2,0,1:T(8,128)S(1)}, f32[16,15,128]{2,0,1:T(8,128)}, u32[]{:S(2)}) copy-start(f32[16,15,128]{2,0,1:T(8,128)} %copy-done.2) | copy-start | bytes 368644 | tf_op jit(solution)/shard_map/while
  175.6 3.4 copy-start.5
  175.6 4.4 %copy-start.7 = (f32[16,15,128]{2,0,1:T(8,128)S(1)}, f32[16,15,128]{2,0,1:T(8,128)}, u32[]{:S(2)}) copy-start(f32[16,15,128]{2,0,1:T(8,128)} %copy-done.6) | copy-start | bytes 368644 | tf_op jit(solution)/shard_map/while
  180.1 1.9 copy-start.9
  182.0 2.3 copy-start.8
  191.0 4.4 %copy-start.3 = (f32[16,15,128]{2,0,1:T(8,128)S(1)}, f32[16,15,128]{2,0,1:T(8,128)}, u32[]{:S(2)}) copy-start(f32[16,15,128]{2,0,1:T(8,128)} %copy-done.2) | copy-start | bytes 368644 | tf_op jit(solution)/shard_map/while
  195.4 3.4 copy-start.5
  195.4 4.5 %copy-start.7 = (f32[16,15,128]{2,0,1:T(8,128)S(1)}, f32[16,15,128]{2,0,1:T(8,128)}, u32[]{:S(2)}) copy-start(f32[16,15,128]{2,0,1:T(8,128)} %copy-done.6) | copy-start | bytes 368644 | tf_op jit(solution)/shard_map/while
  199.8 1.9 copy-start.9
  201.7 2.3 copy-start.8
  210.7 4.4 %copy-start.3 = (f32[16,15,128]{2,0,1:T(8,128)S(1)}, f32[16,15,128]{2,0,1:T(8,128)}, u32[]{:S(2)}) copy-start(f32[16,15,128]{2,0,1:T(8,128)} %copy-done.2) | copy-start | bytes 368644 | tf_op jit(solution)/shard_map/while
  215.1 3.4 copy-start.5
  215.1 4.5 %copy-start.7 = (f32[16,15,128]{2,0,1:T(8,128)S(1)}, f32[16,15,128]{2,0,1:T(8,128)}, u32[]{:S(2)}) copy-start(f32[16,15,128]{2,0,1:T(8,128)} %copy-done.6) | copy-start | bytes 368644 | tf_op jit(solution)/shard_map/while
  219.5 1.9 copy-start.9
  221.4 2.3 copy-start.8
  230.4 4.4 %copy-start.3 = (f32[16,15,128]{2,0,1:T(8,128)S(1)}, f32[16,15,128]{2,0,1:T(8,128)}, u32[]{:S(2)}) copy-start(f32[16,15,128]{2,0,1:T(8,128)} %copy-done.2) | copy-start | bytes 368644 | tf_op jit(solution)/shard_map/while
  234.8 3.4 copy-start.5
  234.8 4.4 %copy-start.7 = (f32[16,15,128]{2,0,1:T(8,128)S(1)}, f32[16,15,128]{2,0,1:T(8,128)}, u32[]{:S(2)}) copy-start(f32[16,15,128]{2,0,1:T(8,128)} %copy-done.6) | copy-start | bytes 368644 | tf_op jit(solution)/shard_map/while
  239.2 1.9 copy-start.9
  239.2 1.9 copy-start.11
  241.2 2.3 copy-start.8
  250.2 4.4 %copy-start.3 = (f32[16,15,128]{2,0,1:T(8,128)S(1)}, f32[16,15,128]{2,0,1:T(8,128)}, u32[]{:S(2)}) copy-start(f32[16,15,128]{2,0,1:T(8,128)} %copy-done.2) | copy-start | bytes 368644 | tf_op jit(solution)/shard_map/while
  254.5 3.4 copy-start.5
  254.5 4.5 %copy-start.7 = (f32[16,15,128]{2,0,1:T(8,128)S(1)}, f32[16,15,128]{2,0,1:T(8,128)}, u32[]{:S(2)}) copy-start(f32[16,15,128]{2,0,1:T(8,128)} %copy-done.6) | copy-start | bytes 368644 | tf_op jit(solution)/shard_map/while
  259.0 1.9 copy-start.9
  260.9 17.0 %copy-start.12 = (bf16[680,152]{0,1:T(8,128)(2,1)S(1)}, bf16[680,152]{0,1:T(8,128)(2,1)}, u32[]{:S(2)}) copy-start(bf16[680,152]{0,1:T(8,128)(2,1)} %param.27) | copy-start | bytes 620164
  274.3 60.4 %copy-start.18 = (s32[2048,16]{0,1:T(8,128)S(1)}, s32[2048,16]{0,1:T(8,128)}, u32[]{:S(2)}) copy-start(s32[2048,16]{0,1:T(8,128)} %param.25) | copy-start | bytes 393220
  315.5 20.1 %collective-permute-start = (bf16[2,8,680]{2,1,0:T(8,128)(2,1)S(1)}, bf16[2,8,680]{2,1,0:T(8,128)(2,1)S(1)}, u32[]{:S(2)}, u32[]{:S(2)}) collective-permute-start(bf16[2,8,680]{2,1,0:T(8,128)(2,1)S(1)} %get-tuple-element.198), channel_id=1, source_target_pairs={{0,4},{4,8},{8,12},{12,16},{16,20},{20,24},{24,28},{28,32},{32,36}... | collective-permute-start | bytes 65288 | tf_op jit(solution)/shard_map/ppermute | solution.py:52
  332.5 5.1 %collective-permute-start.1 = (bf16[2,8,680]{2,1,0:T(8,128)(2,1)S(1)}, bf16[2,8,680]{2,1,0:T(8,128)(2,1)S(1)}, u32[]{:S(2)}, u32[]{:S(2)}) collective-permute-start(bf16[2,8,680]{2,1,0:T(8,128)(2,1)S(1)} %get-tuple-element.199), channel_id=1, source_target_pairs={{4,0},{8,4},{12,8},{16,12},{20,16},{24,20},{28,24},{32,28},{36,32}... | collective-permute-start | bytes 65288 | tf_op jit(solution)/shard_map/ppermute | solution.py:53
  346.6 16.7 %copy-start.19 = (bf16[8,152,152]{2,1,0:T(8,128)(2,1)S(1)}, bf16[8,152,152]{2,1,0:T(8,128)(2,1)}, u32[]{:S(2)}) copy-start(bf16[8,152,152]{2,1,0:T(8,128)(2,1)} %param.29) | copy-start | bytes 1108996
  346.6 16.7 %copy-start.20 = (bf16[152,680]{1,0:T(8,128)(2,1)S(1)}, bf16[152,680]{1,0:T(8,128)(2,1)}, u32[]{:S(2)}) copy-start(bf16[152,680]{1,0:T(8,128)(2,1)} %param.30) | copy-start | bytes 620164
  (28 other events, 23.8 us)
Sparse Core Ops, SparseCore 0:
  315.5 29.0 all-gather.4
where the time goes:
time: 373 us; the launch traced here: 371 us
  local copies, waits for them, and re-layouts  120 us (32%)
  waiting for transfers between devices  87.7 us (24%)
  blocking collectives  58.6 us (16%)
  matrix products  41.5 us (11%)
  starting transfers between devices  40.8 us (11%)
  between operations  13.9 us (4%)
  other arithmetic  7.44 us (2%)
    all_to_all x1, waiting for transfers between devices, shards(): lax.all_to_all(picked.reshape(sources, item_count, local_species, coef_wi...  72.3 us
    gather x12, local copies, waits for them, and re-layouts, evaluate(): dense_coef = jnp.take(padded, jnp.asarray(lookup), axis=-1)  64.8 us
    all_gather x2, blocking collectives, gather_in_order(): pieces = lax.all_gather(pieces, axes[k])  37.4 us
    dot_general x6, matrix products, evaluate(): jnp.einsum('sqk,kp->sqp', dense_coef, along_z, precision=precise)  20.5 us
    ppermute x1, starting transfers between devices, extended(): before = lax.ppermute(last, axis, up)  17 us
    reshape x1, local copies, waits for them, and re-layouts, joined_along(): return jnp.moveaxis(pieces, 0, dim).reshape(lengths)  14 us
    all_to_all x1, starting transfers between devices, moved_by_axis(): filled = lax.all_to_all(filled, axes[k], k, k, tiled=True)  13.1 us
    all_to_all x1, waiting for transfers between devices, moved_by_axis(): filled = lax.all_to_all(filled, axes[k], k, k, tiled=True)  12.5 us
  transfers between devices with their start and end apart: 5, of which 4 were waited for; matrix products, arithmetic and copies ran while one was open for 3% of the time, Pallas kernels for 0%

commit v1 on v0

v1 whole, which is shorter than its diff:
```python
import functools

import jax
import jax.numpy as jnp
import numpy as np
from jax import lax
from jax.experimental import pallas as pl
from jax.experimental.pallas import tpu as pltpu
from jax.sharding import Mesh
from jax.sharding import PartitionSpec as P

ORDER = 14
DEG = ORDER + 1
BLOCKS = 6
PB = 128
MOVE = 4
REACH = 4
MARGIN = MOVE + REACH
CAP = 2
PAIR_ROWS = 128
LANES = 384
SEG = ("seg_0", "seg_1", "seg_2")
F32 = jnp.float32
BF16 = jnp.bfloat16


def degree_pairs():
    return [(i, d - i) for d in range(DEG) for i in range(d + 1)]


def coefficient_table():
    number = {}
    for i in range(DEG):
        for j in range(DEG - i):
            for k in range(DEG - i - j):
                number[i, j, k] = len(number)
    table = np.full((DEG, PAIR_ROWS), -1, np.int32)
    for k in range(DEG):
        for q, (i, j) in enumerate(degree_pairs()):
            if i + j + k <= ORDER:
                table[k, q] = number[i, j, k]
    return table.reshape(1, DEG * PAIR_ROWS)


def high_low(value):
    high = value.astype(BF16)
    return high, (value - high.astype(F32)).astype(BF16)


def polynomials(x):
    terms = [jnp.ones_like(x), x]
    for _ in range(2, DEG):
        terms.append(2.0 * x * terms[-1] - terms[-2])
    return terms


def route_kernel(part_ref, owner_ref, points_ref, request_ref, place_ref, count_ref, line_ref):
    part = part_ref[0]
    leaves, blocks = owner_ref.shape
    coordinate = jnp.minimum(part, 2)
    request_ref[...] = jnp.zeros_like(request_ref)
    for m in range(blocks):
        line_ref[m * leaves : (m + 1) * leaves] = points_ref[coordinate, :, m * PB : (m + 1) * PB]

    @pl.loop(0, count_ref.shape[0])
    def _(d):
        count_ref[d] = 0

    @pl.loop(0, leaves)
    def _(leaf):
        for m in range(blocks):
            owner = owner_ref[leaf, m]
            target = lax.shift_right_logical(owner, 4)
            used = count_ref[target]
            count_ref[target] = used + 1
            row = target * CAP + used
            place_ref[leaf * blocks + m] = row
            line = line_ref[pl.ds(m * leaves + leaf, 1), :]
            index = jnp.full((1, PB), (owner & 15).astype(F32), F32)
            request_ref[pl.ds(row, 1), :] = jnp.where(part == 3, index, line)


def evaluate_kernel(index_ref, request_ref, coeffs_ref, table_ref, out_ref, split_ref, left_ref, pair_ref, z_ref):
    species, leaves, width = coeffs_ref.shape
    per_leaf = 4 * 16
    split_ref[...] = jnp.zeros_like(split_ref)
    parts = []
    for s in range(species):
        parts.append(coeffs_ref[s])
    both = jnp.concatenate(parts, axis=0)
    rest = both - both.astype(BF16).astype(F32)
    stacked = jnp.concatenate([both, rest], axis=0).astype(BF16)
    for k in range(DEG):
        wanted = table_ref[:, k * PAIR_ROWS : (k + 1) * PAIR_ROWS]
        rows = lax.broadcasted_iota(jnp.int32, (width, PAIR_ROWS), 0)
        pick = jnp.where(rows == wanted, 1.0, 0.0).astype(BF16)
        moved = jnp.dot(stacked, pick, preferred_element_type=F32)
        for h in range(2 * species):
            split_ref[pl.ds(h * 16 + k, leaves, stride=per_leaf), :] = moved[h * leaves : (h + 1) * leaves]

    @pl.loop(0, leaves)
    def _(leaf):
        block = split_ref[pl.ds(leaf * per_leaf, per_leaf), :]
        half = per_leaf // 2
        upper = jnp.concatenate([block[:half], jnp.zeros_like(block[:half])], axis=0)
        left_ref[leaf] = jnp.concatenate([block, upper], axis=1).astype(BF16)

    for i in range(8):
        pair_ref[pl.ds(i * PAIR_ROWS + 120, 8), :] = jnp.zeros((8, PB), F32)
        z_ref[pl.ds(i * 16 + 8, 8), :] = jnp.zeros((8, PB), F32)

    @pl.loop(0, request_ref.shape[1] // 8)
    def _(group):
        at = pl.ds(pl.multiple_of(group * 8, 8), 8)
        along_x = polynomials(request_ref[0, at, :])
        along_y = polynomials(request_ref[1, at, :])
        along_z = polynomials(request_ref[2, at, :])
        for q, (i, j) in enumerate(degree_pairs()):
            product = along_x[i] if j == 0 else along_y[j] if i == 0 else along_x[i] * along_y[j]
            pair_ref[pl.ds(q, 8, stride=PAIR_ROWS), :] = product
        for k in range(DEG):
            z_ref[pl.ds(k, 8, stride=16), :] = along_z[k]
        for i in range(8):
            high, low = high_low(pair_ref[pl.ds(i * PAIR_ROWS, PAIR_ROWS), :])
            right = jnp.concatenate([high, low], axis=0)
            leaf = index_ref[group * 8 + i]
            sums = jnp.dot(left_ref[leaf], right, preferred_element_type=F32)
            sums = sums[:32] + sums[32:]
            weight = z_ref[pl.ds(i * 16, 16), :]
            for s in range(species):
                line = jnp.sum(sums[s * 16 : (s + 1) * 16] * weight, axis=0, keepdims=True)
                out_ref[pl.ds(group * 16 + i * 2 + s, 1), :] = line


def collect_kernel(place_ref, rows_ref, out_ref, line_ref):
    species, leaves, nodes = out_ref.shape

    @pl.loop(0, leaves)
    def _(leaf):
        for m in range(BLOCKS):
            row = place_ref[leaf * BLOCKS + m]
            for s in range(species):
                at = (s * BLOCKS + m) * leaves + leaf
                line_ref[pl.ds(at, 1), :] = rows_ref[pl.ds(row * species + s, 1), :]

    for s in range(species):
        for m in range(BLOCKS):
            at = (s * BLOCKS + m) * leaves
            out_ref[s, :, m * PB : (m + 1) * PB] = line_ref[at : at + leaves]


def fit_kernel(part_ref, reaction_ref, values_ref, fit_ref, up_ref, ghosts_ref, equivalent_ref):
    part = part_ref[0]
    all_species = values_ref.shape[0]
    species, leaves, width = ghosts_ref.shape
    reacted = []
    for s in range(species):
        row = part * species + s
        mixing = reaction_ref[row, 0] * values_ref[0]
        for r in range(1, all_species):
            mixing = mixing + reaction_ref[row, r] * values_ref[r]
        reacted.append(values_ref[row] + jnp.tanh(mixing))
    reacted = jnp.concatenate(reacted, axis=0)
    rows = species * leaves
    high = reacted.astype(BF16)
    stacked = jnp.concatenate([reacted, reacted - high.astype(F32)], axis=0).astype(BF16)
    fit_high, fit_low = high_low(fit_ref[...])
    first = jnp.dot(stacked, fit_high, preferred_element_type=F32)
    second = jnp.dot(high, fit_low, preferred_element_type=F32)
    ghosts = (first[:rows] + first[rows:] + second).astype(BF16)
    equivalent = jnp.dot(ghosts, up_ref[...], preferred_element_type=F32).astype(BF16)
    points = up_ref.shape[1]
    equivalent_ref[...] = jnp.zeros_like(equivalent_ref)
    for s in range(species):
        ghosts_ref[s] = ghosts[s * leaves : (s + 1) * leaves]
        equivalent_ref[:, s * points : (s + 1) * points] = equivalent[s * leaves : (s + 1) * leaves]


def update_kernel(
    where_ref, before_ref, ghosts_ref, after_ref, near_src_ref, near_op_ref, far_src_ref, live_ref,
    near_mat_ref, mine_ref, other_ref, trans_ref, down_ref, out_ref, wide_ref,
):
    segment = where_ref[0]
    core = where_ref[1]
    species, slots, width = out_ref.shape
    leaves = ghosts_ref.shape[1]
    live = live_ref[...] > 0
    span = leaves + 2 * MARGIN
    source = near_src_ref[...]
    offset = jnp.where(live & (source >= 0), source - (segment * leaves - MARGIN), -1)
    kind = near_op_ref[...]
    columns = lax.broadcasted_iota(jnp.int32, (slots, span), 1)
    weights = []
    for o in range(near_mat_ref.shape[0]):
        chosen = jnp.where(kind == o, offset, -1)
        weight = jnp.zeros((slots, span), F32)
        for q in range(source.shape[1]):
            weight = weight + jnp.where(chosen[:, q : q + 1] == columns, 1.0, 0.0)
        weights.append(weight)
    own = []
    around = []
    for s in range(species):
        wide_ref[s, 0:MARGIN, :] = before_ref[s].astype(F32)
        wide_ref[s, MARGIN : MARGIN + leaves, :] = ghosts_ref[s].astype(F32)
        wide_ref[s, MARGIN + leaves : span, :] = after_ref[s].astype(F32)
        own.append(wide_ref[s, MOVE : MOVE + slots, :])
        around.append(wide_ref[s].astype(BF16))
    total = jnp.concatenate(own, axis=0)
    rows = species * slots
    for o in range(near_mat_ref.shape[0]):
        weight = weights[o].astype(BF16)
        grouped = jnp.concatenate(
            [jnp.dot(weight, around[s], preferred_element_type=F32) for s in range(species)], axis=0
        )
        rest = grouped - grouped.astype(BF16).astype(F32)
        stacked = jnp.concatenate([grouped, rest], axis=0).astype(BF16)
        term = jnp.dot(stacked, near_mat_ref[o], preferred_element_type=F32)
        total = total + term[:rows] + term[rows:]

    far = far_src_ref[...]
    far_segment = lax.shift_right_logical(far, 4)
    far_row = lax.shift_right_logical(far_segment, 1) * leaves + (far & 15)
    far_ok = live & (far >= 0)
    here = (far_segment & 1) == core
    mine_row = jnp.where(far_ok & here, far_row, -1)
    other_row = jnp.where(far_ok & jnp.logical_not(here), far_row, -1)
    operators = far.shape[1]
    held = mine_ref.shape[0]
    taken = None
    for row, table in ((mine_row, mine_ref), (other_row, other_ref)):
        column = jnp.concatenate([row[:, o : o + 1] for o in range(operators)], axis=0)
        ids = lax.broadcasted_iota(jnp.int32, (operators * slots, held), 1)
        pick = jnp.where(column == ids, 1.0, 0.0).astype(BF16)
        part = jnp.dot(pick, table[...], preferred_element_type=F32)
        taken = part if taken is None else taken + part
    points = trans_ref.shape[1]
    local = None
    for o in range(operators):
        lines = taken[o * slots : (o + 1) * slots]
        both = jnp.concatenate([lines[:, s * points : (s + 1) * points] for s in range(species)], axis=0)
        term = jnp.dot(both.astype(BF16), trans_ref[o], preferred_element_type=F32)
        local = term if local is None else local + term
    total = total + jnp.dot(local.astype(BF16), down_ref[...], preferred_element_type=F32)
    for s in range(species):
        out_ref[s] = jnp.where(live, total[s * slots : (s + 1) * slots], 0.0)


def spaces(text):
    names = {"s": pltpu.SMEM, "v": pltpu.VMEM}
    return [pl.BlockSpec(memory_space=names[c]) for c in text]


def within(mebibytes):
    return pltpu.CompilerParams(vmem_limit_bytes=mebibytes * 1024 * 1024)


def shards(
    coeffs, points, owner_leaf, reaction, fit_matrix, new_seg, near_src, near_op, near_mat, up_mat,
    far_src, trans_mat, down_mat,
):
    species, leaves, width = coeffs.shape
    segments = lax.axis_size(SEG)
    segment = lax.axis_index(SEG)
    part = lax.axis_index("sp")
    part_id = jnp.full((1,), part, jnp.int32)
    slots = segments * CAP
    shape = jax.ShapeDtypeStruct

    request, place = pl.pallas_call(
        route_kernel,
        out_shape=(shape((slots, PB), F32), shape((leaves * BLOCKS,), jnp.int32)),
        in_specs=spaces("ssv"),
        out_specs=tuple(spaces("vs")),
        scratch_shapes=[pltpu.SMEM((segments,), jnp.int32), pltpu.VMEM((leaves * BLOCKS, PB), F32)],
        compiler_params=within(4),
    )(part_id, owner_leaf, points)
    request = lax.all_to_all(request.reshape(segments, CAP, PB), SEG, 0, 0, tiled=True)
    request = lax.all_gather(request.reshape(slots, PB), "sp", axis=0)
    index = jnp.clip(request[3, :, 0].astype(jnp.int32), 0, leaves - 1)
    answers = pl.pallas_call(
        evaluate_kernel,
        out_shape=shape((slots * species, PB), F32),
        in_specs=spaces("svvv"),
        out_specs=spaces("v")[0],
        scratch_shapes=[
            pltpu.VMEM((leaves * 64, PB), F32),
            pltpu.VMEM((leaves, 64, 2 * PB), BF16),
            pltpu.VMEM((8 * PAIR_ROWS, PB), F32),
            pltpu.VMEM((8 * 16, PB), F32),
        ],
        compiler_params=within(16),
    )(index, request, coeffs, jnp.asarray(coefficient_table()))
    answers = lax.all_to_all(answers.reshape(segments, CAP * species, PB), SEG, 0, 0, tiled=True)
    values = pl.pallas_call(
        collect_kernel,
        out_shape=shape((species, leaves, BLOCKS * PB), F32),
        in_specs=spaces("sv"),
        out_specs=spaces("v")[0],
        scratch_shapes=[pltpu.VMEM((species * leaves * BLOCKS, PB), F32)],
        compiler_params=within(4),
    )(place, answers.reshape(slots * species, PB))
    gathered = lax.all_gather(values, "sp", axis=0, tiled=True)
    ghosts, equivalent = pl.pallas_call(
        fit_kernel,
        out_shape=(shape((species, leaves, width), BF16), shape((leaves, LANES), BF16)),
        in_specs=spaces("ssvvv"),
        out_specs=tuple(spaces("vv")),
        compiler_params=within(24),
    )(part_id, reaction, gathered, fit_matrix, up_mat)

    up = [(i, i + 1) for i in range(segments - 1)]
    down = [(j, i) for i, j in up]
    before = lax.ppermute(ghosts[:, leaves - MARGIN :], SEG, up)
    after = lax.ppermute(ghosts[:, :MARGIN], SEG, down)

    z_size = lax.axis_size("seg_1")
    spread = jnp.broadcast_to(equivalent[None], (z_size, leaves, LANES))
    along_z = lax.all_to_all(spread, "seg_1", 0, 0, tiled=True)
    mine = lax.all_gather(along_z.reshape(z_size * leaves, LANES), "seg_0", axis=0, tiled=True)
    other = lax.ppermute(mine, "seg_2", [(0, 1), (1, 0)])

    slot_total = leaves + 2 * MOVE
    leaf_total = new_seg.shape[0]
    target = segment * leaves - MOVE + jnp.arange(slot_total, dtype=jnp.int32)
    inside = (target >= 0) & (target < leaf_total)
    clipped = jnp.clip(target, 0, leaf_total - 1)
    live = (inside & (new_seg[clipped] == segment)).astype(jnp.int32)[:, None]
    where = jnp.stack([segment, lax.axis_index("seg_2")]).astype(jnp.int32)
    return pl.pallas_call(
        update_kernel,
        out_shape=shape((species, slot_total, width), F32),
        in_specs=spaces("svvvvvvvvvvvv"),
        out_specs=spaces("v")[0],
        scratch_shapes=[pltpu.VMEM((species, leaves + 2 * MARGIN, width), F32)],
        compiler_params=within(24),
    )(
        where, before, ghosts, after, near_src[clipped], near_op[clipped], far_src[clipped], live,
        near_mat, mine, other, trans_mat, down_mat,
    )


def solution(mesh):
    torus = Mesh(
        mesh.devices.reshape(4, 16, 2, mesh.shape["sp"]), ("seg_0", "seg_1", "seg_2", "sp")
    )
    whole = P()
    return jax.shard_map(
        shards,
        mesh=torus,
        in_specs=(P("sp", SEG, None), P(None, SEG, None), P(SEG, None)) + (whole,) * 10,
        out_specs=P("sp", SEG, None),
        check_vma=False,
    )
```

time: 373 us -> 190 us (0.51)
  local copies, waits for them, and re-layouts: 120 us -> 27.8 us
  waiting for transfers between devices: 87.7 us -> 31.2 us
  matrix products: 41.5 us -> 0 us
  Pallas kernels: 0 us -> 27.4 us
  between operations: 13.9 us -> 0.18 us
  starting transfers between devices: 40.8 us -> 30.7 us
  blocking collectives: 58.6 us -> 68.6 us
  other arithmetic: 7.44 us -> 3.29 us
    gather x21 -> x4, local copies, waits for them, and re-layouts: 80.5 us -> 8.7 us  [the longest x1 2.5 us: shards(): near_op[clipped]]
    all_to_all x2, waiting for transfers between devices: 84.8 us -> 31.2 us  [the longest x1 20.3 us: shards(): lax.all_to_all(answers.reshape(segments, CAP * species, PB), SEG, 0, 0, t...]
    dot_general x24 -> x0, matrix products: 41.5 us -> none  [the longest x6 20.5 us: evaluate(): jnp.einsum('sqk,kp->sqp', dense_coef, along_z, precision=precise)]
    all_to_all x1, blocking collectives: 10.2 us -> 37.6 us  [shards(): lax.all_to_all(request.reshape(segments, CAP, PB), SEG, 0, 0, tiled=True)]
    pallas_call x0 -> x5, Pallas kernels: none -> 27.4 us  [the longest x1 19 us: shards(): pl.pallas_call(evaluate_kernel, out_shape=shape((slots * species, PB), F3...]
    all_gather x2, blocking collectives: 37.4 us -> 20.9 us  [the longest x1 10.7 us: shards(): lax.all_gather(along_z.reshape(z_size * leaves, LANES), 'seg_0', axis=0,...]
    reshape x5 -> x0, local copies, waits for them, and re-layouts: 14.2 us -> none  [the longest x1 14 us: joined_along(): return jnp.moveaxis(pieces, 0, dim).reshape(lengths)]
    unnamed x29 -> x36, local copies, waits for them, and re-layouts: 3.94 us -> 16.5 us
  transfers between devices with their start and end apart: 5 -> 5, of which waited for: 4 -> 2; matrix products, arithmetic and copies ran while one was open for 3% -> 12% of each run, Pallas kernels for 0% -> 0%
where the time goes in v1:
time: 190 us; the launch traced here: 189 us
  blocking collectives  68.6 us (36%)
  waiting for transfers between devices  31.2 us (16%)
  starting transfers between devices  30.7 us (16%)
  local copies, waits for them, and re-layouts  27.8 us (15%)
  Pallas kernels  27.4 us (14%)
  other arithmetic  3.29 us (2%)
    all_to_all x1, blocking collectives, shards(): lax.all_to_all(request.reshape(segments, CAP, PB), SEG, 0, 0, tiled=True)  37.6 us
    all_to_all x1, waiting for transfers between devices, shards(): lax.all_to_all(answers.reshape(segments, CAP * species, PB), SEG, 0, 0, t...  20.3 us
    pallas_call x1, Pallas kernels, shards(): pl.pallas_call(evaluate_kernel, out_shape=shape((slots * species, PB), F3...  19 us
    unnamed x36, local copies, waits for them, and re-layouts  16.5 us
    ppermute x1, starting transfers between devices, shards(): other = lax.ppermute(mine, 'seg_2', [(0, 1), (1, 0)])  11.3 us
    all_to_all x1, waiting for transfers between devices, shards(): along_z = lax.all_to_all(spread, 'seg_1', 0, 0, tiled=True)  11 us
    all_gather x1, blocking collectives, shards(): lax.all_gather(along_z.reshape(z_size * leaves, LANES), 'seg_0', axis=0,...  10.7 us
    all_to_all x1, starting transfers between devices, shards(): lax.all_to_all(answers.reshape(segments, CAP * species, PB), SEG, 0, 0, t...  10.7 us
  transfers between devices with their start and end apart: 5, of which 2 were waited for; matrix products, arithmetic and copies ran while one was open for 12% of the time, Pallas kernels for 0%

profile of v1, /device:TPU:1, one launch (start us, length us, event | category | flops | bytes accessed | tf_op | source)
XLA Modules:
  0.0 189.2 jit_solution(14090871188298981204)
XLA Ops:
  0.0 0.8 copy.29.owner_ref
  0.8 0.9 copy-done.4
  1.7 2.6 %shard_map.136 = (f32[256,128]{1,0:T(8,128)S(1)}, s32[96]{0:T(128)S(1)}) custom-call(s32[1]{0:T(128)} %bitcast.2.part_ref, s32[16,6]{1,0:T(8,128)S(1)} %copy.29.owner_ref, f32[3,16,768]{2,1,0:T(8,128)S(1)} %copy-done.4), custom_call_target="tpu_custom_call" | custom-call | tf_op jit(solution)/shard_map/pallas_call | solution.py:269
  4.3 37.6 %all_to_all.15 = f32[128,2,128]{2,1,0:T(2,128)S(1)} all-to-all(f32[128,2,128]{2,1,0:T(2,128)S(1)} %bitcast.11), channel_id=1, replica_groups=mesh['seg_0'=4,'seg_1'=16,'seg_2'=2,'sp'=4] {'seg_0','seg_1','seg_2'}, dimensions={0} | all-to-all | bytes 262144 | tf_op jit(solution)/shard_map/all_to_all | solution.py:277
  41.9 10.2 %all_gather.9.request_ref = f32[4,256,128]{2,1,0:T(8,128)S(1)} all-gather(f32[1,256,128]{2,1,0:T(8,128)S(1)} %bitcast.13), channel_id=1, replica_groups=mesh['seg_0'=4,'seg_1'=16,'seg_2'=2,'sp'=4] {'sp'}, dimensions={0}, use_global_device_ids=true | all-gather | bytes 655360 | tf_op jit(solution)/shard_map/all_gather | solution.py:278
  52.1 0.1 fusion.1.index_ref
  52.2 0.0 copy-start.5
  52.3 0.9 copy-done.5
  53.1 0.7 copy-done.10
  53.8 19.0 %shard_map.137 = f32[512,128]{1,0:T(8,128)} custom-call(s32[256]{0:T(256)S(1)} %fusion.1.index_ref, f32[4,256,128]{2,1,0:T(8,128)S(1)} %all_gather.9.request_ref, f32[2,16,680]{2,1,0:T(8,128)S(1)} %copy-done.5, s32[1,1920]{1,0:T(1,128)S(1)} %copy-done.10), custom_call_target="tpu_custom_call" | custom-call | tf_op jit(solution)/shard_map/pallas_call | solution.py:280
  72.8 10.7 %all-to-all-start.1 = ((f32[128,4,128]{2,1,0:T(4,128)}), f32[128,4,128]{2,1,0:T(4,128)S(1)}, u32[]{:S(2)}, u32[]{:S(2)}) async-start(f32[128,4,128]{2,1,0:T(4,128)} %bitcast.5), calls=%async_computation.1 | async-start | bytes 524288 | tf_op jit(solution)/shard_map/all_to_all | solution.py:293
  83.5 0.0 copy-start.13
  83.5 0.0 copy-start.11
  83.5 2.0 %copy.30.fit_ref = f32[768,680]{1,0:T(8,128)S(1)} copy(f32[768,680]{0,1:T(8,128)} %param.18) | data formatting | bytes 4177920 | tf_op args[4]
  85.6 0.2 copy.31.up_ref
  85.7 20.3 %all-to-all-done.1 = f32[128,4,128]{2,1,0:T(4,128)S(1)} async-done(((f32[128,4,128]{2,1,0:T(4,128)}), f32[128,4,128]{2,1,0:T(4,128)S(1)}, u32[]{:S(2)}, u32[]{:S(2)}) %all-to-all-start.1) | async-done | bytes 262176 | tf_op jit(solution)/shard_map/all_to_all | solution.py:293
  106.0 0.8 shard_map.138
  106.8 10.1 %all_gather.10.values_ref = f32[8,16,768]{2,1,0:T(8,128)S(1)} all-gather(f32[2,16,768]{2,1,0:T(8,128)S(1)} %shard_map.138), channel_id=1, replica_groups=mesh['seg_0'=4,'seg_1'=16,'seg_2'=2,'sp'=4] {'sp'}, dimensions={0}, use_global_device_ids=true | all-gather | bytes 491520 | tf_op jit(solution)/shard_map/all_gather | solution.py:302
  116.9 1.4 shard_map.139
  118.2 0.7 broadcast_in_dim.5
  119.0 3.9 %all-to-all-start.2 = ((bf16[16,16,384]{2,1,0:T(8,128)(2,1)}), bf16[16,16,384]{2,1,0:T(8,128)(2,1)S(1)}, u32[]{:S(2)}, u32[]{:S(2)}) async-start(bf16[16,16,384]{2,1,0:T(8,128)(2,1)} %broadcast_in_dim.5), calls=%async_computation.2 | async-start | bytes 393216 | tf_op jit(solution)/shard_map/all_to_all | solution.py:318
  122.9 0.1 fusion.2
  123.0 1.2 gather_fusion.3
  124.3 11.0 %all-to-all-done.2 = bf16[16,16,384]{2,1,0:T(8,128)(2,1)S(1)} async-done(((bf16[16,16,384]{2,1,0:T(8,128)(2,1)}), bf16[16,16,384]{2,1,0:T(8,128)(2,1)S(1)}, u32[]{:S(2)}, u32[]{:S(2)}) %all-to-all-start.2) | async-done | bytes 196640 | tf_op jit(solution)/shard_map/all_to_all | solution.py:318
  135.2 10.7 %all_gather.11.mine_ref = bf16[1024,384]{1,0:T(8,128)(2,1)S(1)} all-gather(bf16[256,384]{1,0:T(8,128)(2,1)S(1)} %bitcast.12), channel_id=1, replica_groups=mesh['seg_0'=4,'seg_1'=16,'seg_2'=2,'sp'=4] {'seg_0'}, dimensions={0}, use_global_device_ids=true | all-gather | bytes 983040 | tf_op jit(solution)/shard_map/all_gather | solution.py:319
  145.9 11.3 %collective-permute-start.2 = (bf16[1024,384]{1,0:T(8,128)(2,1)S(1)}, bf16[1024,384]{1,0:T(8,128)(2,1)}, u32[]{:S(2)}, u32[]{:S(2)}) collective-permute-start(bf16[1024,384]{1,0:T(8,128)(2,1)S(1)} %all_gather.11.mine_ref), channel_id=1, source_target_pairs={{0,4},{4,0},{1,5},{5,1},{2,6},{6,2},{3,7},{7,3},{8,12},{12,8},{9,1... | collective-permute-start | bytes 2359304 | tf_op jit(solution)/shard_map/ppermute | solution.py:320
  157.2 1.1 compare_bitcast_fusion
  158.3 1.2 copy.35
  159.6 1.3 fusion.7.live_ref
  160.9 0.6 fusion.8
  161.5 3.0 %collective-permute-start = (bf16[2,8,680]{2,1,0:T(8,128)(2,1)}, bf16[2,8,680]{2,1,0:T(8,128)(2,1)}, u32[]{:S(2)}, u32[]{:S(2)}) collective-permute-start(bf16[2,8,680]{2,1,0:T(8,128)(2,1)} %get-tuple-element.14), channel_id=1, source_target_pairs={{0,4},{4,8},{8,12},{12,16},{16,20},{20,24},{24,28},{28,32},{32,36}... | collective-permute-start | bytes 65288 | tf_op jit(solution)/shard_map/ppermute | solution.py:313
  164.5 1.9 %collective-permute-start.1 = (bf16[2,8,680]{2,1,0:T(8,128)(2,1)}, bf16[2,8,680]{2,1,0:T(8,128)(2,1)}, u32[]{:S(2)}, u32[]{:S(2)}) collective-permute-start(bf16[2,8,680]{2,1,0:T(8,128)(2,1)} %get-tuple-element.13), channel_id=1, source_target_pairs={{4,0},{8,4},{12,8},{16,12},{20,16},{24,20},{28,24},{32,28},{36,32}... | collective-permute-start | bytes 65288 | tf_op jit(solution)/shard_map/ppermute | solution.py:314
  166.4 0.6 pad_add_fusion.where_ref
  167.0 2.2 %copy.32 = s32[2048,16]{1,0:T(8,128)} copy(s32[2048,16]{0,1:T(8,128)} %param.20) | data formatting | bytes 262144 | tf_op args[6]
  169.2 2.5 %gather_fusion = s32[24,16]{1,0:T(8,128)} fusion(s32[2048,16]{1,0:T(8,128)} %copy.32, s32[1024]{0:T(1024)} %copy-done.14), kind=kCustom, calls=%fused_computation | custom fusion | bytes 3168 | tf_op jit(solution)/shard_map/gather | solution.py:337
  171.7 2.2 %copy.33 = s32[2048,16]{1,0:T(8,128)} copy(s32[2048,16]{0,1:T(8,128)} %param.21) | data formatting | bytes 262144 | tf_op args[7]
  173.9 2.5 %gather_fusion.1 = s32[24,16]{1,0:T(8,128)} fusion(s32[2048,16]{1,0:T(8,128)} %copy.33, s32[1024]{0:T(1024)} %copy-done.14), kind=kCustom, calls=%fused_computation.1 | custom fusion | bytes 3168 | tf_op jit(solution)/shard_map/gather | solution.py:337
  176.4 2.2 %copy.34 = s32[2048,8]{1,0:T(8,128)} copy(s32[2048,8]{0,1:T(8,128)} %param.24) | data formatting | bytes 131072 | tf_op args[10]
  178.6 2.5 %gather_fusion.2 = s32[24,8]{1,0:T(8,128)} fusion(s32[2048,8]{1,0:T(8,128)} %copy.34, s32[1024]{0:T(1024)} %copy-done.14), kind=kCustom, calls=%fused_computation.2 | custom fusion | bytes 1632 | tf_op jit(solution)/shard_map/gather | solution.py:337
  181.1 0.0 collective-permute-done.before_ref
  181.1 0.0 copy-start.3
  181.1 0.9 copy-done.3
  182.1 0.7 copy-done.6
  182.8 0.7 copy-done.7
  183.5 0.7 copy-done.8
  184.2 0.7 copy-done.9
  184.9 0.6 copy-done.12
  185.5 3.7 %shard_map.140 = f32[2,24,680]{2,1,0:T(8,128)} custom-call(s32[2]{0:T(128)S(1)} %copy-done.12, bf16[2,8,680]{2,1,0:T(8,128)(2,1)} %collective-permute-done.before_ref, bf16[2,16,680]{2,1,0:T(8,128)(2,1)S(1)} %get-tuple-element.11.ghosts_ref, bf16[2,8,680]{2,1,0:T(8,128)(2,1)} %collective-permute-done.1.after_ref, s32[24,16]{1,0:T(8,128)S(1)} %copy-done.6, ...), custom_call_target="tpu_custom_call" | custom-call | tf_op jit(solution)/shard_map/pallas_call | solution.py:329
  (20 shorter events, 0.0 us)
Async XLA Ops:
  0.0 123.0 %copy-start = (s32[2048]{0:T(1024)S(1)}, s32[2048]{0:T(1024)}, u32[]{:S(2)}) copy-start(s32[2048]{0:T(1024)} %param.19) | copy-start | bytes 24580
  0.8 0.9 copy-start.4
  52.2 0.9 copy-start.5
  53.1 0.7 copy-start.10
  72.8 33.2 %all-to-all-start.1 = ((f32[128,4,128]{2,1,0:T(4,128)}), f32[128,4,128]{2,1,0:T(4,128)S(1)}, u32[]{:S(2)}, u32[]{:S(2)}) async-start(f32[128,4,128]{2,1,0:T(4,128)} %bitcast.5), calls=%async_computation.1 | async-start | bytes 524288 | tf_op jit(solution)/shard_map/all_to_all | solution.py:293
  83.5 2.1 %copy-start.13 = (bf16[680,152]{0,1:T(8,128)(2,1)S(1)}, bf16[680,152]{0,1:T(8,128)(2,1)}, u32[]{:S(2)}) copy-start(bf16[680,152]{0,1:T(8,128)(2,1)} %param.23) | copy-start | bytes 620164
  83.5 33.4 %copy-start.11 = (f32[8,8]{1,0:T(8,128)S(1)}, f32[8,8]{1,0:T(8,128)}, u32[]{:S(2)}) copy-start(f32[8,8]{1,0:T(8,128)} %reaction_ref.1) | copy-start | bytes 772
  119.0 16.2 %all-to-all-start.2 = ((bf16[16,16,384]{2,1,0:T(8,128)(2,1)}), bf16[16,16,384]{2,1,0:T(8,128)(2,1)S(1)}, u32[]{:S(2)}, u32[]{:S(2)}) async-start(bf16[16,16,384]{2,1,0:T(8,128)(2,1)} %broadcast_in_dim.5), calls=%async_computation.2 | async-start | bytes 393216 | tf_op jit(solution)/shard_map/all_to_all | solution.py:318
  123.0 12.2 %copy-start.14 = (s32[1024]{0:T(1024)}, s32[1024]{0:T(1024)S(1)}, u32[]{:S(2)}) copy-start(s32[1024]{0:T(1024)S(1)} %pad_clamp_fusion) | copy-start | bytes 12292
  145.9 35.2 %copy-start.1 = (bf16[2,680,680]{2,1,0:T(8,128)(2,1)S(1)}, bf16[2,680,680]{2,1,0:T(8,128)(2,1)}, u32[]{:S(2)}) copy-start(bf16[2,680,680]{2,1,0:T(8,128)(2,1)} %near_mat_ref.1) | copy-start | bytes 5548804
  145.9 35.2 %copy-start.2 = (bf16[8,152,152]{2,1,0:T(8,128)(2,1)S(1)}, bf16[8,152,152]{2,1,0:T(8,128)(2,1)}, u32[]{:S(2)}) copy-start(bf16[8,152,152]{2,1,0:T(8,128)(2,1)} %trans_ref.1) | copy-start | bytes 1108996
  145.9 35.2 %collective-permute-start.2 = (bf16[1024,384]{1,0:T(8,128)(2,1)S(1)}, bf16[1024,384]{1,0:T(8,128)(2,1)}, u32[]{:S(2)}, u32[]{:S(2)}) collective-permute-start(bf16[1024,384]{1,0:T(8,128)(2,1)S(1)} %all_gather.11.mine_ref), channel_id=1, source_target_pairs={{0,4},{4,0},{1,5},{5,1},{2,6},{6,2},{3,7},{7,3},{8,12},{12,8},{9,1... | collective-permute-start | bytes 2359304 | tf_op jit(solution)/shard_map/ppermute | solution.py:320
  161.5 19.6 %collective-permute-start = (bf16[2,8,680]{2,1,0:T(8,128)(2,1)}, bf16[2,8,680]{2,1,0:T(8,128)(2,1)}, u32[]{:S(2)}, u32[]{:S(2)}) collective-permute-start(bf16[2,8,680]{2,1,0:T(8,128)(2,1)} %get-tuple-element.14), channel_id=1, source_target_pairs={{0,4},{4,8},{8,12},{12,16},{16,20},{20,24},{24,28},{28,32},{32,36}... | collective-permute-start | bytes 65288 | tf_op jit(solution)/shard_map/ppermute | solution.py:313
  164.5 16.7 %collective-permute-start.1 = (bf16[2,8,680]{2,1,0:T(8,128)(2,1)}, bf16[2,8,680]{2,1,0:T(8,128)(2,1)}, u32[]{:S(2)}, u32[]{:S(2)}) collective-permute-start(bf16[2,8,680]{2,1,0:T(8,128)(2,1)} %get-tuple-element.13), channel_id=1, source_target_pairs={{4,0},{8,4},{12,8},{16,12},{20,16},{24,20},{28,24},{32,28},{36,32}... | collective-permute-start | bytes 65288 | tf_op jit(solution)/shard_map/ppermute | solution.py:314
  181.1 0.9 copy-start.3
  182.1 0.7 copy-start.6
  182.8 0.7 copy-start.7
  183.5 0.7 copy-start.8
  184.2 0.7 copy-start.9
  184.9 0.6 copy-start.12

commit v2 on v1

--- a/solution.py
+++ b/solution.py
@@ -25,7 +25,11 @@
 
 
 def degree_pairs():
-    return [(i, d - i) for d in range(DEG) for i in range(d + 1)]
+    pairs = []
+    for i in range(8):
+        for r in range(16):
+            pairs.append((i, r) if r < DEG - i else (DEG - i, r - (DEG - i)))
+    return pairs
 
 
 def coefficient_table():
@@ -80,9 +84,10 @@
             request_ref[pl.ds(row, 1), :] = jnp.where(part == 3, index, line)
 
 
-def evaluate_kernel(index_ref, request_ref, coeffs_ref, table_ref, out_ref, split_ref, left_ref, pair_ref, z_ref):
+def evaluate_kernel(index_ref, request_ref, coeffs_ref, table_ref, out_ref, split_ref, left_ref, x_ref, y_ref, z_ref):
     species, leaves, width = coeffs_ref.shape
     per_leaf = 4 * 16
+    stride = per_leaf + 8
     split_ref[...] = jnp.zeros_like(split_ref)
     parts = []
     for s in range(species):
@@ -96,18 +101,18 @@
         pick = jnp.where(rows == wanted, 1.0, 0.0).astype(BF16)
         moved = jnp.dot(stacked, pick, preferred_element_type=F32)
         for h in range(2 * species):
-            split_ref[pl.ds(h * 16 + k, leaves, stride=per_leaf), :] = moved[h * leaves : (h + 1) * leaves]
+            split_ref[pl.ds(h * 16 + k, leaves, stride=stride), :] = moved[h * leaves : (h + 1) * leaves]
 
     @pl.loop(0, leaves)
     def _(leaf):
-        block = split_ref[pl.ds(leaf * per_leaf, per_leaf), :]
+        block = split_ref[pl.ds(pl.multiple_of(leaf * stride, 8), per_leaf), :]
         half = per_leaf // 2
         upper = jnp.concatenate([block[:half], jnp.zeros_like(block[:half])], axis=0)
         left_ref[leaf] = jnp.concatenate([block, upper], axis=1).astype(BF16)
 
-    for i in range(8):
-        pair_ref[pl.ds(i * PAIR_ROWS + 120, 8), :] = jnp.zeros((8, PB), F32)
-        z_ref[pl.ds(i * 16 + 8, 8), :] = jnp.zeros((8, PB), F32)
+    y_ref[...] = jnp.zeros_like(y_ref)
+    z_ref[...] = jnp.zeros_like(z_ref)
+    row = lax.broadcasted_iota(jnp.int32, (8, PB), 0)
 
     @pl.loop(0, request_ref.shape[1] // 8)
     def _(group):
@@ -115,25 +120,34 @@
         along_x = polynomials(request_ref[0, at, :])
         along_y = polynomials(request_ref[1, at, :])
         along_z = polynomials(request_ref[2, at, :])
-        for q, (i, j) in enumerate(degree_pairs()):
-            product = along_x[i] if j == 0 else along_y[j] if i == 0 else along_x[i] * along_y[j]
-            pair_ref[pl.ds(q, 8, stride=PAIR_ROWS), :] = product
         for k in range(DEG):
-            z_ref[pl.ds(k, 8, stride=16), :] = along_z[k]
+            x_ref[k * 8 : (k + 1) * 8] = along_x[k]
+            y_ref[pl.ds(k, 8, stride=24), :] = along_y[k]
+            z_ref[pl.ds(k, 8, stride=24), :] = along_z[k]
         for i in range(8):
-            high, low = high_low(pair_ref[pl.ds(i * PAIR_ROWS, PAIR_ROWS), :])
+            x_rows = [jnp.broadcast_to(x_ref[pl.ds(k * 8 + i, 1), :], (8, PB)) for k in range(DEG)]
+            y_first = y_ref[i * 24 : i * 24 + 8]
+            y_last = y_ref[i * 24 + 8 : i * 24 + 16]
+            products = []
+            for b in range(8):
+                before = row < DEG - 8 - b
+                turned = pltpu.roll(y_first, 7 - b, 0) if b < 7 else y_first
+                x_late = x_rows[DEG - b] if b > 0 else x_rows[0]
+                products.append(x_rows[b] * y_first)
+                products.append(jnp.where(before, x_rows[b], x_late) * jnp.where(before, y_last, turned))
+            high, low = high_low(jnp.concatenate(products, axis=0))
             right = jnp.concatenate([high, low], axis=0)
             leaf = index_ref[group * 8 + i]
             sums = jnp.dot(left_ref[leaf], right, preferred_element_type=F32)
             sums = sums[:32] + sums[32:]
-            weight = z_ref[pl.ds(i * 16, 16), :]
+            weight = z_ref[i * 24 : i * 24 + 16]
             for s in range(species):
                 line = jnp.sum(sums[s * 16 : (s + 1) * 16] * weight, axis=0, keepdims=True)
                 out_ref[pl.ds(group * 16 + i * 2 + s, 1), :] = line
 
 
 def collect_kernel(place_ref, rows_ref, out_ref, line_ref):
-    species, leaves, nodes = out_ref.shape
+    copies, species, leaves, nodes = out_ref.shape
 
     @pl.loop(0, leaves)
     def _(leaf):
@@ -146,10 +160,13 @@
     for s in range(species):
         for m in range(BLOCKS):
             at = (s * BLOCKS + m) * leaves
-            out_ref[s, :, m * PB : (m + 1) * PB] = line_ref[at : at + leaves]
-
-
-def fit_kernel(part_ref, reaction_ref, values_ref, fit_ref, up_ref, ghosts_ref, equivalent_ref):
+            for c in range(copies):
+                out_ref[c, s, :, m * PB : (m + 1) * PB] = line_ref[at : at + leaves]
+
+
+def fit_kernel(
+    part_ref, reaction_ref, values_ref, fit_ref, up_ref, ghosts_ref, first_ref, last_ref, equivalent_ref
+):
     part = part_ref[0]
     all_species = values_ref.shape[0]
     species, leaves, width = ghosts_ref.shape
@@ -170,25 +187,47 @@
     ghosts = (first[:rows] + first[rows:] + second).astype(BF16)
     equivalent = jnp.dot(ghosts, up_ref[...], preferred_element_type=F32).astype(BF16)
     points = up_ref.shape[1]
-    equivalent_ref[...] = jnp.zeros_like(equivalent_ref)
-    for s in range(species):
-        ghosts_ref[s] = ghosts[s * leaves : (s + 1) * leaves]
-        equivalent_ref[:, s * points : (s + 1) * points] = equivalent[s * leaves : (s + 1) * leaves]
+    for s in range(species):
+        here = ghosts[s * leaves : (s + 1) * leaves]
+        ghosts_ref[s] = here
+        first_ref[s] = here[:MARGIN]
+        last_ref[s] = here[leaves - MARGIN :]
+    copies, _, lanes = equivalent_ref.shape
+    pieces = [equivalent[s * leaves : (s + 1) * leaves] for s in range(species)]
+    pieces.append(jnp.zeros((leaves, lanes - species * points), BF16))
+    line = jnp.concatenate(pieces, axis=1)
+    for c in range(copies):
+        equivalent_ref[c] = line
 
 
 def update_kernel(
-    where_ref, before_ref, ghosts_ref, after_ref, near_src_ref, near_op_ref, far_src_ref, live_ref,
+    segment_ref, core_ref, before_ref, ghosts_ref, after_ref, near_src_ref, near_op_ref, far_src_ref, new_seg_ref,
     near_mat_ref, mine_ref, other_ref, trans_ref, down_ref, out_ref, wide_ref,
 ):
-    segment = where_ref[0]
-    core = where_ref[1]
+    segment = segment_ref[0]
+    core = core_ref[0]
     species, slots, width = out_ref.shape
     leaves = ghosts_ref.shape[1]
-    live = live_ref[...] > 0
     span = leaves + 2 * MARGIN
-    source = near_src_ref[...]
+    total_leaves = new_seg_ref.shape[1]
+    near = near_src_ref.shape[0]
+    operators = far_src_ref.shape[0]
+
+    start = segment * leaves - MOVE
+    window = jnp.clip(lax.shift_right_arithmetic(start, 7) * 128, 0, total_leaves - 256)
+    window = pl.multiple_of(window, 128)
+    lists = [ref[:, pl.ds(window, 256)] for ref in (near_src_ref, near_op_ref, far_src_ref)]
+    lists.append(jnp.broadcast_to(new_seg_ref[:, pl.ds(window, 256)], (8, 256)))
+    lists = jnp.concatenate(lists, axis=0)
+    lists = pltpu.roll(lists, (window - start) & 255, 1)
+    lists = lists[:, :128].T[:slots]
+    source = lists[:, :near]
+    kind = lists[:, near : 2 * near]
+    far = lists[:, 2 * near : 2 * near + operators]
+    target = start + lax.broadcasted_iota(jnp.int32, (slots, 1), 0)
+    live = (target >= 0) & (target < total_leaves) & (lists[:, 2 * near + operators :][:, :1] == segment)
+
     offset = jnp.where(live & (source >= 0), source - (segment * leaves - MARGIN), -1)
-    kind = near_op_ref[...]
     columns = lax.broadcasted_iota(jnp.int32, (slots, span), 1)
     weights = []
     for o in range(near_mat_ref.shape[0]):
@@ -217,14 +256,12 @@
         term = jnp.dot(stacked, near_mat_ref[o], preferred_element_type=F32)
         total = total + term[:rows] + term[rows:]
 
-    far = far_src_ref[...]
     far_segment = lax.shift_right_logical(far, 4)
     far_row = lax.shift_right_logical(far_segment, 1) * leaves + (far & 15)
     far_ok = live & (far >= 0)
     here = (far_segment & 1) == core
     mine_row = jnp.where(far_ok & here, far_row, -1)
     other_row = jnp.where(far_ok & jnp.logical_not(here), far_row, -1)
-    operators = far.shape[1]
     held = mine_ref.shape[0]
     taken = None
     for row, table in ((mine_row, mine_ref), (other_row, other_ref)):
@@ -262,6 +299,7 @@
     segments = lax.axis_size(SEG)
     segment = lax.axis_index(SEG)
     part = lax.axis_index("sp")
+    parts = lax.axis_size("sp")
     part_id = jnp.full((1,), part, jnp.int32)
     slots = segments * CAP
     shape = jax.ShapeDtypeStruct
@@ -275,7 +313,8 @@
         compiler_params=within(4),
     )(part_id, owner_leaf, points)
     request = lax.all_to_all(request.reshape(segments, CAP, PB), SEG, 0, 0, tiled=True)
-    request = lax.all_gather(request.reshape(slots, PB), "sp", axis=0)
+    request = jnp.broadcast_to(request.reshape(1, slots, PB), (parts, slots, PB))
+    request = lax.all_to_all(request, "sp", 0, 0, tiled=True)
     index = jnp.clip(request[3, :, 0].astype(jnp.int32), 0, leaves - 1)
     answers = pl.pallas_call(
         evaluate_kernel,
@@ -283,58 +322,53 @@
         in_specs=spaces("svvv"),
         out_specs=spaces("v")[0],
         scratch_shapes=[
-            pltpu.VMEM((leaves * 64, PB), F32),
+            pltpu.VMEM((leaves * 72, PB), F32),
             pltpu.VMEM((leaves, 64, 2 * PB), BF16),
-            pltpu.VMEM((8 * PAIR_ROWS, PB), F32),
-            pltpu.VMEM((8 * 16, PB), F32),
+            pltpu.VMEM((DEG * 8, PB), F32),
+            pltpu.VMEM((8 * 24, PB), F32),
+            pltpu.VMEM((8 * 24, PB), F32),
         ],
         compiler_params=within(16),
     )(index, request, coeffs, jnp.asarray(coefficient_table()))
     answers = lax.all_to_all(answers.reshape(segments, CAP * species, PB), SEG, 0, 0, tiled=True)
     values = pl.pallas_call(
         collect_kernel,
-        out_shape=shape((species, leaves, BLOCKS * PB), F32),
+        out_shape=shape((parts, species, leaves, BLOCKS * PB), F32),
         in_specs=spaces("sv"),
         out_specs=spaces("v")[0],
         scratch_shapes=[pltpu.VMEM((species * leaves * BLOCKS, PB), F32)],
         compiler_params=within(4),
     )(place, answers.reshape(slots * species, PB))
-    gathered = lax.all_gather(values, "sp", axis=0, tiled=True)
-    ghosts, equivalent = pl.pallas_call(
+    gathered = lax.all_to_all(values, "sp", 0, 0, tiled=True).reshape(parts * species, leaves, BLOCKS * PB)
+    z_size = lax.axis_size("seg_1")
+    edge = shape((species, MARGIN, width), BF16)
+    ghosts, first, last, spread = pl.pallas_call(
         fit_kernel,
-        out_shape=(shape((species, leaves, width), BF16), shape((leaves, LANES), BF16)),
+        out_shape=(shape((species, leaves, width), BF16), edge, edge, shape((z_size, leaves, LANES), BF16)),
         in_specs=spaces("ssvvv"),
-        out_specs=tuple(spaces("vv")),
+        out_specs=tuple(spaces("vvvv")),
         compiler_params=within(24),
     )(part_id, reaction, gathered, fit_matrix, up_mat)
 
     up = [(i, i + 1) for i in range(segments - 1)]
     down = [(j, i) for i, j in up]
-    before = lax.ppermute(ghosts[:, leaves - MARGIN :], SEG, up)
-    after = lax.ppermute(ghosts[:, :MARGIN], SEG, down)
-
-    z_size = lax.axis_size("seg_1")
-    spread = jnp.broadcast_to(equivalent[None], (z_size, leaves, LANES))
+    before = lax.ppermute(last, SEG, up)
+    after = lax.ppermute(first, SEG, down)
     along_z = lax.all_to_all(spread, "seg_1", 0, 0, tiled=True)
     mine = lax.all_gather(along_z.reshape(z_size * leaves, LANES), "seg_0", axis=0, tiled=True)
     other = lax.ppermute(mine, "seg_2", [(0, 1), (1, 0)])
 
     slot_total = leaves + 2 * MOVE
-    leaf_total = new_seg.shape[0]
-    target = segment * leaves - MOVE + jnp.arange(slot_total, dtype=jnp.int32)
-    inside = (target >= 0) & (target < leaf_total)
-    clipped = jnp.clip(target, 0, leaf_total - 1)
-    live = (inside & (new_seg[clipped] == segment)).astype(jnp.int32)[:, None]
-    where = jnp.stack([segment, lax.axis_index("seg_2")]).astype(jnp.int32)
     return pl.pallas_call(
         update_kernel,
         out_shape=shape((species, slot_total, width), F32),
-        in_specs=spaces("svvvvvvvvvvvv"),
+        in_specs=spaces("ssvvvvvvvvvvvv"),
         out_specs=spaces("v")[0],
         scratch_shapes=[pltpu.VMEM((species, leaves + 2 * MARGIN, width), F32)],
         compiler_params=within(24),
     )(
-        where, before, ghosts, after, near_src[clipped], near_op[clipped], far_src[clipped], live,
+        jnp.full((1,), segment, jnp.int32), jnp.full((1,), lax.axis_index("seg_2"), jnp.int32),
+        before, ghosts, after, near_src.T, near_op.T, far_src.T, new_seg.reshape(1, -1),
         near_mat, mine, other, trans_mat, down_mat,
     )
 

time: 190 us -> 163 us (0.86)
  blocking collectives: 68.6 us -> 109 us
  waiting for transfers between devices: 31.2 us -> 7.36 us
  local copies, waits for them, and re-layouts: 27.8 us -> 8.32 us
  starting transfers between devices: 30.7 us -> 17.7 us
  Pallas kernels: 27.4 us -> 19.6 us
  other arithmetic: 3.29 us -> 0.11 us
    all_to_all x0 -> x3, blocking collectives: none -> 59.5 us  [the longest x1 31.1 us: shards(): lax.all_to_all(answers.reshape(segments, CAP * species, PB), SEG, 0, 0, t...]
    all_to_all x2 -> x1, waiting for transfers between devices: 31.2 us -> 3.95 us  [shards(): lax.all_to_all(values, 'sp', 0, 0, tiled=True)]
    all_gather x2 -> x0, blocking collectives: 20.3 us -> none  [the longest x1 10.2 us: shards(): request = lax.all_gather(request.reshape(slots, PB), 'sp', axis=0)]
    all_to_all x2 -> x1, starting transfers between devices: 14.6 us -> 3.46 us  [shards(): lax.all_to_all(values, 'sp', 0, 0, tiled=True)]
    gather x4 -> x0, local copies, waits for them, and re-layouts: 8.7 us -> none  [the longest x1 2.5 us: shards(): near_op[clipped]]
    unnamed x36 -> x31, local copies, waits for them, and re-layouts: 16.5 us -> 8.29 us
    pallas_call x1, Pallas kernels: 19 us -> 10.8 us  [shards(): pl.pallas_call(evaluate_kernel, out_shape=shape((slots * species, PB), F3...]
    ppermute x2, waiting for transfers between devices: 0.01 us -> 3.41 us  [the longest x1 3.41 us: shards(): after = lax.ppermute(first, SEG, down)]
  transfers between devices with their start and end apart: 5 -> 4, of which waited for: 2 -> 2; matrix products, arithmetic and copies ran while one was open for 12% -> 1% of each run, Pallas kernels for 0% -> 0%
where the time goes in v2:
time: 163 us; the launch traced here: 162 us
  blocking collectives  109 us (67%)
  Pallas kernels  19.6 us (12%)
  starting transfers between devices  17.7 us (11%)
  local copies, waits for them, and re-layouts  8.32 us (5%)
  waiting for transfers between devices  7.36 us (5%)
    all_to_all x1, blocking collectives, shards(): lax.all_to_all(request.reshape(segments, CAP, PB), SEG, 0, 0, tiled=True)  37.6 us
    all_to_all x1, blocking collectives, shards(): lax.all_to_all(answers.reshape(segments, CAP * species, PB), SEG, 0, 0, t...  31.1 us
    all_to_all x1, blocking collectives, shards(): along_z = lax.all_to_all(spread, 'seg_1', 0, 0, tiled=True)  17.5 us
    all_gather x1, blocking collectives, shards(): lax.all_gather(along_z.reshape(z_size * leaves, LANES), 'seg_0', axis=0,...  11.6 us
    all_to_all x1, blocking collectives, shards(): request = lax.all_to_all(request, 'sp', 0, 0, tiled=True)  10.9 us
    pallas_call x1, Pallas kernels, shards(): pl.pallas_call(evaluate_kernel, out_shape=shape((slots * species, PB), F3...  10.8 us
    ppermute x1, starting transfers between devices, shards(): other = lax.ppermute(mine, 'seg_2', [(0, 1), (1, 0)])  9.41 us
    unnamed x31, local copies, waits for them, and re-layouts  8.29 us
  transfers between devices with their start and end apart: 4, of which 2 were waited for; matrix products, arithmetic and copies ran while one was open for 1% of the time, Pallas kernels for 0%

profile of v2, /device:TPU:1, one launch (start us, length us, event | category | flops | bytes accessed | tf_op | source)
XLA Modules:
  0.0 162.0 jit_solution(7252424161875048432)
XLA Ops:
  0.0 0.0 copy-start.11
  0.0 0.8 copy.18.owner_ref
  0.8 0.0 copy-start.3
  0.8 0.9 copy-done.3
  1.7 0.0 copy-start.6
  1.7 2.6 %shard_map.136 = (f32[256,128]{1,0:T(8,128)S(1)}, s32[96]{0:T(128)S(1)}) custom-call(s32[1]{0:T(128)} %bitcast.2.part_ref, s32[16,6]{1,0:T(8,128)S(1)} %copy.18.owner_ref, f32[3,16,768]{2,1,0:T(8,128)S(1)} %copy-done.3), custom_call_target="tpu_custom_call" | custom-call | tf_op jit(solution)/shard_map/pallas_call | solution.py:307
  4.3 37.6 %all_to_all.25 = f32[128,2,128]{2,1,0:T(2,128)S(1)} all-to-all(f32[128,2,128]{2,1,0:T(2,128)S(1)} %bitcast.18), channel_id=1, replica_groups=mesh['seg_0'=4,'seg_1'=16,'seg_2'=2,'sp'=4] {'seg_0','seg_1','seg_2'}, dimensions={0} | all-to-all | bytes 262144 | tf_op jit(solution)/shard_map/all_to_all | solution.py:315
  41.9 10.9 %all_to_all.26.request_ref = f32[4,256,128]{2,1,0:T(8,128)S(1)} all-to-all(f32[4,256,128]{2,1,0:T(8,128)S(1)} %broadcast_in_dim.20), channel_id=1, replica_groups=mesh['seg_0'=4,'seg_1'=16,'seg_2'=2,'sp'=4] {'sp'}, dimensions={0} | all-to-all | bytes 1048576 | tf_op jit(solution)/shard_map/all_to_all | solution.py:317
  52.8 0.1 fusion.1.index_ref
  52.9 0.0 copy-done.11
  52.9 0.0 copy-done.6
  53.0 10.8 %shard_map.137 = f32[512,128]{1,0:T(8,128)S(1)} custom-call(s32[256]{0:T(256)S(1)} %fusion.1.index_ref, f32[4,256,128]{2,1,0:T(8,128)S(1)} %all_to_all.26.request_ref, f32[2,16,680]{2,1,0:T(8,128)S(1)} %copy-done.6, s32[1,1920]{1,0:T(1,128)S(1)} %copy-done.11), custom_call_target="tpu_custom_call" | custom-call | tf_op jit(solution)/shard_map/pallas_call | solution.py:319
  63.8 31.1 %all_to_all.27 = f32[128,4,128]{2,1,0:T(4,128)S(1)} all-to-all(f32[128,4,128]{2,1,0:T(4,128)S(1)} %bitcast.14), channel_id=1, replica_groups=mesh['seg_0'=4,'seg_1'=16,'seg_2'=2,'sp'=4] {'seg_0','seg_1','seg_2'}, dimensions={0} | all-to-all | bytes 524288 | tf_op jit(solution)/shard_map/all_to_all | solution.py:333
  94.9 1.5 shard_map.138
  96.5 3.5 %all-to-all-start.3 = ((f32[4,2,16,768]{3,2,1,0:T(8,128)}), f32[4,2,16,768]{3,2,1,0:T(8,128)S(1)}, u32[]{:S(2)}, u32[]{:S(2)}) async-start(f32[4,2,16,768]{3,2,1,0:T(8,128)} %shard_map.138), calls=%async_computation.3 | async-start | bytes 786432 | tf_op jit(solution)/shard_map/all_to_all | solution.py:342
  99.9 0.0 copy-start.13
  99.9 0.0 copy-start.12
  99.9 2.0 %copy.19.fit_ref = f32[768,680]{1,0:T(8,128)S(1)} copy(f32[768,680]{0,1:T(8,128)} %param.18) | data formatting | bytes 4177920 | tf_op args[4]
  102.0 0.0 copy-done.13
  102.0 0.2 copy.20.up_ref
  102.2 3.9 %all-to-all-done.3 = f32[4,2,16,768]{3,2,1,0:T(8,128)S(1)} async-done(((f32[4,2,16,768]{3,2,1,0:T(8,128)}), f32[4,2,16,768]{3,2,1,0:T(8,128)S(1)}, u32[]{:S(2)}, u32[]{:S(2)}) %all-to-all-start.3) | async-done | bytes 393248 | tf_op jit(solution)/shard_map/all_to_all | solution.py:342
  106.1 0.0 copy-done.12
  106.1 0.0 copy-start.2
  106.1 0.0 copy-start.4
  106.1 0.0 copy-start.7
  106.1 0.0 copy-start.10
  106.1 1.9 %shard_map.139 = (bf16[2,16,680]{2,1,0:T(8,128)(2,1)S(1)}, bf16[2,8,680]{2,1,0:T(8,128)(2,1)}, bf16[2,8,680]{2,1,0:T(8,128)(2,1)}, bf16[16,16,384]{2,1,0:T(8,128)(2,1)S(1)}) custom-call(s32[1]{0:T(128)} %bitcast.2.part_ref, f32[8,8]{1,0:T(8,128)S(1)} %copy-done.12, f32[8,16,768]{2,1,0:T(8,128)S(1)} %bitcast.13, f32[768,680]{1,0:T(8,128)S(1)} %copy.19.fit_ref, ...), custom_call_target="tpu_custom_call" | custom-call | tf_op jit(solution)/shard_map/pallas_call | solution.py:345
  108.0 0.0 copy-start.8
  108.0 17.5 %all_to_all.28 = bf16[16,16,384]{2,1,0:T(8,128)(2,1)S(1)} all-to-all(bf16[16,16,384]{2,1,0:T(8,128)(2,1)S(1)} %get-tuple-element.16), channel_id=1, replica_groups=mesh['seg_0'=4,'seg_1'=16,'seg_2'=2,'sp'=4] {'seg_1'}, dimensions={0} | all-to-all | bytes 393216 | tf_op jit(solution)/shard_map/all_to_all | solution.py:357
  125.5 0.0 copy-done.8
  125.5 11.6 %all_gather.3.mine_ref = bf16[1024,384]{1,0:T(8,128)(2,1)S(1)} all-gather(bf16[256,384]{1,0:T(8,128)(2,1)S(1)} %bitcast.21), channel_id=1, replica_groups=mesh['seg_0'=4,'seg_1'=16,'seg_2'=2,'sp'=4] {'seg_0'}, dimensions={0}, use_global_device_ids=true | all-gather | bytes 983040 | tf_op jit(solution)/shard_map/all_gather | solution.py:358
  137.1 9.4 %collective-permute-start.2 = (bf16[1024,384]{1,0:T(8,128)(2,1)S(1)}, bf16[1024,384]{1,0:T(8,128)(2,1)S(1)}, u32[]{:S(2)}, u32[]{:S(2)}) collective-permute-start(bf16[1024,384]{1,0:T(8,128)(2,1)S(1)} %all_gather.3.mine_ref), channel_id=1, source_target_pairs={{0,4},{4,0},{1,5},{5,1},{2,6},{6,2},{3,7},{7,3},{8,12},{12,8},{9,1... | collective-permute-start | bytes 2359304 | tf_op jit(solution)/shard_map/ppermute | solution.py:359
  146.5 2.9 %collective-permute-start = (bf16[2,8,680]{2,1,0:T(8,128)(2,1)}, bf16[2,8,680]{2,1,0:T(8,128)(2,1)S(1)}, u32[]{:S(2)}, u32[]{:S(2)}) collective-permute-start(bf16[2,8,680]{2,1,0:T(8,128)(2,1)} %get-tuple-element.13), channel_id=1, source_target_pairs={{0,4},{4,8},{8,12},{12,16},{16,20},{20,24},{24,28},{28,32},{32,36}... | collective-permute-start | bytes 65288 | tf_op jit(solution)/shard_map/ppermute | solution.py:355
  149.5 1.9 %collective-permute-start.1 = (bf16[2,8,680]{2,1,0:T(8,128)(2,1)}, bf16[2,8,680]{2,1,0:T(8,128)(2,1)S(1)}, u32[]{:S(2)}, u32[]{:S(2)}) collective-permute-start(bf16[2,8,680]{2,1,0:T(8,128)(2,1)} %get-tuple-element.15), channel_id=1, source_target_pairs={{4,0},{8,4},{12,8},{16,12},{20,16},{24,20},{28,24},{32,28},{36,32}... | collective-permute-start | bytes 65288 | tf_op jit(solution)/shard_map/ppermute | solution.py:356
  151.4 0.0 collective-permute-done.before_ref
  151.4 3.4 %collective-permute-done.1.after_ref = bf16[2,8,680]{2,1,0:T(8,128)(2,1)S(1)} collective-permute-done((bf16[2,8,680]{2,1,0:T(8,128)(2,1)}, bf16[2,8,680]{2,1,0:T(8,128)(2,1)S(1)}, u32[]{:S(2)}, u32[]{:S(2)}) %collective-permute-start.1) | collective-permute-done | bytes 21792 | tf_op jit(solution)/shard_map/ppermute | solution.py:356
  154.8 0.0 collective-permute-done.2.other_ref
  154.8 0.0 copy-done.2
  154.8 0.0 copy-done.4
  154.8 0.0 copy-done.7
  154.8 0.0 copy-done.10
  154.8 0.0 copy-start
  154.9 1.6 copy-done
  156.4 0.0 copy-start.1
  156.4 1.1 copy-done.1
  157.5 0.9 copy-done.5
  158.4 0.8 copy-done.9
  159.2 2.7 %shard_map.140 = f32[2,24,680]{2,1,0:T(8,128)} custom-call(s32[1]{0:T(128)} %bitcast.segment_ref, s32[1]{0:T(128)} %bitcast.1.core_ref, bf16[2,8,680]{2,1,0:T(8,128)(2,1)S(1)} %collective-permute-done.before_ref, bf16[2,16,680]{2,1,0:T(8,128)(2,1)S(1)} %copy-done.9, bf16[2,8,680]{2,1,0:T(8,128)(2,1)S(1)} %collective-permute-done.1.after_ref, ...), custom_call_target="tpu_custom_call" | custom-call | tf_op jit(solution)/shard_map/pallas_call | solution.py:362
  (3 shorter events, 0.0 us)
Async XLA Ops:
  0.0 52.9 %copy-start.11 = (s32[1,1920]{1,0:T(1,128)S(1)}, s32[1,1920]{1,0:T(1,128)}, u32[]{:S(2)}) copy-start(s32[1,1920]{1,0:T(1,128)} %constant.28.clone.table_ref) | copy-start | bytes 23044
  0.8 0.9 copy-start.3
  1.7 51.3 %copy-start.6 = (f32[2,16,680]{2,1,0:T(8,128)S(1)}, f32[2,16,680]{2,1,0:T(8,128)}, u32[]{:S(2)}) copy-start(f32[2,16,680]{2,1,0:T(8,128)} %coeffs_ref.1) | copy-start | bytes 261124
  96.5 9.7 %all-to-all-start.3 = ((f32[4,2,16,768]{3,2,1,0:T(8,128)}), f32[4,2,16,768]{3,2,1,0:T(8,128)S(1)}, u32[]{:S(2)}, u32[]{:S(2)}) async-start(f32[4,2,16,768]{3,2,1,0:T(8,128)} %shard_map.138), calls=%async_computation.3 | async-start | bytes 786432 | tf_op jit(solution)/shard_map/all_to_all | solution.py:342
  99.9 2.1 %copy-start.13 = (bf16[680,152]{0,1:T(8,128)(2,1)S(1)}, bf16[680,152]{0,1:T(8,128)(2,1)}, u32[]{:S(2)}) copy-start(bf16[680,152]{0,1:T(8,128)(2,1)} %param.23) | copy-start | bytes 620164
  99.9 6.2 %copy-start.12 = (f32[8,8]{1,0:T(8,128)S(1)}, f32[8,8]{1,0:T(8,128)}, u32[]{:S(2)}) copy-start(f32[8,8]{1,0:T(8,128)} %reaction_ref.1) | copy-start | bytes 772
  106.1 48.7 %copy-start.2 = (bf16[152,680]{1,0:T(8,128)(2,1)S(1)}, bf16[152,680]{1,0:T(8,128)(2,1)}, u32[]{:S(2)}) copy-start(bf16[152,680]{1,0:T(8,128)(2,1)} %down_ref.1) | copy-start | bytes 620164
  106.1 48.7 %copy-start.4 = (s32[2048,16]{0,1:T(8,128)S(1)}, s32[2048,16]{0,1:T(8,128)}, u32[]{:S(2)}) copy-start(s32[2048,16]{0,1:T(8,128)} %param.20) | copy-start | bytes 393220
  106.1 48.7 %copy-start.7 = (s32[2048,8]{0,1:T(8,128)S(1)}, s32[2048,8]{0,1:T(8,128)}, u32[]{:S(2)}) copy-start(s32[2048,8]{0,1:T(8,128)} %param.24) | copy-start | bytes 196612
  106.1 48.7 %copy-start.10 = (s32[2048]{0:T(1024)S(1)}, s32[2048]{0:T(1024)}, u32[]{:S(2)}) copy-start(s32[2048]{0:T(1024)} %param.19) | copy-start | bytes 24580
  108.0 17.5 %copy-start.8 = (bf16[2,16,680]{2,1,0:T(8,128)(2,1)}, bf16[2,16,680]{2,1,0:T(8,128)(2,1)S(1)}, u32[]{:S(2)}) copy-start(bf16[2,16,680]{2,1,0:T(8,128)(2,1)S(1)} %get-tuple-element.14.ghosts_ref) | copy-start | bytes 130564
  137.1 17.7 %collective-permute-start.2 = (bf16[1024,384]{1,0:T(8,128)(2,1)S(1)}, bf16[1024,384]{1,0:T(8,128)(2,1)S(1)}, u32[]{:S(2)}, u32[]{:S(2)}) collective-permute-start(bf16[1024,384]{1,0:T(8,128)(2,1)S(1)} %all_gather.3.mine_ref), channel_id=1, source_target_pairs={{0,4},{4,0},{1,5},{5,1},{2,6},{6,2},{3,7},{7,3},{8,12},{12,8},{9,1... | collective-permute-start | bytes 2359304 | tf_op jit(solution)/shard_map/ppermute | solution.py:359
  146.5 4.8 %collective-permute-start = (bf16[2,8,680]{2,1,0:T(8,128)(2,1)}, bf16[2,8,680]{2,1,0:T(8,128)(2,1)S(1)}, u32[]{:S(2)}, u32[]{:S(2)}) collective-permute-start(bf16[2,8,680]{2,1,0:T(8,128)(2,1)} %get-tuple-element.13), channel_id=1, source_target_pairs={{0,4},{4,8},{8,12},{12,16},{16,20},{20,24},{24,28},{28,32},{32,36}... | collective-permute-start | bytes 65288 | tf_op jit(solution)/shard_map/ppermute | solution.py:355
  149.5 5.4 %collective-permute-start.1 = (bf16[2,8,680]{2,1,0:T(8,128)(2,1)}, bf16[2,8,680]{2,1,0:T(8,128)(2,1)S(1)}, u32[]{:S(2)}, u32[]{:S(2)}) collective-permute-start(bf16[2,8,680]{2,1,0:T(8,128)(2,1)} %get-tuple-element.15), channel_id=1, source_target_pairs={{4,0},{8,4},{12,8},{16,12},{20,16},{24,20},{28,24},{32,28},{36,32}... | collective-permute-start | bytes 65288 | tf_op jit(solution)/shard_map/ppermute | solution.py:356
  154.8 1.6 copy-start
  156.4 1.1 copy-start.1
  157.5 0.9 copy-start.5
  158.4 0.8 copy-start.9

commit v3 on v2

--- a/solution.py
+++ b/solution.py
@@ -8,6 +8,7 @@
 from jax.experimental.pallas import tpu as pltpu
 from jax.sharding import Mesh
 from jax.sharding import PartitionSpec as P
+
 
 ORDER = 14
 DEG = ORDER + 1
@@ -58,30 +59,42 @@
     return terms
 
 
-def route_kernel(part_ref, owner_ref, points_ref, request_ref, place_ref, count_ref, line_ref):
+def route_kernel(
+    part_ref, owner_hbm, points_ref, request_ref, place_ref, count_ref, owner_ref, plane_ref, line_ref, sem, owner_sem
+):
     part = part_ref[0]
-    leaves, blocks = owner_ref.shape
-    coordinate = jnp.minimum(part, 2)
+    owners = pltpu.make_async_copy(owner_hbm, owner_ref, owner_sem)
+    owners.start()
+    blocks, leaves = owner_ref.shape
+    fetch = pltpu.make_async_copy(points_ref.at[jnp.minimum(part, 2)], plane_ref, sem)
+    fetch.start()
     request_ref[...] = jnp.zeros_like(request_ref)
-    for m in range(blocks):
-        line_ref[m * leaves : (m + 1) * leaves] = points_ref[coordinate, :, m * PB : (m + 1) * PB]
-
-    @pl.loop(0, count_ref.shape[0])
+
+    @pl.loop(0, count_ref.shape[0] // 8)
     def _(d):
-        count_ref[d] = 0
+        for i in range(8):
+            count_ref[d * 8 + i] = 0
+
+    owners.wait()
 
     @pl.loop(0, leaves)
     def _(leaf):
         for m in range(blocks):
-            owner = owner_ref[leaf, m]
-            target = lax.shift_right_logical(owner, 4)
+            target = lax.shift_right_logical(owner_ref[m, leaf], 4)
             used = count_ref[target]
             count_ref[target] = used + 1
-            row = target * CAP + used
-            place_ref[leaf * blocks + m] = row
+            place_ref[leaf * blocks + m] = target * CAP + used
+
+    fetch.wait()
+    for m in range(blocks):
+        line_ref[m * leaves : (m + 1) * leaves] = plane_ref[:, m * PB : (m + 1) * PB]
+
+    @pl.loop(0, leaves)
+    def _(leaf):
+        for m in range(blocks):
             line = line_ref[pl.ds(m * leaves + leaf, 1), :]
-            index = jnp.full((1, PB), (owner & 15).astype(F32), F32)
-            request_ref[pl.ds(row, 1), :] = jnp.where(part == 3, index, line)
+            index = jnp.full((1, PB), (owner_ref[m, leaf] & 15).astype(F32), F32)
+            request_ref[pl.ds(place_ref[leaf * blocks + m], 1), :] = jnp.where(part == 3, index, line)
 
 
 def evaluate_kernel(index_ref, request_ref, coeffs_ref, table_ref, out_ref, split_ref, left_ref, x_ref, y_ref, z_ref):
@@ -147,7 +160,7 @@
 
 
 def collect_kernel(place_ref, rows_ref, out_ref, line_ref):
-    copies, species, leaves, nodes = out_ref.shape
+    copies, species, leaves, _ = out_ref.shape
 
     @pl.loop(0, leaves)
     def _(leaf):
@@ -165,11 +178,22 @@
 
 
 def fit_kernel(
-    part_ref, reaction_ref, values_ref, fit_ref, up_ref, ghosts_ref, first_ref, last_ref, equivalent_ref
+    part_ref, segment_ref, reaction_ref, values_ref, fit_ref, up_ref, near_src_ref, near_op_ref, far_src_ref,
+    new_seg_ref, ghosts_ref, first_ref, last_ref, equivalent_ref, lists_ref, window_ref, owned_ref, sems,
 ):
     part = part_ref[0]
+    start = segment_ref[0] * ghosts_ref.shape[1] - MOVE
+    window = jnp.clip(lax.shift_right_arithmetic(start, 7) * 128, 0, new_seg_ref.shape[1] - 256)
+    window = pl.multiple_of(window, 128)
+    fetches = []
+    at = 0
+    for n, ref in enumerate((near_src_ref, near_op_ref, far_src_ref, new_seg_ref)):
+        held = window_ref.at[pl.ds(at, ref.shape[0])] if n < 3 else owned_ref
+        fetches.append(pltpu.make_async_copy(ref.at[:, pl.ds(window, 256)], held, sems.at[n]))
+        fetches[-1].start()
+        at += ref.shape[0]
     all_species = values_ref.shape[0]
-    species, leaves, width = ghosts_ref.shape
+    species, leaves, _ = ghosts_ref.shape
     reacted = []
     for s in range(species):
         row = part * species + s
@@ -198,63 +222,36 @@
     line = jnp.concatenate(pieces, axis=1)
     for c in range(copies):
         equivalent_ref[c] = line
+    for fetch in fetches:
+        fetch.wait()
+    lists = jnp.concatenate([window_ref[...], jnp.broadcast_to(owned_ref[...], (8, 256))], axis=0)
+    lists = pltpu.roll(lists, (window - start) & 255, 1)
+    lists_ref[...] = lists[:, :128].T[: lists_ref.shape[0]]
 
 
 def update_kernel(
-    segment_ref, core_ref, before_ref, ghosts_ref, after_ref, near_src_ref, near_op_ref, far_src_ref, new_seg_ref,
-    near_mat_ref, mine_ref, other_ref, trans_ref, down_ref, out_ref, wide_ref,
+    total_leaves, near, segment_ref, core_ref, before_ref, ghosts_ref, after_ref, lists_ref, near_mat_hbm, mine_ref,
+    other_ref, trans_hbm, down_hbm, out_ref, wide_ref, near_mat_ref, trans_ref, down_ref, sems,
 ):
     segment = segment_ref[0]
     core = core_ref[0]
-    species, slots, width = out_ref.shape
+    species, slots, _ = out_ref.shape
     leaves = ghosts_ref.shape[1]
     span = leaves + 2 * MARGIN
-    total_leaves = new_seg_ref.shape[1]
-    near = near_src_ref.shape[0]
-    operators = far_src_ref.shape[0]
-
+    operators = trans_ref.shape[0]
+    fetches = []
+    for n, (ref, held) in enumerate(
+        ((trans_hbm, trans_ref), (down_hbm, down_ref), (near_mat_hbm, near_mat_ref))
+    ):
+        fetches.append(pltpu.make_async_copy(ref, held, sems.at[n]))
+        fetches[-1].start()
     start = segment * leaves - MOVE
-    window = jnp.clip(lax.shift_right_arithmetic(start, 7) * 128, 0, total_leaves - 256)
-    window = pl.multiple_of(window, 128)
-    lists = [ref[:, pl.ds(window, 256)] for ref in (near_src_ref, near_op_ref, far_src_ref)]
-    lists.append(jnp.broadcast_to(new_seg_ref[:, pl.ds(window, 256)], (8, 256)))
-    lists = jnp.concatenate(lists, axis=0)
-    lists = pltpu.roll(lists, (window - start) & 255, 1)
-    lists = lists[:, :128].T[:slots]
+    lists = lists_ref[...]
     source = lists[:, :near]
     kind = lists[:, near : 2 * near]
     far = lists[:, 2 * near : 2 * near + operators]
     target = start + lax.broadcasted_iota(jnp.int32, (slots, 1), 0)
-    live = (target >= 0) & (target < total_leaves) & (lists[:, 2 * near + operators :][:, :1] == segment)
-
-    offset = jnp.where(live & (source >= 0), source - (segment * leaves - MARGIN), -1)
-    columns = lax.broadcasted_iota(jnp.int32, (slots, span), 1)
-    weights = []
-    for o in range(near_mat_ref.shape[0]):
-        chosen = jnp.where(kind == o, offset, -1)
-        weight = jnp.zeros((slots, span), F32)
-        for q in range(source.shape[1]):
-            weight = weight + jnp.where(chosen[:, q : q + 1] == columns, 1.0, 0.0)
-        weights.append(weight)
-    own = []
-    around = []
-    for s in range(species):
-        wide_ref[s, 0:MARGIN, :] = before_ref[s].astype(F32)
-        wide_ref[s, MARGIN : MARGIN + leaves, :] = ghosts_ref[s].astype(F32)
-        wide_ref[s, MARGIN + leaves : span, :] = after_ref[s].astype(F32)
-        own.append(wide_ref[s, MOVE : MOVE + slots, :])
-        around.append(wide_ref[s].astype(BF16))
-    total = jnp.concatenate(own, axis=0)
-    rows = species * slots
-    for o in range(near_mat_ref.shape[0]):
-        weight = weights[o].astype(BF16)
-        grouped = jnp.concatenate(
-            [jnp.dot(weight, around[s], preferred_element_type=F32) for s in range(species)], axis=0
-        )
-        rest = grouped - grouped.astype(BF16).astype(F32)
-        stacked = jnp.concatenate([grouped, rest], axis=0).astype(BF16)
-        term = jnp.dot(stacked, near_mat_ref[o], preferred_element_type=F32)
-        total = total + term[:rows] + term[rows:]
+    live = (target >= 0) & (target < total_leaves) & (lists[:, 2 * near + operators : 2 * near + operators + 1] == segment)
 
     far_segment = lax.shift_right_logical(far, 4)
     far_row = lax.shift_right_logical(far_segment, 1) * leaves + (far & 15)
@@ -271,19 +268,52 @@
         part = jnp.dot(pick, table[...], preferred_element_type=F32)
         taken = part if taken is None else taken + part
     points = trans_ref.shape[1]
+    fetches[0].wait()
     local = None
     for o in range(operators):
         lines = taken[o * slots : (o + 1) * slots]
         both = jnp.concatenate([lines[:, s * points : (s + 1) * points] for s in range(species)], axis=0)
         term = jnp.dot(both.astype(BF16), trans_ref[o], preferred_element_type=F32)
         local = term if local is None else local + term
-    total = total + jnp.dot(local.astype(BF16), down_ref[...], preferred_element_type=F32)
+    fetches[1].wait()
+    total = jnp.dot(local.astype(BF16), down_ref[...], preferred_element_type=F32)
+
+    offset = jnp.where(live & (source >= 0), source - (segment * leaves - MARGIN), -1)
+    columns = lax.broadcasted_iota(jnp.int32, (slots, span), 1)
+    weights = []
+    for o in range(near_mat_ref.shape[0]):
+        chosen = jnp.where(kind == o, offset, -1)
+        weight = jnp.zeros((slots, span), F32)
+        for q in range(source.shape[1]):
+            weight = weight + jnp.where(chosen[:, q : q + 1] == columns, 1.0, 0.0)
+        weights.append(weight)
+    own = []
+    around = []
+    for s in range(species):
+        wide_ref[s, 0:MARGIN, :] = before_ref[s].astype(F32)
+        wide_ref[s, MARGIN : MARGIN + leaves, :] = ghosts_ref[s].astype(F32)
+        wide_ref[s, MARGIN + leaves : span, :] = after_ref[s].astype(F32)
+        own.append(wide_ref[s, MOVE : MOVE + slots, :])
+        around.append(wide_ref[s].astype(BF16))
+    total = total + jnp.concatenate(own, axis=0)
+    rows = species * slots
+    fetches[2].wait()
+    for o in range(near_mat_ref.shape[0]):
+        weight = weights[o].astype(BF16)
+        grouped = jnp.concatenate(
+            [jnp.dot(weight, around[s], preferred_element_type=F32) for s in range(species)], axis=0
+        )
+        rest = grouped - grouped.astype(BF16).astype(F32)
+        stacked = jnp.concatenate([grouped, rest], axis=0).astype(BF16)
+        term = jnp.dot(stacked, near_mat_ref[o], preferred_element_type=F32)
+        total = total + term[:rows] + term[rows:]
+
     for s in range(species):
         out_ref[s] = jnp.where(live, total[s * slots : (s + 1) * slots], 0.0)
 
 
 def spaces(text):
-    names = {"s": pltpu.SMEM, "v": pltpu.VMEM}
+    names = {"s": pltpu.SMEM, "v": pltpu.VMEM, "h": pltpu.HBM}
     return [pl.BlockSpec(memory_space=names[c]) for c in text]
 
 
@@ -301,17 +331,25 @@
     part = lax.axis_index("sp")
     parts = lax.axis_size("sp")
     part_id = jnp.full((1,), part, jnp.int32)
+    segment_id = jnp.full((1,), segment, jnp.int32)
     slots = segments * CAP
     shape = jax.ShapeDtypeStruct
 
     request, place = pl.pallas_call(
         route_kernel,
         out_shape=(shape((slots, PB), F32), shape((leaves * BLOCKS,), jnp.int32)),
-        in_specs=spaces("ssv"),
+        in_specs=spaces("shh"),
         out_specs=tuple(spaces("vs")),
-        scratch_shapes=[pltpu.SMEM((segments,), jnp.int32), pltpu.VMEM((leaves * BLOCKS, PB), F32)],
+        scratch_shapes=[
+            pltpu.SMEM((segments,), jnp.int32),
+            pltpu.SMEM((BLOCKS, leaves), jnp.int32),
+            pltpu.VMEM((leaves, BLOCKS * PB), F32),
+            pltpu.VMEM((leaves * BLOCKS, PB), F32),
+            pltpu.SemaphoreType.DMA,
+            pltpu.SemaphoreType.DMA,
+        ],
         compiler_params=within(4),
-    )(part_id, owner_leaf, points)
+    )(part_id, owner_leaf.T, points)
     request = lax.all_to_all(request.reshape(segments, CAP, PB), SEG, 0, 0, tiled=True)
     request = jnp.broadcast_to(request.reshape(1, slots, PB), (parts, slots, PB))
     request = lax.all_to_all(request, "sp", 0, 0, tiled=True)
@@ -342,13 +380,25 @@
     gathered = lax.all_to_all(values, "sp", 0, 0, tiled=True).reshape(parts * species, leaves, BLOCKS * PB)
     z_size = lax.axis_size("seg_1")
     edge = shape((species, MARGIN, width), BF16)
-    ghosts, first, last, spread = pl.pallas_call(
+    slot_total = leaves + 2 * MOVE
+    near = near_src.shape[1]
+    listed = 2 * near + far_src.shape[1] + 8
+    ghosts, first, last, spread, lists = pl.pallas_call(
         fit_kernel,
-        out_shape=(shape((species, leaves, width), BF16), edge, edge, shape((z_size, leaves, LANES), BF16)),
-        in_specs=spaces("ssvvv"),
-        out_specs=tuple(spaces("vvvv")),
+        out_shape=(
+            shape((species, leaves, width), BF16), edge, edge, shape((z_size, leaves, LANES), BF16),
+            shape((slot_total, listed), jnp.int32),
+        ),
+        in_specs=spaces("sssvvvhhhh"),
+        out_specs=tuple(spaces("vvvvv")),
+        scratch_shapes=[
+            pltpu.VMEM((listed - 8, 256), jnp.int32), pltpu.VMEM((1, 256), jnp.int32), pltpu.SemaphoreType.DMA((4,)),
+        ],
         compiler_params=within(24),
-    )(part_id, reaction, gathered, fit_matrix, up_mat)
+    )(
+        part_id, segment_id, reaction, gathered, fit_matrix, up_mat, near_src.T, near_op.T, far_src.T,
+        new_seg.reshape(1, -1),
+    )
 
     up = [(i, i + 1) for i in range(segments - 1)]
     down = [(j, i) for i, j in up]
@@ -358,18 +408,22 @@
     mine = lax.all_gather(along_z.reshape(z_size * leaves, LANES), "seg_0", axis=0, tiled=True)
     other = lax.ppermute(mine, "seg_2", [(0, 1), (1, 0)])
 
-    slot_total = leaves + 2 * MOVE
     return pl.pallas_call(
-        update_kernel,
+        functools.partial(update_kernel, new_seg.shape[0], near),
         out_shape=shape((species, slot_total, width), F32),
-        in_specs=spaces("ssvvvvvvvvvvvv"),
+        in_specs=spaces("ssvvvvhvvhh"),
         out_specs=spaces("v")[0],
-        scratch_shapes=[pltpu.VMEM((species, leaves + 2 * MARGIN, width), F32)],
+        scratch_shapes=[
+            pltpu.VMEM((species, leaves + 2 * MARGIN, width), F32),
+            pltpu.VMEM(near_mat.shape, BF16),
+            pltpu.VMEM(trans_mat.shape, BF16),
+            pltpu.VMEM(down_mat.shape, BF16),
+            pltpu.SemaphoreType.DMA((3,)),
+        ],
         compiler_params=within(24),
     )(
-        jnp.full((1,), segment, jnp.int32), jnp.full((1,), lax.axis_index("seg_2"), jnp.int32),
-        before, ghosts, after, near_src.T, near_op.T, far_src.T, new_seg.reshape(1, -1),
-        near_mat, mine, other, trans_mat, down_mat,
+        segment_id, jnp.full((1,), lax.axis_index("seg_2"), jnp.int32), before, ghosts, after, lists, near_mat, mine,
+        other, trans_mat, down_mat,
     )
 
 

time: 163 us -> 159 us (0.975)
  local copies, waits for them, and re-layouts: 8.32 us -> 3.96 us
    unnamed x31 -> x28, local copies, waits for them, and re-layouts: 8.29 us -> 3.92 us
where the time goes in v3:
time: 159 us; the launch traced here: 158 us
  blocking collectives  109 us (69%)
  Pallas kernels  20.1 us (13%)
  starting transfers between devices  17.7 us (11%)
  waiting for transfers between devices  7.06 us (4%)
  local copies, waits for them, and re-layouts  3.96 us (2%)
    all_to_all x1, blocking collectives, shards(): lax.all_to_all(request.reshape(segments, CAP, PB), SEG, 0, 0, tiled=True)  37.6 us
    all_to_all x1, blocking collectives, shards(): lax.all_to_all(answers.reshape(segments, CAP * species, PB), SEG, 0, 0, t...  31.1 us
    all_to_all x1, blocking collectives, shards(): along_z = lax.all_to_all(spread, 'seg_1', 0, 0, tiled=True)  17.5 us
    all_gather x1, blocking collectives, shards(): lax.all_gather(along_z.reshape(z_size * leaves, LANES), 'seg_0', axis=0,...  11.6 us
    all_to_all x1, blocking collectives, shards(): request = lax.all_to_all(request, 'sp', 0, 0, tiled=True)  11 us
    pallas_call x1, Pallas kernels, shards(): pl.pallas_call(evaluate_kernel, out_shape=shape((slots * species, PB), F3...  10.8 us
    ppermute x1, starting transfers between devices, shards(): other = lax.ppermute(mine, 'seg_2', [(0, 1), (1, 0)])  9.41 us
    pallas_call x1, Pallas kernels, shards(): pl.pallas_call(functools.partial(update_kernel, new_seg.shape[0], near),...  4.12 us
  transfers between devices with their start and end apart: 4, of which 2 were waited for; matrix products, arithmetic and copies ran while one was open for 1% of the time, Pallas kernels for 0%

profile of v3, /device:TPU:1, one launch (start us, length us, event | category | flops | bytes accessed | tf_op | source)
XLA Modules:
  0.0 158.1 jit_solution(7447667444796645257)
XLA Ops:
  0.0 0.0 copy-start.9
  0.0 0.0 copy-start.3
  0.0 0.9 copy-done.3
  0.9 0.0 copy-start.11
  0.9 0.7 copy-done.11
  1.6 0.0 copy-start.6
  1.6 2.0 %shard_map.136 = (f32[256,128]{1,0:T(8,128)S(1)}, s32[96]{0:T(128)S(1)}) custom-call(s32[1]{0:T(128)} %bitcast.2.part_ref, s32[6,16]{1,0:T(8,128)S(1)} %bitcast.22, f32[3,16,768]{2,1,0:T(8,128)S(1)} %copy-done.3), custom_call_target="tpu_custom_call" | custom-call | tf_op jit(solution)/shard_map/pallas_call | solution.py:338
  3.6 37.6 %all_to_all.25 = f32[128,2,128]{2,1,0:T(2,128)S(1)} all-to-all(f32[128,2,128]{2,1,0:T(2,128)S(1)} %bitcast.19), channel_id=1, replica_groups=mesh['seg_0'=4,'seg_1'=16,'seg_2'=2,'sp'=4] {'seg_0','seg_1','seg_2'}, dimensions={0} | all-to-all | bytes 262144 | tf_op jit(solution)/shard_map/all_to_all | solution.py:353
  41.3 0.0 copy-start.12
  41.3 11.0 %all_to_all.26.request_ref = f32[4,256,128]{2,1,0:T(8,128)S(1)} all-to-all(f32[4,256,128]{2,1,0:T(8,128)S(1)} %broadcast_in_dim.20), channel_id=1, replica_groups=mesh['seg_0'=4,'seg_1'=16,'seg_2'=2,'sp'=4] {'sp'}, dimensions={0} | all-to-all | bytes 1048576 | tf_op jit(solution)/shard_map/all_to_all | solution.py:355
  52.3 0.1 fusion.1.index_ref
  52.4 0.0 copy-done.9
  52.4 0.0 copy-done.6
  52.4 10.8 %shard_map.137 = f32[512,128]{1,0:T(8,128)S(1)} custom-call(s32[256]{0:T(256)S(1)} %fusion.1.index_ref, f32[4,256,128]{2,1,0:T(8,128)S(1)} %all_to_all.26.request_ref, f32[2,16,680]{2,1,0:T(8,128)S(1)} %copy-done.6, s32[1,1920]{1,0:T(1,128)S(1)} %copy-done.9), custom_call_target="tpu_custom_call" | custom-call | tf_op jit(solution)/shard_map/pallas_call | solution.py:357
  63.3 31.1 %all_to_all.27 = f32[128,4,128]{2,1,0:T(4,128)S(1)} all-to-all(f32[128,4,128]{2,1,0:T(4,128)S(1)} %bitcast.15), channel_id=1, replica_groups=mesh['seg_0'=4,'seg_1'=16,'seg_2'=2,'sp'=4] {'seg_0','seg_1','seg_2'}, dimensions={0} | all-to-all | bytes 524288 | tf_op jit(solution)/shard_map/all_to_all | solution.py:371
  94.4 1.5 shard_map.138
  95.9 3.5 %all-to-all-start.3 = ((f32[4,2,16,768]{3,2,1,0:T(8,128)}), f32[4,2,16,768]{3,2,1,0:T(8,128)S(1)}, u32[]{:S(2)}, u32[]{:S(2)}) async-start(f32[4,2,16,768]{3,2,1,0:T(8,128)} %shard_map.138), calls=%async_computation.3 | async-start | bytes 786432 | tf_op jit(solution)/shard_map/all_to_all | solution.py:380
  99.4 0.0 copy-done.12
  99.4 0.2 copy.18.up_ref
  99.6 0.0 copy-start.4
  99.6 0.0 copy-start.5
  99.6 0.0 copy-start.7
  99.6 0.0 copy-start.8
  99.6 0.0 copy-start.10
  99.6 2.1 %copy.17.fit_ref = f32[768,680]{1,0:T(8,128)S(1)} copy(f32[768,680]{0,1:T(8,128)} %param.18) | data formatting | bytes 4177920 | tf_op args[4]
  101.7 3.8 %all-to-all-done.3 = f32[4,2,16,768]{3,2,1,0:T(8,128)S(1)} async-done(((f32[4,2,16,768]{3,2,1,0:T(8,128)}), f32[4,2,16,768]{3,2,1,0:T(8,128)S(1)}, u32[]{:S(2)}, u32[]{:S(2)}) %all-to-all-start.3) | async-done | bytes 393248 | tf_op jit(solution)/shard_map/all_to_all | solution.py:380
  105.6 0.0 copy-done.4
  105.6 0.0 copy-done.5
  105.6 0.0 copy-done.7
  105.6 0.0 copy-done.8
  105.6 0.0 copy-done.10
  105.6 0.0 copy-start
  105.6 0.0 copy-start.1
  105.6 0.0 copy-start.2
  105.7 1.7 %shard_map.139 = (bf16[2,16,680]{2,1,0:T(8,128)(2,1)S(1)}, bf16[2,8,680]{2,1,0:T(8,128)(2,1)S(1)}, bf16[2,8,680]{2,1,0:T(8,128)(2,1)S(1)}, bf16[16,16,384]{2,1,0:T(8,128)(2,1)S(1)}, s32[24,48]{1,0:T(8,128)S(1)}) custom-call(s32[1]{0:T(128)} %bitcast.2.part_ref, s32[1]{0:T(128)} %bitcast.segment_ref, f32[8,8]{1,0:T(8,128)S(1)} %copy-done.10, ...), custom_call_target="tpu_custom_call" | custom-call | tf_op jit(solution)/shard_map/pallas_call | solution.py:386
  107.3 17.5 %all_to_all.28 = bf16[16,16,384]{2,1,0:T(8,128)(2,1)S(1)} all-to-all(bf16[16,16,384]{2,1,0:T(8,128)(2,1)S(1)} %get-tuple-element.18), channel_id=1, replica_groups=mesh['seg_0'=4,'seg_1'=16,'seg_2'=2,'sp'=4] {'seg_1'}, dimensions={0} | all-to-all | bytes 393216 | tf_op jit(solution)/shard_map/all_to_all | solution.py:407
  124.8 11.6 %all_gather.3.mine_ref = bf16[1024,384]{1,0:T(8,128)(2,1)S(1)} all-gather(bf16[256,384]{1,0:T(8,128)(2,1)S(1)} %bitcast.23), channel_id=1, replica_groups=mesh['seg_0'=4,'seg_1'=16,'seg_2'=2,'sp'=4] {'seg_0'}, dimensions={0}, use_global_device_ids=true | all-gather | bytes 983040 | tf_op jit(solution)/shard_map/all_gather | solution.py:408
  136.5 9.4 %collective-permute-start.2 = (bf16[1024,384]{1,0:T(8,128)(2,1)S(1)}, bf16[1024,384]{1,0:T(8,128)(2,1)S(1)}, u32[]{:S(2)}, u32[]{:S(2)}) collective-permute-start(bf16[1024,384]{1,0:T(8,128)(2,1)S(1)} %all_gather.3.mine_ref), channel_id=1, source_target_pairs={{0,4},{4,0},{1,5},{5,1},{2,6},{6,2},{3,7},{7,3},{8,12},{12,8},{9,1... | collective-permute-start | bytes 2359304 | tf_op jit(solution)/shard_map/ppermute | solution.py:409
  145.9 2.9 %collective-permute-start = (bf16[2,8,680]{2,1,0:T(8,128)(2,1)S(1)}, bf16[2,8,680]{2,1,0:T(8,128)(2,1)S(1)}, u32[]{:S(2)}, u32[]{:S(2)}) collective-permute-start(bf16[2,8,680]{2,1,0:T(8,128)(2,1)S(1)} %get-tuple-element.14), channel_id=1, source_target_pairs={{0,4},{4,8},{8,12},{12,16},{16,20},{20,24},{24,28},{28,32},{32,36}... | collective-permute-start | bytes 65288 | tf_op jit(solution)/shard_map/ppermute | solution.py:405
  148.8 1.9 %collective-permute-start.1 = (bf16[2,8,680]{2,1,0:T(8,128)(2,1)S(1)}, bf16[2,8,680]{2,1,0:T(8,128)(2,1)S(1)}, u32[]{:S(2)}, u32[]{:S(2)}) collective-permute-start(bf16[2,8,680]{2,1,0:T(8,128)(2,1)S(1)} %get-tuple-element.16), channel_id=1, source_target_pairs={{4,0},{8,4},{12,8},{16,12},{20,16},{24,20},{28,24},{32,28},{36,32}... | collective-permute-start | bytes 65288 | tf_op jit(solution)/shard_map/ppermute | solution.py:406
  150.7 0.0 collective-permute-done.before_ref
  150.7 3.2 %collective-permute-done.1.after_ref = bf16[2,8,680]{2,1,0:T(8,128)(2,1)S(1)} collective-permute-done((bf16[2,8,680]{2,1,0:T(8,128)(2,1)S(1)}, bf16[2,8,680]{2,1,0:T(8,128)(2,1)S(1)}, u32[]{:S(2)}, u32[]{:S(2)}) %collective-permute-start.1) | collective-permute-done | bytes 21792 | tf_op jit(solution)/shard_map/ppermute | solution.py:406
  153.9 0.0 collective-permute-done.2.other_ref
  153.9 0.0 copy-done
  153.9 0.0 copy-done.1
  153.9 0.0 copy-done.2
  154.0 4.1 %shard_map.140 = f32[2,24,680]{2,1,0:T(8,128)} custom-call(s32[1]{0:T(128)} %bitcast.segment_ref, s32[1]{0:T(128)} %bitcast.1.core_ref, bf16[2,8,680]{2,1,0:T(8,128)(2,1)S(1)} %collective-permute-done.before_ref, bf16[2,16,680]{2,1,0:T(8,128)(2,1)S(1)} %get-tuple-element.15.ghosts_ref, bf16[2,8,680]{2,1,0:T(8,128)(2,1)S(1)} %collective-permute-done.1.after_ref, ...), custom_call_target="tpu_custom_call" | custom-call | tf_op jit(solution)/shard_map/pallas_call | solution.py:411
  (1 shorter events, 0.0 us)
Async XLA Ops:
  0.0 52.4 %copy-start.9 = (s32[1,1920]{1,0:T(1,128)S(1)}, s32[1,1920]{1,0:T(1,128)}, u32[]{:S(2)}) copy-start(s32[1,1920]{1,0:T(1,128)} %constant.28.clone.table_ref) | copy-start | bytes 23044
  0.0 0.9 copy-start.3
  0.9 0.7 copy-start.11
  1.6 50.8 %copy-start.6 = (f32[2,16,680]{2,1,0:T(8,128)S(1)}, f32[2,16,680]{2,1,0:T(8,128)}, u32[]{:S(2)}) copy-start(f32[2,16,680]{2,1,0:T(8,128)} %coeffs_ref.1) | copy-start | bytes 261124
  41.3 58.1 %copy-start.12 = (bf16[680,152]{0,1:T(8,128)(2,1)S(1)}, bf16[680,152]{0,1:T(8,128)(2,1)}, u32[]{:S(2)}) copy-start(bf16[680,152]{0,1:T(8,128)(2,1)} %param.23) | copy-start | bytes 620164
  95.9 9.7 %all-to-all-start.3 = ((f32[4,2,16,768]{3,2,1,0:T(8,128)}), f32[4,2,16,768]{3,2,1,0:T(8,128)S(1)}, u32[]{:S(2)}, u32[]{:S(2)}) async-start(f32[4,2,16,768]{3,2,1,0:T(8,128)} %shard_map.138), calls=%async_computation.3 | async-start | bytes 786432 | tf_op jit(solution)/shard_map/all_to_all | solution.py:380
  99.6 6.0 %copy-start.4 = (s32[2048,16]{0,1:T(8,128)S(1)}, s32[2048,16]{0,1:T(8,128)}, u32[]{:S(2)}) copy-start(s32[2048,16]{0,1:T(8,128)} %param.20) | copy-start | bytes 393220
  99.6 6.0 %copy-start.5 = (s32[2048,16]{0,1:T(8,128)S(1)}, s32[2048,16]{0,1:T(8,128)}, u32[]{:S(2)}) copy-start(s32[2048,16]{0,1:T(8,128)} %param.21) | copy-start | bytes 393220
  99.6 6.0 %copy-start.7 = (s32[2048,8]{0,1:T(8,128)S(1)}, s32[2048,8]{0,1:T(8,128)}, u32[]{:S(2)}) copy-start(s32[2048,8]{0,1:T(8,128)} %param.24) | copy-start | bytes 196612
  99.6 6.0 %copy-start.8 = (s32[2048]{0:T(1024)S(1)}, s32[2048]{0:T(1024)}, u32[]{:S(2)}) copy-start(s32[2048]{0:T(1024)} %param.19) | copy-start | bytes 24580
  99.6 6.0 %copy-start.10 = (f32[8,8]{1,0:T(8,128)S(1)}, f32[8,8]{1,0:T(8,128)}, u32[]{:S(2)}) copy-start(f32[8,8]{1,0:T(8,128)} %reaction_ref.1) | copy-start | bytes 772
  105.6 48.3 %copy-start = (bf16[2,680,680]{2,1,0:T(8,128)(2,1)S(1)}, bf16[2,680,680]{2,1,0:T(8,128)(2,1)}, u32[]{:S(2)}) copy-start(bf16[2,680,680]{2,1,0:T(8,128)(2,1)} %near_mat_hbm.1) | copy-start | bytes 5548804
  105.6 48.3 %copy-start.1 = (bf16[8,152,152]{2,1,0:T(8,128)(2,1)S(1)}, bf16[8,152,152]{2,1,0:T(8,128)(2,1)}, u32[]{:S(2)}) copy-start(bf16[8,152,152]{2,1,0:T(8,128)(2,1)} %trans_hbm.1) | copy-start | bytes 1108996
  105.6 48.3 %copy-start.2 = (bf16[152,680]{1,0:T(8,128)(2,1)S(1)}, bf16[152,680]{1,0:T(8,128)(2,1)}, u32[]{:S(2)}) copy-start(bf16[152,680]{1,0:T(8,128)(2,1)} %down_hbm.1) | copy-start | bytes 620164
  136.5 17.5 %collective-permute-start.2 = (bf16[1024,384]{1,0:T(8,128)(2,1)S(1)}, bf16[1024,384]{1,0:T(8,128)(2,1)S(1)}, u32[]{:S(2)}, u32[]{:S(2)}) collective-permute-start(bf16[1024,384]{1,0:T(8,128)(2,1)S(1)} %all_gather.3.mine_ref), channel_id=1, source_target_pairs={{0,4},{4,0},{1,5},{5,1},{2,6},{6,2},{3,7},{7,3},{8,12},{12,8},{9,1... | collective-permute-start | bytes 2359304 | tf_op jit(solution)/shard_map/ppermute | solution.py:409
  145.9 4.8 %collective-permute-start = (bf16[2,8,680]{2,1,0:T(8,128)(2,1)S(1)}, bf16[2,8,680]{2,1,0:T(8,128)(2,1)S(1)}, u32[]{:S(2)}, u32[]{:S(2)}) collective-permute-start(bf16[2,8,680]{2,1,0:T(8,128)(2,1)S(1)} %get-tuple-element.14), channel_id=1, source_target_pairs={{0,4},{4,8},{8,12},{12,16},{16,20},{20,24},{24,28},{28,32},{32,36}... | collective-permute-start | bytes 65288 | tf_op jit(solution)/shard_map/ppermute | solution.py:405
  148.8 5.1 %collective-permute-start.1 = (bf16[2,8,680]{2,1,0:T(8,128)(2,1)S(1)}, bf16[2,8,680]{2,1,0:T(8,128)(2,1)S(1)}, u32[]{:S(2)}, u32[]{:S(2)}) collective-permute-start(bf16[2,8,680]{2,1,0:T(8,128)(2,1)S(1)} %get-tuple-element.16), channel_id=1, source_target_pairs={{4,0},{8,4},{12,8},{16,12},{20,16},{24,20},{28,24},{32,28},{36,32}... | collective-permute-start | bytes 65288 | tf_op jit(solution)/shard_map/ppermute | solution.py:406

commit v4 on v3

--- a/solution.py
+++ b/solution.py
@@ -97,15 +97,12 @@
             request_ref[pl.ds(place_ref[leaf * blocks + m], 1), :] = jnp.where(part == 3, index, line)
 
 
-def evaluate_kernel(index_ref, request_ref, coeffs_ref, table_ref, out_ref, split_ref, left_ref, x_ref, y_ref, z_ref):
+def arrange_kernel(coeffs_ref, table_ref, left_ref, split_ref):
     species, leaves, width = coeffs_ref.shape
     per_leaf = 4 * 16
     stride = per_leaf + 8
     split_ref[...] = jnp.zeros_like(split_ref)
-    parts = []
-    for s in range(species):
-        parts.append(coeffs_ref[s])
-    both = jnp.concatenate(parts, axis=0)
+    both = jnp.concatenate([coeffs_ref[s] for s in range(species)], axis=0)
     rest = both - both.astype(BF16).astype(F32)
     stacked = jnp.concatenate([both, rest], axis=0).astype(BF16)
     for k in range(DEG):
@@ -123,6 +120,8 @@
         upper = jnp.concatenate([block[:half], jnp.zeros_like(block[:half])], axis=0)
         left_ref[leaf] = jnp.concatenate([block, upper], axis=1).astype(BF16)
 
+
+def evaluate_kernel(species, index_ref, request_ref, left_ref, out_ref, x_ref, y_ref, z_ref):
     y_ref[...] = jnp.zeros_like(y_ref)
     z_ref[...] = jnp.zeros_like(z_ref)
     row = lax.broadcasted_iota(jnp.int32, (8, PB), 0)
@@ -230,8 +229,8 @@
 
 
 def update_kernel(
-    total_leaves, near, segment_ref, core_ref, before_ref, ghosts_ref, after_ref, lists_ref, near_mat_hbm, mine_ref,
-    other_ref, trans_hbm, down_hbm, out_ref, wide_ref, near_mat_ref, trans_ref, down_ref, sems,
+    total_leaves, near, segment_ref, core_ref, before_ref, ghosts_ref, after_ref, lists_ref, near_mat_ref, mine_ref,
+    other_ref, trans_ref, down_ref, out_ref, wide_ref,
 ):
     segment = segment_ref[0]
     core = core_ref[0]
@@ -239,12 +238,6 @@
     leaves = ghosts_ref.shape[1]
     span = leaves + 2 * MARGIN
     operators = trans_ref.shape[0]
-    fetches = []
-    for n, (ref, held) in enumerate(
-        ((trans_hbm, trans_ref), (down_hbm, down_ref), (near_mat_hbm, near_mat_ref))
-    ):
-        fetches.append(pltpu.make_async_copy(ref, held, sems.at[n]))
-        fetches[-1].start()
     start = segment * leaves - MOVE
     lists = lists_ref[...]
     source = lists[:, :near]
@@ -268,14 +261,12 @@
         part = jnp.dot(pick, table[...], preferred_element_type=F32)
         taken = part if taken is None else taken + part
     points = trans_ref.shape[1]
-    fetches[0].wait()
     local = None
     for o in range(operators):
         lines = taken[o * slots : (o + 1) * slots]
         both = jnp.concatenate([lines[:, s * points : (s + 1) * points] for s in range(species)], axis=0)
         term = jnp.dot(both.astype(BF16), trans_ref[o], preferred_element_type=F32)
         local = term if local is None else local + term
-    fetches[1].wait()
     total = jnp.dot(local.astype(BF16), down_ref[...], preferred_element_type=F32)
 
     offset = jnp.where(live & (source >= 0), source - (segment * leaves - MARGIN), -1)
@@ -297,7 +288,6 @@
         around.append(wide_ref[s].astype(BF16))
     total = total + jnp.concatenate(own, axis=0)
     rows = species * slots
-    fetches[2].wait()
     for o in range(near_mat_ref.shape[0]):
         weight = weights[o].astype(BF16)
         grouped = jnp.concatenate(
@@ -348,26 +338,32 @@
             pltpu.SemaphoreType.DMA,
             pltpu.SemaphoreType.DMA,
         ],
-        compiler_params=within(4),
+        compiler_params=within(60),
     )(part_id, owner_leaf.T, points)
     request = lax.all_to_all(request.reshape(segments, CAP, PB), SEG, 0, 0, tiled=True)
+    left = pl.pallas_call(
+        arrange_kernel,
+        out_shape=shape((leaves, 64, 2 * PB), BF16),
+        in_specs=spaces("vv"),
+        out_specs=spaces("v")[0],
+        scratch_shapes=[pltpu.VMEM((leaves * 72, PB), F32)],
+        compiler_params=within(8),
+    )(coeffs, jnp.asarray(coefficient_table()))
     request = jnp.broadcast_to(request.reshape(1, slots, PB), (parts, slots, PB))
     request = lax.all_to_all(request, "sp", 0, 0, tiled=True)
     index = jnp.clip(request[3, :, 0].astype(jnp.int32), 0, leaves - 1)
     answers = pl.pallas_call(
-        evaluate_kernel,
+        functools.partial(evaluate_kernel, species),
         out_shape=shape((slots * species, PB), F32),
-        in_specs=spaces("svvv"),
+        in_specs=spaces("svv"),
         out_specs=spaces("v")[0],
         scratch_shapes=[
-            pltpu.VMEM((leaves * 72, PB), F32),
-            pltpu.VMEM((leaves, 64, 2 * PB), BF16),
             pltpu.VMEM((DEG * 8, PB), F32),
             pltpu.VMEM((8 * 24, PB), F32),
             pltpu.VMEM((8 * 24, PB), F32),
         ],
         compiler_params=within(16),
-    )(index, request, coeffs, jnp.asarray(coefficient_table()))
+    )(index, request, left)
     answers = lax.all_to_all(answers.reshape(segments, CAP * species, PB), SEG, 0, 0, tiled=True)
     values = pl.pallas_call(
         collect_kernel,
@@ -411,16 +407,10 @@
     return pl.pallas_call(
         functools.partial(update_kernel, new_seg.shape[0], near),
         out_shape=shape((species, slot_total, width), F32),
-        in_specs=spaces("ssvvvvhvvhh"),
+        in_specs=spaces("ssvvvvvvvvv"),
         out_specs=spaces("v")[0],
-        scratch_shapes=[
-            pltpu.VMEM((species, leaves + 2 * MARGIN, width), F32),
-            pltpu.VMEM(near_mat.shape, BF16),
-            pltpu.VMEM(trans_mat.shape, BF16),
-            pltpu.VMEM(down_mat.shape, BF16),
-            pltpu.SemaphoreType.DMA((3,)),
-        ],
-        compiler_params=within(24),
+        scratch_shapes=[pltpu.VMEM((species, leaves + 2 * MARGIN, width), F32)],
+        compiler_params=within(10),
     )(
         segment_id, jnp.full((1,), lax.axis_index("seg_2"), jnp.int32), before, ghosts, after, lists, near_mat, mine,
         other, trans_mat, down_mat,

time: 159 us -> 156 us (0.981)
  blocking collectives: 109 us -> 98 us
  waiting for transfers between devices: 7.06 us -> 13.5 us
  starting transfers between devices: 17.7 us -> 21.7 us
    all_to_all x1 -> x0, blocking collectives: 11 us -> none  [shards(): request = lax.all_to_all(request, 'sp', 0, 0, tiled=True)]
    all_to_all x0 -> x1, waiting for transfers between devices: none -> 6.43 us  [shards(): request = lax.all_to_all(request, 'sp', 0, 0, tiled=True)]
    all_to_all x0 -> x1, starting transfers between devices: none -> 4.01 us  [shards(): request = lax.all_to_all(request, 'sp', 0, 0, tiled=True)]
    unnamed x28 -> x26, local copies, waits for them, and re-layouts: 3.92 us -> 2.31 us
    pallas_call x1 -> x2, Pallas kernels: 10.8 us -> 10.8 us  [the longest x1 10.1 us: shards(): pl.pallas_call(functools.partial(evaluate_kernel, species), out_shape=sha...]
  transfers between devices with their start and end apart: 4 -> 5, of which waited for: 2 -> 3; matrix products, arithmetic and copies ran while one was open for 1% -> 1% of each run, Pallas kernels for 0% -> 0%
where the time goes in v4:
time: 156 us
  blocking collectives  98 us (63%)
  starting transfers between devices  21.7 us (14%)
  Pallas kernels  19.2 us (12%)
  waiting for transfers between devices  13.5 us (9%)
  local copies, waits for them, and re-layouts  3.16 us (2%)
    all_to_all x1, blocking collectives, shards(): lax.all_to_all(request.reshape(segments, CAP, PB), SEG, 0, 0, tiled=True)  37.9 us
    all_to_all x1, blocking collectives, shards(): lax.all_to_all(answers.reshape(segments, CAP * species, PB), SEG, 0, 0, t...  31 us
    all_to_all x1, blocking collectives, shards(): along_z = lax.all_to_all(spread, 'seg_1', 0, 0, tiled=True)  17.5 us
    all_gather x1, blocking collectives, shards(): lax.all_gather(along_z.reshape(z_size * leaves, LANES), 'seg_0', axis=0,...  11.6 us
    pallas_call x1, Pallas kernels, shards(): pl.pallas_call(functools.partial(evaluate_kernel, species), out_shape=sha...  10.1 us
    ppermute x1, starting transfers between devices, shards(): other = lax.ppermute(mine, 'seg_2', [(0, 1), (1, 0)])  9.41 us
    all_to_all x1, waiting for transfers between devices, shards(): request = lax.all_to_all(request, 'sp', 0, 0, tiled=True)  6.43 us
    all_to_all x1, starting transfers between devices, shards(): request = lax.all_to_all(request, 'sp', 0, 0, tiled=True)  4.01 us
  transfers between devices with their start and end apart: 5, of which 3 were waited for; matrix products, arithmetic and copies ran while one was open for 1% of the time, Pallas kernels for 0%

profile of v4, /device:TPU:1, one launch (start us, length us, event | category | flops | bytes accessed | tf_op | source)
XLA Modules:
  0.0 155.8 jit_solution(16757430241064703108)
XLA Ops:
  0.0 0.0 copy-start.8
  0.0 0.0 copy-start.5
  0.0 2.3 %shard_map.136 = (f32[256,128]{1,0:T(8,128)}, s32[96]{0:T(128)}) custom-call(s32[1]{0:T(128)} %bitcast.2.part_ref, s32[6,16]{1,0:T(8,128)} %bitcast.24, f32[3,16,768]{2,1,0:T(8,128)} %points_ref.1), custom_call_target="tpu_custom_call" | custom-call | tf_op jit(solution)/shard_map/pallas_call | solution.py:328
  2.3 37.9 %all_to_all.25 = f32[128,2,128]{2,1,0:T(2,128)S(1)} all-to-all(f32[128,2,128]{2,1,0:T(2,128)} %bitcast.23), channel_id=1, replica_groups=mesh['seg_0'=4,'seg_1'=16,'seg_2'=2,'sp'=4] {'seg_0','seg_1','seg_2'}, dimensions={0} | all-to-all | bytes 262144 | tf_op jit(solution)/shard_map/all_to_all | solution.py:343
  40.2 0.0 copy-start.10
  40.2 0.8 broadcast_in_dim.20
  41.1 4.0 %all-to-all-start.1 = ((f32[4,256,128]{2,1,0:T(8,128)}), f32[4,256,128]{2,1,0:T(8,128)S(1)}, u32[]{:S(2)}, u32[]{:S(2)}) async-start(f32[4,256,128]{2,1,0:T(8,128)} %broadcast_in_dim.20), calls=%async_computation.1 | async-start | bytes 1048576 | tf_op jit(solution)/shard_map/all_to_all | solution.py:353
  45.1 0.0 copy-done.8
  45.1 0.0 copy-done.5
  45.1 0.0 copy-start.11
  45.1 0.7 shard_map.137.left_ref
  45.8 6.4 %all-to-all-done.1.request_ref = f32[4,256,128]{2,1,0:T(8,128)S(1)} async-done(((f32[4,256,128]{2,1,0:T(8,128)}), f32[4,256,128]{2,1,0:T(8,128)S(1)}, u32[]{:S(2)}, u32[]{:S(2)}) %all-to-all-start.1) | async-done | bytes 524320 | tf_op jit(solution)/shard_map/all_to_all | solution.py:353
  52.2 0.1 fusion.1.index_ref
  52.4 10.1 %shard_map.138 = f32[512,128]{1,0:T(8,128)S(1)} custom-call(s32[256]{0:T(256)S(1)} %fusion.1.index_ref, f32[4,256,128]{2,1,0:T(8,128)S(1)} %all-to-all-done.1.request_ref, bf16[16,64,256]{2,1,0:T(8,128)(2,1)S(1)} %shard_map.137.left_ref), custom_call_target="tpu_custom_call" | custom-call | tf_op jit(solution)/shard_map/pallas_call | solution.py:355
  62.5 31.0 %all_to_all.26 = f32[128,4,128]{2,1,0:T(4,128)S(1)} all-to-all(f32[128,4,128]{2,1,0:T(4,128)S(1)} %bitcast.16), channel_id=1, replica_groups=mesh['seg_0'=4,'seg_1'=16,'seg_2'=2,'sp'=4] {'seg_0','seg_1','seg_2'}, dimensions={0} | all-to-all | bytes 524288 | tf_op jit(solution)/shard_map/all_to_all | solution.py:367
  93.5 0.0 copy-done.10
  93.5 1.5 shard_map.139
  95.0 3.5 %all-to-all-start.3 = ((f32[4,2,16,768]{3,2,1,0:T(8,128)}), f32[4,2,16,768]{3,2,1,0:T(8,128)S(1)}, u32[]{:S(2)}, u32[]{:S(2)}) async-start(f32[4,2,16,768]{3,2,1,0:T(8,128)} %shard_map.139), calls=%async_computation.3 | async-start | bytes 786432 | tf_op jit(solution)/shard_map/all_to_all | solution.py:376
  98.5 0.0 copy-done.11
  98.5 0.2 copy.18.up_ref
  98.7 0.0 copy-start.3
  98.7 0.0 copy-start.4
  98.7 0.0 copy-start.6
  98.7 0.0 copy-start.7
  98.7 0.0 copy-start.9
  98.7 2.1 %copy.17.fit_ref = f32[768,680]{1,0:T(8,128)S(1)} copy(f32[768,680]{0,1:T(8,128)} %param.18) | data formatting | bytes 4177920 | tf_op args[4]
  100.8 3.8 %all-to-all-done.3 = f32[4,2,16,768]{3,2,1,0:T(8,128)S(1)} async-done(((f32[4,2,16,768]{3,2,1,0:T(8,128)}), f32[4,2,16,768]{3,2,1,0:T(8,128)S(1)}, u32[]{:S(2)}, u32[]{:S(2)}) %all-to-all-start.3) | async-done | bytes 393248 | tf_op jit(solution)/shard_map/all_to_all | solution.py:376
  104.7 0.0 copy-done.3
  104.7 0.0 copy-done.4
  104.7 0.0 copy-done.6
  104.7 0.0 copy-done.7
  104.7 0.0 copy-done.9
  104.7 0.0 copy-start
  104.7 0.0 copy-start.1
  104.7 0.0 copy-start.2
  104.7 1.7 %shard_map.140 = (bf16[2,16,680]{2,1,0:T(8,128)(2,1)S(1)}, bf16[2,8,680]{2,1,0:T(8,128)(2,1)S(1)}, bf16[2,8,680]{2,1,0:T(8,128)(2,1)S(1)}, bf16[16,16,384]{2,1,0:T(8,128)(2,1)S(1)}, s32[24,48]{1,0:T(8,128)S(1)}) custom-call(s32[1]{0:T(128)} %bitcast.2.part_ref, s32[1]{0:T(128)} %bitcast.segment_ref, f32[8,8]{1,0:T(8,128)S(1)} %copy-done.9, ...), custom_call_target="tpu_custom_call" | custom-call | tf_op jit(solution)/shard_map/pallas_call | solution.py:382
  106.4 17.5 %all_to_all.27 = bf16[16,16,384]{2,1,0:T(8,128)(2,1)S(1)} all-to-all(bf16[16,16,384]{2,1,0:T(8,128)(2,1)S(1)} %get-tuple-element.18), channel_id=1, replica_groups=mesh['seg_0'=4,'seg_1'=16,'seg_2'=2,'sp'=4] {'seg_1'}, dimensions={0} | all-to-all | bytes 393216 | tf_op jit(solution)/shard_map/all_to_all | solution.py:403
  123.9 11.6 %all_gather.3.mine_ref = bf16[1024,384]{1,0:T(8,128)(2,1)S(1)} all-gather(bf16[256,384]{1,0:T(8,128)(2,1)S(1)} %bitcast.21), channel_id=1, replica_groups=mesh['seg_0'=4,'seg_1'=16,'seg_2'=2,'sp'=4] {'seg_0'}, dimensions={0}, use_global_device_ids=true | all-gather | bytes 983040 | tf_op jit(solution)/shard_map/all_gather | solution.py:404
  135.5 9.4 %collective-permute-start.2 = (bf16[1024,384]{1,0:T(8,128)(2,1)S(1)}, bf16[1024,384]{1,0:T(8,128)(2,1)S(1)}, u32[]{:S(2)}, u32[]{:S(2)}) collective-permute-start(bf16[1024,384]{1,0:T(8,128)(2,1)S(1)} %all_gather.3.mine_ref), channel_id=1, source_target_pairs={{0,4},{4,0},{1,5},{5,1},{2,6},{6,2},{3,7},{7,3},{8,12},{12,8},{9,1... | collective-permute-start | bytes 2359304 | tf_op jit(solution)/shard_map/ppermute | solution.py:405
  145.0 2.9 %collective-permute-start = (bf16[2,8,680]{2,1,0:T(8,128)(2,1)S(1)}, bf16[2,8,680]{2,1,0:T(8,128)(2,1)S(1)}, u32[]{:S(2)}, u32[]{:S(2)}) collective-permute-start(bf16[2,8,680]{2,1,0:T(8,128)(2,1)S(1)} %get-tuple-element.14), channel_id=1, source_target_pairs={{0,4},{4,8},{8,12},{12,16},{16,20},{20,24},{24,28},{28,32},{32,36}... | collective-permute-start | bytes 65288 | tf_op jit(solution)/shard_map/ppermute | solution.py:401
  147.9 1.9 %collective-permute-start.1 = (bf16[2,8,680]{2,1,0:T(8,128)(2,1)S(1)}, bf16[2,8,680]{2,1,0:T(8,128)(2,1)S(1)}, u32[]{:S(2)}, u32[]{:S(2)}) collective-permute-start(bf16[2,8,680]{2,1,0:T(8,128)(2,1)S(1)} %get-tuple-element.16), channel_id=1, source_target_pairs={{4,0},{8,4},{12,8},{16,12},{20,16},{24,20},{28,24},{32,28},{36,32}... | collective-permute-start | bytes 65288 | tf_op jit(solution)/shard_map/ppermute | solution.py:402
  149.8 0.0 collective-permute-done.before_ref
  149.8 3.2 %collective-permute-done.1.after_ref = bf16[2,8,680]{2,1,0:T(8,128)(2,1)S(1)} collective-permute-done((bf16[2,8,680]{2,1,0:T(8,128)(2,1)S(1)}, bf16[2,8,680]{2,1,0:T(8,128)(2,1)S(1)}, u32[]{:S(2)}, u32[]{:S(2)}) %collective-permute-start.1) | collective-permute-done | bytes 21792 | tf_op jit(solution)/shard_map/ppermute | solution.py:402
  153.0 0.0 collective-permute-done.2.other_ref
  153.0 0.0 copy-done
  153.0 0.0 copy-done.1
  153.0 0.0 copy-done.2
  153.0 2.8 %shard_map.141 = f32[2,24,680]{2,1,0:T(8,128)} custom-call(s32[1]{0:T(128)} %bitcast.segment_ref, s32[1]{0:T(128)} %bitcast.1.core_ref, bf16[2,8,680]{2,1,0:T(8,128)(2,1)S(1)} %collective-permute-done.before_ref, bf16[2,16,680]{2,1,0:T(8,128)(2,1)S(1)} %get-tuple-element.15.ghosts_ref, bf16[2,8,680]{2,1,0:T(8,128)(2,1)S(1)} %collective-permute-done.1.after_ref, ...), custom_call_target="tpu_custom_call" | custom-call | tf_op jit(solution)/shard_map/pallas_call | solution.py:407
Async XLA Ops:
  0.0 45.1 %copy-start.8 = (s32[1,1920]{1,0:T(1,128)S(1)}, s32[1,1920]{1,0:T(1,128)}, u32[]{:S(2)}) copy-start(s32[1,1920]{1,0:T(1,128)} %constant.28.clone.table_ref) | copy-start | bytes 23044
  0.0 45.1 %copy-start.5 = (f32[2,16,680]{2,1,0:T(8,128)S(1)}, f32[2,16,680]{2,1,0:T(8,128)}, u32[]{:S(2)}) copy-start(f32[2,16,680]{2,1,0:T(8,128)} %coeffs_ref.1) | copy-start | bytes 261124
  40.2 53.3 %copy-start.10 = (s32[96]{0:T(128)S(1)}, s32[96]{0:T(128)}, u32[]{:S(2)}) copy-start(s32[96]{0:T(128)} %get-tuple-element.12.place_ref) | copy-start | bytes 1156
  41.1 11.2 %all-to-all-start.1 = ((f32[4,256,128]{2,1,0:T(8,128)}), f32[4,256,128]{2,1,0:T(8,128)S(1)}, u32[]{:S(2)}, u32[]{:S(2)}) async-start(f32[4,256,128]{2,1,0:T(8,128)} %broadcast_in_dim.20), calls=%async_computation.1 | async-start | bytes 1048576 | tf_op jit(solution)/shard_map/all_to_all | solution.py:353
  45.1 53.4 %copy-start.11 = (bf16[680,152]{0,1:T(8,128)(2,1)S(1)}, bf16[680,152]{0,1:T(8,128)(2,1)}, u32[]{:S(2)}) copy-start(bf16[680,152]{0,1:T(8,128)(2,1)} %param.23) | copy-start | bytes 620164
  95.0 9.7 %all-to-all-start.3 = ((f32[4,2,16,768]{3,2,1,0:T(8,128)}), f32[4,2,16,768]{3,2,1,0:T(8,128)S(1)}, u32[]{:S(2)}, u32[]{:S(2)}) async-start(f32[4,2,16,768]{3,2,1,0:T(8,128)} %shard_map.139), calls=%async_computation.3 | async-start | bytes 786432 | tf_op jit(solution)/shard_map/all_to_all | solution.py:376
  98.7 6.0 %copy-start.3 = (s32[2048,16]{0,1:T(8,128)S(1)}, s32[2048,16]{0,1:T(8,128)}, u32[]{:S(2)}) copy-start(s32[2048,16]{0,1:T(8,128)} %param.20) | copy-start | bytes 393220
  98.7 6.0 %copy-start.4 = (s32[2048,16]{0,1:T(8,128)S(1)}, s32[2048,16]{0,1:T(8,128)}, u32[]{:S(2)}) copy-start(s32[2048,16]{0,1:T(8,128)} %param.21) | copy-start | bytes 393220
  98.7 6.0 %copy-start.6 = (s32[2048,8]{0,1:T(8,128)S(1)}, s32[2048,8]{0,1:T(8,128)}, u32[]{:S(2)}) copy-start(s32[2048,8]{0,1:T(8,128)} %param.24) | copy-start | bytes 196612
  98.7 6.0 %copy-start.7 = (s32[2048]{0:T(1024)S(1)}, s32[2048]{0:T(1024)}, u32[]{:S(2)}) copy-start(s32[2048]{0:T(1024)} %param.19) | copy-start | bytes 24580
  98.7 6.0 %copy-start.9 = (f32[8,8]{1,0:T(8,128)S(1)}, f32[8,8]{1,0:T(8,128)}, u32[]{:S(2)}) copy-start(f32[8,8]{1,0:T(8,128)} %reaction_ref.1) | copy-start | bytes 772
  104.7 48.3 %copy-start = (bf16[2,680,680]{2,1,0:T(8,128)(2,1)S(1)}, bf16[2,680,680]{2,1,0:T(8,128)(2,1)}, u32[]{:S(2)}) copy-start(bf16[2,680,680]{2,1,0:T(8,128)(2,1)} %near_mat_ref.1) | copy-start | bytes 5548804
  104.7 48.3 %copy-start.1 = (bf16[8,152,152]{2,1,0:T(8,128)(2,1)S(1)}, bf16[8,152,152]{2,1,0:T(8,128)(2,1)}, u32[]{:S(2)}) copy-start(bf16[8,152,152]{2,1,0:T(8,128)(2,1)} %trans_ref.1) | copy-start | bytes 1108996
  104.7 48.3 %copy-start.2 = (bf16[152,680]{1,0:T(8,128)(2,1)S(1)}, bf16[152,680]{1,0:T(8,128)(2,1)}, u32[]{:S(2)}) copy-start(bf16[152,680]{1,0:T(8,128)(2,1)} %down_ref.1) | copy-start | bytes 620164
  135.5 17.5 %collective-permute-start.2 = (bf16[1024,384]{1,0:T(8,128)(2,1)S(1)}, bf16[1024,384]{1,0:T(8,128)(2,1)S(1)}, u32[]{:S(2)}, u32[]{:S(2)}) collective-permute-start(bf16[1024,384]{1,0:T(8,128)(2,1)S(1)} %all_gather.3.mine_ref), channel_id=1, source_target_pairs={{0,4},{4,0},{1,5},{5,1},{2,6},{6,2},{3,7},{7,3},{8,12},{12,8},{9,1... | collective-permute-start | bytes 2359304 | tf_op jit(solution)/shard_map/ppermute | solution.py:405
  145.0 4.8 %collective-permute-start = (bf16[2,8,680]{2,1,0:T(8,128)(2,1)S(1)}, bf16[2,8,680]{2,1,0:T(8,128)(2,1)S(1)}, u32[]{:S(2)}, u32[]{:S(2)}) collective-permute-start(bf16[2,8,680]{2,1,0:T(8,128)(2,1)S(1)} %get-tuple-element.14), channel_id=1, source_target_pairs={{0,4},{4,8},{8,12},{12,16},{16,20},{20,24},{24,28},{28,32},{32,36}... | collective-permute-start | bytes 65288 | tf_op jit(solution)/shard_map/ppermute | solution.py:401
  147.9 5.1 %collective-permute-start.1 = (bf16[2,8,680]{2,1,0:T(8,128)(2,1)S(1)}, bf16[2,8,680]{2,1,0:T(8,128)(2,1)S(1)}, u32[]{:S(2)}, u32[]{:S(2)}) collective-permute-start(bf16[2,8,680]{2,1,0:T(8,128)(2,1)S(1)} %get-tuple-element.16), channel_id=1, source_target_pairs={{4,0},{8,4},{12,8},{16,12},{20,16},{24,20},{28,24},{32,28},{36,32}... | collective-permute-start | bytes 65288 | tf_op jit(solution)/shard_map/ppermute | solution.py:402

commit v5 on v4

--- a/solution.py
+++ b/solution.py
@@ -158,7 +158,7 @@
                 out_ref[pl.ds(group * 16 + i * 2 + s, 1), :] = line
 
 
-def collect_kernel(place_ref, rows_ref, out_ref, line_ref):
+def collect_kernel(place_ref, rows_ref, own_ref, out_ref, line_ref):
     copies, species, leaves, _ = out_ref.shape
 
     @pl.loop(0, leaves)
@@ -172,12 +172,18 @@
     for s in range(species):
         for m in range(BLOCKS):
             at = (s * BLOCKS + m) * leaves
+            piece = line_ref[at : at + leaves]
+            own_ref[s, :, m * PB : (m + 1) * PB] = piece
             for c in range(copies):
-                out_ref[c, s, :, m * PB : (m + 1) * PB] = line_ref[at : at + leaves]
+                out_ref[c, s, :, m * PB : (m + 1) * PB] = piece.astype(BF16)
+
+
+def parts_kernel(turned_ref, parts_ref):
+    parts_ref[0], parts_ref[1] = high_low(turned_ref[...].T)
 
 
 def fit_kernel(
-    part_ref, segment_ref, reaction_ref, values_ref, fit_ref, up_ref, near_src_ref, near_op_ref, far_src_ref,
+    part_ref, segment_ref, reaction_ref, own_ref, values_ref, fit_ref, up_ref, near_src_ref, near_op_ref, far_src_ref,
     new_seg_ref, ghosts_ref, first_ref, last_ref, equivalent_ref, lists_ref, window_ref, owned_ref, sems,
 ):
     part = part_ref[0]
@@ -196,17 +202,19 @@
     reacted = []
     for s in range(species):
         row = part * species + s
-        mixing = reaction_ref[row, 0] * values_ref[0]
+        mixing = reaction_ref[row, 0] * values_ref[0].astype(F32)
         for r in range(1, all_species):
-            mixing = mixing + reaction_ref[row, r] * values_ref[r]
-        reacted.append(values_ref[row] + jnp.tanh(mixing))
+            mixing = mixing + reaction_ref[row, r] * values_ref[r].astype(F32)
+        for r in range(species):
+            mine = part * species + r
+            mixing = mixing + reaction_ref[row, mine] * (own_ref[r] - values_ref[mine].astype(F32))
+        reacted.append(own_ref[s] + jnp.tanh(mixing))
     reacted = jnp.concatenate(reacted, axis=0)
     rows = species * leaves
     high = reacted.astype(BF16)
     stacked = jnp.concatenate([reacted, reacted - high.astype(F32)], axis=0).astype(BF16)
-    fit_high, fit_low = high_low(fit_ref[...])
-    first = jnp.dot(stacked, fit_high, preferred_element_type=F32)
-    second = jnp.dot(high, fit_low, preferred_element_type=F32)
+    first = jnp.dot(stacked, fit_ref[0], preferred_element_type=F32)
+    second = jnp.dot(high, fit_ref[1], preferred_element_type=F32)
     ghosts = (first[:rows] + first[rows:] + second).astype(BF16)
     equivalent = jnp.dot(ghosts, up_ref[...], preferred_element_type=F32).astype(BF16)
     points = up_ref.shape[1]
@@ -365,11 +373,20 @@
         compiler_params=within(16),
     )(index, request, left)
     answers = lax.all_to_all(answers.reshape(segments, CAP * species, PB), SEG, 0, 0, tiled=True)
-    values = pl.pallas_call(
+    fit_parts = pl.pallas_call(
+        parts_kernel,
+        out_shape=shape((2,) + fit_matrix.shape, BF16),
+        in_specs=spaces("v"),
+        out_specs=spaces("v")[0],
+        compiler_params=within(12),
+    )(fit_matrix.T)
+    own, values = pl.pallas_call(
         collect_kernel,
-        out_shape=shape((parts, species, leaves, BLOCKS * PB), F32),
+        out_shape=(
+            shape((species, leaves, BLOCKS * PB), F32), shape((parts, species, leaves, BLOCKS * PB), BF16),
+        ),
         in_specs=spaces("sv"),
-        out_specs=spaces("v")[0],
+        out_specs=tuple(spaces("vv")),
         scratch_shapes=[pltpu.VMEM((species * leaves * BLOCKS, PB), F32)],
         compiler_params=within(4),
     )(place, answers.reshape(slots * species, PB))
@@ -385,14 +402,14 @@
             shape((species, leaves, width), BF16), edge, edge, shape((z_size, leaves, LANES), BF16),
             shape((slot_total, listed), jnp.int32),
         ),
-        in_specs=spaces("sssvvvhhhh"),
+        in_specs=spaces("sssvvvvhhhh"),
         out_specs=tuple(spaces("vvvvv")),
         scratch_shapes=[
             pltpu.VMEM((listed - 8, 256), jnp.int32), pltpu.VMEM((1, 256), jnp.int32), pltpu.SemaphoreType.DMA((4,)),
         ],
         compiler_params=within(24),
     )(
-        part_id, segment_id, reaction, gathered, fit_matrix, up_mat, near_src.T, near_op.T, far_src.T,
+        part_id, segment_id, reaction, own, gathered, fit_parts, up_mat, near_src.T, near_op.T, far_src.T,
         new_seg.reshape(1, -1),
     )
 

time: 156 us -> 154 us (0.987)
  transfers between devices with their start and end apart: 5 -> 5, of which waited for: 3 -> 3; matrix products, arithmetic and copies ran while one was open for 1% -> 0% of each run, Pallas kernels for 0% -> 1%
where the time goes in v5:
time: 154 us
  blocking collectives  97.1 us (63%)
  starting transfers between devices  21.6 us (14%)
  Pallas kernels  19.7 us (13%)
  waiting for transfers between devices  12.3 us (8%)
  local copies, waits for them, and re-layouts  2.63 us (2%)
    all_to_all x1, blocking collectives, shards(): lax.all_to_all(request.reshape(segments, CAP, PB), SEG, 0, 0, tiled=True)  37.9 us
    all_to_all x1, blocking collectives, shards(): lax.all_to_all(answers.reshape(segments, CAP * species, PB), SEG, 0, 0, t...  31 us
    all_to_all x1, blocking collectives, shards(): along_z = lax.all_to_all(spread, 'seg_1', 0, 0, tiled=True)  16.5 us
    all_gather x1, blocking collectives, shards(): lax.all_gather(along_z.reshape(z_size * leaves, LANES), 'seg_0', axis=0,...  11.8 us
    pallas_call x1, Pallas kernels, shards(): pl.pallas_call(functools.partial(evaluate_kernel, species), out_shape=sha...  10.1 us
    ppermute x1, starting transfers between devices, shards(): other = lax.ppermute(mine, 'seg_2', [(0, 1), (1, 0)])  9.41 us
    all_to_all x1, waiting for transfers between devices, shards(): request = lax.all_to_all(request, 'sp', 0, 0, tiled=True)  6.44 us
    all_to_all x1, starting transfers between devices, shards(): request = lax.all_to_all(request, 'sp', 0, 0, tiled=True)  4.14 us
  transfers between devices with their start and end apart: 5, of which 3 were waited for; matrix products, arithmetic and copies ran while one was open for 0% of the time, Pallas kernels for 1%

profile of v5, /device:TPU:1, one launch (start us, length us, event | category | flops | bytes accessed | tf_op | source)
XLA Modules:
  0.0 153.6 jit_solution(2149133952725840644)
XLA Ops:
  0.0 0.0 copy-start.9
  0.0 0.0 copy-start.6
  0.0 2.3 %shard_map.136 = (f32[256,128]{1,0:T(8,128)}, s32[96]{0:T(128)}) custom-call(s32[1]{0:T(128)} %bitcast.2.part_ref, s32[6,16]{1,0:T(8,128)} %bitcast.26, f32[3,16,768]{2,1,0:T(8,128)} %points_ref.1), custom_call_target="tpu_custom_call" | custom-call | tf_op jit(solution)/shard_map/pallas_call | solution.py:336
  2.3 37.9 %all_to_all.25 = f32[128,2,128]{2,1,0:T(2,128)S(1)} all-to-all(f32[128,2,128]{2,1,0:T(2,128)} %bitcast.25), channel_id=1, replica_groups=mesh['seg_0'=4,'seg_1'=16,'seg_2'=2,'sp'=4] {'seg_0','seg_1','seg_2'}, dimensions={0} | all-to-all | bytes 262144 | tf_op jit(solution)/shard_map/all_to_all | solution.py:351
  40.2 0.0 copy-start.11
  40.2 0.8 broadcast_in_dim.20
  41.0 0.0 copy-start.12
  41.0 4.1 %all-to-all-start.1 = ((f32[4,256,128]{2,1,0:T(8,128)}), f32[4,256,128]{2,1,0:T(8,128)S(1)}, u32[]{:S(2)}, u32[]{:S(2)}) async-start(f32[4,256,128]{2,1,0:T(8,128)} %broadcast_in_dim.20), calls=%async_computation.1 | async-start | bytes 1048576 | tf_op jit(solution)/shard_map/all_to_all | solution.py:361
  45.2 0.0 copy-done.9
  45.2 0.0 copy-done.6
  45.2 0.7 shard_map.137.left_ref
  45.9 6.4 %all-to-all-done.1.request_ref = f32[4,256,128]{2,1,0:T(8,128)S(1)} async-done(((f32[4,256,128]{2,1,0:T(8,128)}), f32[4,256,128]{2,1,0:T(8,128)S(1)}, u32[]{:S(2)}, u32[]{:S(2)}) %all-to-all-start.1) | async-done | bytes 524320 | tf_op jit(solution)/shard_map/all_to_all | solution.py:361
  52.4 0.1 fusion.1.index_ref
  52.5 10.1 %shard_map.138 = f32[512,128]{1,0:T(8,128)S(1)} custom-call(s32[256]{0:T(256)S(1)} %fusion.1.index_ref, f32[4,256,128]{2,1,0:T(8,128)S(1)} %all-to-all-done.1.request_ref, bf16[16,64,256]{2,1,0:T(8,128)(2,1)S(1)} %shard_map.137.left_ref), custom_call_target="tpu_custom_call" | custom-call | tf_op jit(solution)/shard_map/pallas_call | solution.py:363
  62.6 31.0 %all_to_all.26 = f32[128,4,128]{2,1,0:T(4,128)S(1)} all-to-all(f32[128,4,128]{2,1,0:T(4,128)S(1)} %bitcast.17), channel_id=1, replica_groups=mesh['seg_0'=4,'seg_1'=16,'seg_2'=2,'sp'=4] {'seg_0','seg_1','seg_2'}, dimensions={0} | all-to-all | bytes 524288 | tf_op jit(solution)/shard_map/all_to_all | solution.py:375
  93.5 0.0 copy-done.11
  93.5 1.4 shard_map.139
  95.0 3.4 %all-to-all-start.3 = ((bf16[4,2,16,768]{3,2,1,0:T(8,128)(2,1)}), bf16[4,2,16,768]{3,2,1,0:T(8,128)(2,1)S(1)}, u32[]{:S(2)}, u32[]{:S(2)}) async-start(bf16[4,2,16,768]{3,2,1,0:T(8,128)(2,1)} %get-tuple-element.17), calls=%async_computation.3 | async-start | bytes 393216 | tf_op jit(solution)/shard_map/all_to_all | solution.py:393
  98.4 0.0 copy-done.12
  98.4 0.2 copy.16.up_ref
  98.5 0.0 copy-start
  98.6 1.6 %copy-done = f32[768,680]{0,1:T(8,128)S(1)} copy-done((f32[768,680]{0,1:T(8,128)S(1)}, f32[768,680]{0,1:T(8,128)}, u32[]{:S(2)}) %copy-start) | copy-done | bytes 2088984
  100.1 0.0 copy-start.4
  100.1 0.0 copy-start.5
  100.2 0.0 copy-start.10
  100.2 0.7 shard_map.140.fit_ref
  100.9 2.6 %all-to-all-done.3 = bf16[4,2,16,768]{3,2,1,0:T(8,128)(2,1)S(1)} async-done(((bf16[4,2,16,768]{3,2,1,0:T(8,128)(2,1)}), bf16[4,2,16,768]{3,2,1,0:T(8,128)(2,1)S(1)}, u32[]{:S(2)}, u32[]{:S(2)}) %all-to-all-start.3) | async-done | bytes 196640 | tf_op jit(solution)/shard_map/all_to_all | solution.py:393
  103.5 0.0 copy-done.4
  103.5 0.0 copy-done.5
  103.5 0.0 copy-done.7
  103.5 0.0 copy-done.8
  103.5 0.0 copy-done.10
  103.5 0.0 copy-start.1
  103.5 0.0 copy-start.2
  103.6 0.0 copy-start.3
  103.6 1.6 %shard_map.141 = (bf16[2,16,680]{2,1,0:T(8,128)(2,1)S(1)}, bf16[2,8,680]{2,1,0:T(8,128)(2,1)S(1)}, bf16[2,8,680]{2,1,0:T(8,128)(2,1)S(1)}, bf16[16,16,384]{2,1,0:T(8,128)(2,1)S(1)}, s32[24,48]{1,0:T(8,128)S(1)}) custom-call(s32[1]{0:T(128)} %bitcast.2.part_ref, s32[1]{0:T(128)} %bitcast.segment_ref, f32[8,8]{1,0:T(8,128)S(1)} %copy-done.10, ...), custom_call_target="tpu_custom_call" | custom-call | tf_op jit(solution)/shard_map/pallas_call | solution.py:399
  105.2 16.5 %all_to_all.27 = bf16[16,16,384]{2,1,0:T(8,128)(2,1)S(1)} all-to-all(bf16[16,16,384]{2,1,0:T(8,128)(2,1)S(1)} %get-tuple-element.22), channel_id=1, replica_groups=mesh['seg_0'=4,'seg_1'=16,'seg_2'=2,'sp'=4] {'seg_1'}, dimensions={0} | all-to-all | bytes 393216 | tf_op jit(solution)/shard_map/all_to_all | solution.py:420
  121.7 11.8 %all_gather.3.mine_ref = bf16[1024,384]{1,0:T(8,128)(2,1)S(1)} all-gather(bf16[256,384]{1,0:T(8,128)(2,1)S(1)} %bitcast.23), channel_id=1, replica_groups=mesh['seg_0'=4,'seg_1'=16,'seg_2'=2,'sp'=4] {'seg_0'}, dimensions={0}, use_global_device_ids=true | all-gather | bytes 983040 | tf_op jit(solution)/shard_map/all_gather | solution.py:421
  133.4 9.4 %collective-permute-start.2 = (bf16[1024,384]{1,0:T(8,128)(2,1)S(1)}, bf16[1024,384]{1,0:T(8,128)(2,1)S(1)}, u32[]{:S(2)}, u32[]{:S(2)}) collective-permute-start(bf16[1024,384]{1,0:T(8,128)(2,1)S(1)} %all_gather.3.mine_ref), channel_id=1, source_target_pairs={{0,4},{4,0},{1,5},{5,1},{2,6},{6,2},{3,7},{7,3},{8,12},{12,8},{9,1... | collective-permute-start | bytes 2359304 | tf_op jit(solution)/shard_map/ppermute | solution.py:422
  142.8 2.8 %collective-permute-start = (bf16[2,8,680]{2,1,0:T(8,128)(2,1)S(1)}, bf16[2,8,680]{2,1,0:T(8,128)(2,1)S(1)}, u32[]{:S(2)}, u32[]{:S(2)}) collective-permute-start(bf16[2,8,680]{2,1,0:T(8,128)(2,1)S(1)} %get-tuple-element.18), channel_id=1, source_target_pairs={{0,4},{4,8},{8,12},{12,16},{16,20},{20,24},{24,28},{28,32},{32,36}... | collective-permute-start | bytes 65288 | tf_op jit(solution)/shard_map/ppermute | solution.py:418
  145.6 1.9 %collective-permute-start.1 = (bf16[2,8,680]{2,1,0:T(8,128)(2,1)S(1)}, bf16[2,8,680]{2,1,0:T(8,128)(2,1)S(1)}, u32[]{:S(2)}, u32[]{:S(2)}) collective-permute-start(bf16[2,8,680]{2,1,0:T(8,128)(2,1)S(1)} %get-tuple-element.20), channel_id=1, source_target_pairs={{4,0},{8,4},{12,8},{16,12},{20,16},{24,20},{28,24},{32,28},{36,32}... | collective-permute-start | bytes 65288 | tf_op jit(solution)/shard_map/ppermute | solution.py:419
  147.5 0.0 collective-permute-done.before_ref
  147.5 3.2 %collective-permute-done.1.after_ref = bf16[2,8,680]{2,1,0:T(8,128)(2,1)S(1)} collective-permute-done((bf16[2,8,680]{2,1,0:T(8,128)(2,1)S(1)}, bf16[2,8,680]{2,1,0:T(8,128)(2,1)S(1)}, u32[]{:S(2)}, u32[]{:S(2)}) %collective-permute-start.1) | collective-permute-done | bytes 21792 | tf_op jit(solution)/shard_map/ppermute | solution.py:419
  150.8 0.0 collective-permute-done.2.other_ref
  150.8 0.0 copy-done.1
  150.8 0.0 copy-done.2
  150.8 0.0 copy-done.3
  150.8 2.8 %shard_map.142 = f32[2,24,680]{2,1,0:T(8,128)} custom-call(s32[1]{0:T(128)} %bitcast.segment_ref, s32[1]{0:T(128)} %bitcast.1.core_ref, bf16[2,8,680]{2,1,0:T(8,128)(2,1)S(1)} %collective-permute-done.before_ref, bf16[2,16,680]{2,1,0:T(8,128)(2,1)S(1)} %get-tuple-element.19.ghosts_ref, bf16[2,8,680]{2,1,0:T(8,128)(2,1)S(1)} %collective-permute-done.1.after_ref, ...), custom_call_target="tpu_custom_call" | custom-call | tf_op jit(solution)/shard_map/pallas_call | solution.py:424
  (2 shorter events, 0.0 us)
Async XLA Ops:
  0.0 45.2 %copy-start.9 = (s32[1,1920]{1,0:T(1,128)S(1)}, s32[1,1920]{1,0:T(1,128)}, u32[]{:S(2)}) copy-start(s32[1,1920]{1,0:T(1,128)} %constant.28.clone.table_ref) | copy-start | bytes 23044
  0.0 45.2 %copy-start.6 = (f32[2,16,680]{2,1,0:T(8,128)S(1)}, f32[2,16,680]{2,1,0:T(8,128)}, u32[]{:S(2)}) copy-start(f32[2,16,680]{2,1,0:T(8,128)} %coeffs_ref.1) | copy-start | bytes 261124
  40.2 53.3 %copy-start.11 = (s32[96]{0:T(128)S(1)}, s32[96]{0:T(128)}, u32[]{:S(2)}) copy-start(s32[96]{0:T(128)} %get-tuple-element.14.place_ref) | copy-start | bytes 1156
  41.0 57.3 %copy-start.12 = (bf16[680,152]{0,1:T(8,128)(2,1)S(1)}, bf16[680,152]{0,1:T(8,128)(2,1)}, u32[]{:S(2)}) copy-start(bf16[680,152]{0,1:T(8,128)(2,1)} %param.23) | copy-start | bytes 620164
  41.0 11.3 %all-to-all-start.1 = ((f32[4,256,128]{2,1,0:T(8,128)}), f32[4,256,128]{2,1,0:T(8,128)S(1)}, u32[]{:S(2)}, u32[]{:S(2)}) async-start(f32[4,256,128]{2,1,0:T(8,128)} %broadcast_in_dim.20), calls=%async_computation.1 | async-start | bytes 1048576 | tf_op jit(solution)/shard_map/all_to_all | solution.py:361
  95.0 8.5 %all-to-all-start.3 = ((bf16[4,2,16,768]{3,2,1,0:T(8,128)(2,1)}), bf16[4,2,16,768]{3,2,1,0:T(8,128)(2,1)S(1)}, u32[]{:S(2)}, u32[]{:S(2)}) async-start(bf16[4,2,16,768]{3,2,1,0:T(8,128)(2,1)} %get-tuple-element.17), calls=%async_computation.3 | async-start | bytes 393216 | tf_op jit(solution)/shard_map/all_to_all | solution.py:393
  98.5 1.6 %copy-start = (f32[768,680]{0,1:T(8,128)S(1)}, f32[768,680]{0,1:T(8,128)}, u32[]{:S(2)}) copy-start(f32[768,680]{0,1:T(8,128)} %param.18) | copy-start | bytes 6266884
  100.1 3.4 %copy-start.4 = (s32[2048,16]{0,1:T(8,128)S(1)}, s32[2048,16]{0,1:T(8,128)}, u32[]{:S(2)}) copy-start(s32[2048,16]{0,1:T(8,128)} %param.20) | copy-start | bytes 393220
  100.1 3.4 %copy-start.5 = (s32[2048,16]{0,1:T(8,128)S(1)}, s32[2048,16]{0,1:T(8,128)}, u32[]{:S(2)}) copy-start(s32[2048,16]{0,1:T(8,128)} %param.21) | copy-start | bytes 393220
  100.1 3.4 %copy-start.7 = (s32[2048,8]{0,1:T(8,128)S(1)}, s32[2048,8]{0,1:T(8,128)}, u32[]{:S(2)}) copy-start(s32[2048,8]{0,1:T(8,128)} %param.24) | copy-start | bytes 196612
  100.1 3.4 %copy-start.8 = (s32[2048]{0:T(1024)S(1)}, s32[2048]{0:T(1024)}, u32[]{:S(2)}) copy-start(s32[2048]{0:T(1024)} %param.19) | copy-start | bytes 24580
  100.2 3.4 %copy-start.10 = (f32[8,8]{1,0:T(8,128)S(1)}, f32[8,8]{1,0:T(8,128)}, u32[]{:S(2)}) copy-start(f32[8,8]{1,0:T(8,128)} %reaction_ref.1) | copy-start | bytes 772
  103.5 47.2 %copy-start.1 = (bf16[2,680,680]{2,1,0:T(8,128)(2,1)S(1)}, bf16[2,680,680]{2,1,0:T(8,128)(2,1)}, u32[]{:S(2)}) copy-start(bf16[2,680,680]{2,1,0:T(8,128)(2,1)} %near_mat_ref.1) | copy-start | bytes 5548804
  103.5 47.2 %copy-start.2 = (bf16[8,152,152]{2,1,0:T(8,128)(2,1)S(1)}, bf16[8,152,152]{2,1,0:T(8,128)(2,1)}, u32[]{:S(2)}) copy-start(bf16[8,152,152]{2,1,0:T(8,128)(2,1)} %trans_ref.1) | copy-start | bytes 1108996
  103.6 47.2 %copy-start.3 = (bf16[152,680]{1,0:T(8,128)(2,1)S(1)}, bf16[152,680]{1,0:T(8,128)(2,1)}, u32[]{:S(2)}) copy-start(bf16[152,680]{1,0:T(8,128)(2,1)} %down_ref.1) | copy-start | bytes 620164
  133.4 17.3 %collective-permute-start.2 = (bf16[1024,384]{1,0:T(8,128)(2,1)S(1)}, bf16[1024,384]{1,0:T(8,128)(2,1)S(1)}, u32[]{:S(2)}, u32[]{:S(2)}) collective-permute-start(bf16[1024,384]{1,0:T(8,128)(2,1)S(1)} %all_gather.3.mine_ref), channel_id=1, source_target_pairs={{0,4},{4,0},{1,5},{5,1},{2,6},{6,2},{3,7},{7,3},{8,12},{12,8},{9,1... | collective-permute-start | bytes 2359304 | tf_op jit(solution)/shard_map/ppermute | solution.py:422
  142.8 4.7 %collective-permute-start = (bf16[2,8,680]{2,1,0:T(8,128)(2,1)S(1)}, bf16[2,8,680]{2,1,0:T(8,128)(2,1)S(1)}, u32[]{:S(2)}, u32[]{:S(2)}) collective-permute-start(bf16[2,8,680]{2,1,0:T(8,128)(2,1)S(1)} %get-tuple-element.18), channel_id=1, source_target_pairs={{0,4},{4,8},{8,12},{12,16},{16,20},{20,24},{24,28},{28,32},{32,36}... | collective-permute-start | bytes 65288 | tf_op jit(solution)/shard_map/ppermute | solution.py:418
  145.6 5.1 %collective-permute-start.1 = (bf16[2,8,680]{2,1,0:T(8,128)(2,1)S(1)}, bf16[2,8,680]{2,1,0:T(8,128)(2,1)S(1)}, u32[]{:S(2)}, u32[]{:S(2)}) collective-permute-start(bf16[2,8,680]{2,1,0:T(8,128)(2,1)S(1)} %get-tuple-element.20), channel_id=1, source_target_pairs={{4,0},{8,4},{12,8},{16,12},{20,16},{24,20},{28,24},{32,28},{36,32}... | collective-permute-start | bytes 65288 | tf_op jit(solution)/shard_map/ppermute | solution.py:419

commit v6 on v5

--- a/solution.py
+++ b/solution.py
@@ -216,8 +216,9 @@
     first = jnp.dot(stacked, fit_ref[0], preferred_element_type=F32)
     second = jnp.dot(high, fit_ref[1], preferred_element_type=F32)
     ghosts = (first[:rows] + first[rows:] + second).astype(BF16)
-    equivalent = jnp.dot(ghosts, up_ref[...], preferred_element_type=F32).astype(BF16)
-    points = up_ref.shape[1]
+    turned = (((1,), (1,)), ((), ()))
+    equivalent = lax.dot_general(ghosts, up_ref[...], turned, preferred_element_type=F32).astype(BF16)
+    points = up_ref.shape[0]
     for s in range(species):
         here = ghosts[s * leaves : (s + 1) * leaves]
         ghosts_ref[s] = here
@@ -409,7 +410,7 @@
         ],
         compiler_params=within(24),
     )(
-        part_id, segment_id, reaction, own, gathered, fit_parts, up_mat, near_src.T, near_op.T, far_src.T,
+        part_id, segment_id, reaction, own, gathered, fit_parts, up_mat.T, near_src.T, near_op.T, far_src.T,
         new_seg.reshape(1, -1),
     )
 

time: 154 us -> 154 us (level)
  no operation moved by 1% of the time
where the time goes in v6:
time: 154 us; the launch traced here: 153 us
  blocking collectives  97.1 us (63%)
  starting transfers between devices  21.5 us (14%)
  Pallas kernels  19.7 us (13%)
  waiting for transfers between devices  12.5 us (8%)
  local copies, waits for them, and re-layouts  2.47 us (2%)
    all_to_all x1, blocking collectives, shards(): lax.all_to_all(request.reshape(segments, CAP, PB), SEG, 0, 0, tiled=True)  37.9 us
    all_to_all x1, blocking collectives, shards(): lax.all_to_all(answers.reshape(segments, CAP * species, PB), SEG, 0, 0, t...  31 us
    all_to_all x1, blocking collectives, shards(): along_z = lax.all_to_all(spread, 'seg_1', 0, 0, tiled=True)  16.5 us
    all_gather x1, blocking collectives, shards(): lax.all_gather(along_z.reshape(z_size * leaves, LANES), 'seg_0', axis=0,...  11.8 us
    pallas_call x1, Pallas kernels, shards(): pl.pallas_call(functools.partial(evaluate_kernel, species), out_shape=sha...  10.1 us
    ppermute x1, starting transfers between devices, shards(): other = lax.ppermute(mine, 'seg_2', [(0, 1), (1, 0)])  9.41 us
    all_to_all x1, waiting for transfers between devices, shards(): request = lax.all_to_all(request, 'sp', 0, 0, tiled=True)  6.44 us
    all_to_all x1, starting transfers between devices, shards(): request = lax.all_to_all(request, 'sp', 0, 0, tiled=True)  4.01 us
  transfers between devices with their start and end apart: 5, of which 3 were waited for; matrix products, arithmetic and copies ran while one was open for 0% of the time, Pallas kernels for 1%

profile of v6, /device:TPU:1, one launch (start us, length us, event | category | flops | bytes accessed | tf_op | source)
XLA Modules:
  0.0 153.4 jit_solution(18113323838582518247)
XLA Ops:
  0.0 0.0 copy-start.10
  0.0 0.0 copy-start.7
  0.0 2.3 %shard_map.136 = (f32[256,128]{1,0:T(8,128)}, s32[96]{0:T(128)}) custom-call(s32[1]{0:T(128)} %bitcast.2.part_ref, s32[6,16]{1,0:T(8,128)} %bitcast.28, f32[3,16,768]{2,1,0:T(8,128)} %points_ref.1), custom_call_target="tpu_custom_call" | custom-call | tf_op jit(solution)/shard_map/pallas_call | solution.py:337
  2.3 37.9 %all_to_all.25 = f32[128,2,128]{2,1,0:T(2,128)S(1)} all-to-all(f32[128,2,128]{2,1,0:T(2,128)} %bitcast.27), channel_id=1, replica_groups=mesh['seg_0'=4,'seg_1'=16,'seg_2'=2,'sp'=4] {'seg_0','seg_1','seg_2'}, dimensions={0} | all-to-all | bytes 262144 | tf_op jit(solution)/shard_map/all_to_all | solution.py:352
  40.2 0.0 copy-start.12
  40.2 0.8 broadcast_in_dim.20
  41.0 4.0 %all-to-all-start.1 = ((f32[4,256,128]{2,1,0:T(8,128)}), f32[4,256,128]{2,1,0:T(8,128)S(1)}, u32[]{:S(2)}, u32[]{:S(2)}) async-start(f32[4,256,128]{2,1,0:T(8,128)} %broadcast_in_dim.20), calls=%async_computation.1 | async-start | bytes 1048576 | tf_op jit(solution)/shard_map/all_to_all | solution.py:362
  45.1 0.0 copy-done.10
  45.1 0.0 copy-done.7
  45.1 0.7 shard_map.137.left_ref
  45.8 6.4 %all-to-all-done.1.request_ref = f32[4,256,128]{2,1,0:T(8,128)S(1)} async-done(((f32[4,256,128]{2,1,0:T(8,128)}), f32[4,256,128]{2,1,0:T(8,128)S(1)}, u32[]{:S(2)}, u32[]{:S(2)}) %all-to-all-start.1) | async-done | bytes 524320 | tf_op jit(solution)/shard_map/all_to_all | solution.py:362
  52.2 0.1 fusion.1.index_ref
  52.3 10.1 %shard_map.138 = f32[512,128]{1,0:T(8,128)S(1)} custom-call(s32[256]{0:T(256)S(1)} %fusion.1.index_ref, f32[4,256,128]{2,1,0:T(8,128)S(1)} %all-to-all-done.1.request_ref, bf16[16,64,256]{2,1,0:T(8,128)(2,1)S(1)} %shard_map.137.left_ref), custom_call_target="tpu_custom_call" | custom-call | tf_op jit(solution)/shard_map/pallas_call | solution.py:364
  62.4 31.0 %all_to_all.26 = f32[128,4,128]{2,1,0:T(4,128)S(1)} all-to-all(f32[128,4,128]{2,1,0:T(4,128)S(1)} %bitcast.18), channel_id=1, replica_groups=mesh['seg_0'=4,'seg_1'=16,'seg_2'=2,'sp'=4] {'seg_0','seg_1','seg_2'}, dimensions={0} | all-to-all | bytes 524288 | tf_op jit(solution)/shard_map/all_to_all | solution.py:376
  93.4 0.0 copy-done.12
  93.4 1.4 shard_map.139
  94.9 3.4 %all-to-all-start.3 = ((bf16[4,2,16,768]{3,2,1,0:T(8,128)(2,1)}), bf16[4,2,16,768]{3,2,1,0:T(8,128)(2,1)S(1)}, u32[]{:S(2)}, u32[]{:S(2)}) async-start(bf16[4,2,16,768]{3,2,1,0:T(8,128)(2,1)} %get-tuple-element.17), calls=%async_computation.3 | async-start | bytes 393216 | tf_op jit(solution)/shard_map/all_to_all | solution.py:394
  98.2 0.0 copy-start
  98.2 1.6 %copy-done = f32[768,680]{0,1:T(8,128)S(1)} copy-done((f32[768,680]{0,1:T(8,128)S(1)}, f32[768,680]{0,1:T(8,128)}, u32[]{:S(2)}) %copy-start) | copy-done | bytes 2088984
  99.8 0.0 copy-start.3
  99.8 0.0 copy-start.5
  99.8 0.0 copy-start.6
  99.8 0.0 copy-start.9
  99.8 0.0 copy-start.11
  99.9 0.7 shard_map.140.fit_ref
  100.6 2.8 %all-to-all-done.3 = bf16[4,2,16,768]{3,2,1,0:T(8,128)(2,1)S(1)} async-done(((bf16[4,2,16,768]{3,2,1,0:T(8,128)(2,1)}), bf16[4,2,16,768]{3,2,1,0:T(8,128)(2,1)S(1)}, u32[]{:S(2)}, u32[]{:S(2)}) %all-to-all-start.3) | async-done | bytes 196640 | tf_op jit(solution)/shard_map/all_to_all | solution.py:394
  103.4 0.0 copy-done.3
  103.4 0.0 copy-done.5
  103.4 0.0 copy-done.6
  103.4 0.0 copy-done.8
  103.4 0.0 copy-done.9
  103.4 0.0 copy-done.11
  103.4 0.0 copy-start.1
  103.4 0.0 copy-start.2
  103.4 0.0 copy-start.4
  103.4 1.6 %shard_map.141 = (bf16[2,16,680]{2,1,0:T(8,128)(2,1)S(1)}, bf16[2,8,680]{2,1,0:T(8,128)(2,1)S(1)}, bf16[2,8,680]{2,1,0:T(8,128)(2,1)S(1)}, bf16[16,16,384]{2,1,0:T(8,128)(2,1)S(1)}, s32[24,48]{1,0:T(8,128)S(1)}) custom-call(s32[1]{0:T(128)} %bitcast.2.part_ref, s32[1]{0:T(128)} %bitcast.segment_ref, f32[8,8]{1,0:T(8,128)S(1)} %copy-done.11, ...), custom_call_target="tpu_custom_call" | custom-call | tf_op jit(solution)/shard_map/pallas_call | solution.py:400
  105.1 16.5 %all_to_all.27 = bf16[16,16,384]{2,1,0:T(8,128)(2,1)S(1)} all-to-all(bf16[16,16,384]{2,1,0:T(8,128)(2,1)S(1)} %get-tuple-element.22), channel_id=1, replica_groups=mesh['seg_0'=4,'seg_1'=16,'seg_2'=2,'sp'=4] {'seg_1'}, dimensions={0} | all-to-all | bytes 393216 | tf_op jit(solution)/shard_map/all_to_all | solution.py:421
  121.5 11.8 %all_gather.3.mine_ref = bf16[1024,384]{1,0:T(8,128)(2,1)S(1)} all-gather(bf16[256,384]{1,0:T(8,128)(2,1)S(1)} %bitcast.25), channel_id=1, replica_groups=mesh['seg_0'=4,'seg_1'=16,'seg_2'=2,'sp'=4] {'seg_0'}, dimensions={0}, use_global_device_ids=true | all-gather | bytes 983040 | tf_op jit(solution)/shard_map/all_gather | solution.py:422
  133.3 9.4 %collective-permute-start.2 = (bf16[1024,384]{1,0:T(8,128)(2,1)S(1)}, bf16[1024,384]{1,0:T(8,128)(2,1)S(1)}, u32[]{:S(2)}, u32[]{:S(2)}) collective-permute-start(bf16[1024,384]{1,0:T(8,128)(2,1)S(1)} %all_gather.3.mine_ref), channel_id=1, source_target_pairs={{0,4},{4,0},{1,5},{5,1},{2,6},{6,2},{3,7},{7,3},{8,12},{12,8},{9,1... | collective-permute-start | bytes 2359304 | tf_op jit(solution)/shard_map/ppermute | solution.py:423
  142.7 2.8 %collective-permute-start = (bf16[2,8,680]{2,1,0:T(8,128)(2,1)S(1)}, bf16[2,8,680]{2,1,0:T(8,128)(2,1)S(1)}, u32[]{:S(2)}, u32[]{:S(2)}) collective-permute-start(bf16[2,8,680]{2,1,0:T(8,128)(2,1)S(1)} %get-tuple-element.18), channel_id=1, source_target_pairs={{0,4},{4,8},{8,12},{12,16},{16,20},{20,24},{24,28},{28,32},{32,36}... | collective-permute-start | bytes 65288 | tf_op jit(solution)/shard_map/ppermute | solution.py:419
  145.5 1.9 %collective-permute-start.1 = (bf16[2,8,680]{2,1,0:T(8,128)(2,1)S(1)}, bf16[2,8,680]{2,1,0:T(8,128)(2,1)S(1)}, u32[]{:S(2)}, u32[]{:S(2)}) collective-permute-start(bf16[2,8,680]{2,1,0:T(8,128)(2,1)S(1)} %get-tuple-element.20), channel_id=1, source_target_pairs={{4,0},{8,4},{12,8},{16,12},{20,16},{24,20},{28,24},{32,28},{36,32}... | collective-permute-start | bytes 65288 | tf_op jit(solution)/shard_map/ppermute | solution.py:420
  147.4 0.0 collective-permute-done.before_ref
  147.4 3.2 %collective-permute-done.1.after_ref = bf16[2,8,680]{2,1,0:T(8,128)(2,1)S(1)} collective-permute-done((bf16[2,8,680]{2,1,0:T(8,128)(2,1)S(1)}, bf16[2,8,680]{2,1,0:T(8,128)(2,1)S(1)}, u32[]{:S(2)}, u32[]{:S(2)}) %collective-permute-start.1) | collective-permute-done | bytes 21792 | tf_op jit(solution)/shard_map/ppermute | solution.py:420
  150.6 0.0 collective-permute-done.2.other_ref
  150.6 0.0 copy-done.1
  150.6 0.0 copy-done.2
  150.6 0.0 copy-done.4
  150.6 2.8 %shard_map.142 = f32[2,24,680]{2,1,0:T(8,128)} custom-call(s32[1]{0:T(128)} %bitcast.segment_ref, s32[1]{0:T(128)} %bitcast.1.core_ref, bf16[2,8,680]{2,1,0:T(8,128)(2,1)S(1)} %collective-permute-done.before_ref, bf16[2,16,680]{2,1,0:T(8,128)(2,1)S(1)} %get-tuple-element.19.ghosts_ref, bf16[2,8,680]{2,1,0:T(8,128)(2,1)S(1)} %collective-permute-done.1.after_ref, ...), custom_call_target="tpu_custom_call" | custom-call | tf_op jit(solution)/shard_map/pallas_call | solution.py:425
  (1 shorter events, 0.0 us)
Async XLA Ops:
  0.0 45.1 %copy-start.10 = (s32[1,1920]{1,0:T(1,128)S(1)}, s32[1,1920]{1,0:T(1,128)}, u32[]{:S(2)}) copy-start(s32[1,1920]{1,0:T(1,128)} %constant.28.clone.table_ref) | copy-start | bytes 23044
  0.0 45.1 %copy-start.7 = (f32[2,16,680]{2,1,0:T(8,128)S(1)}, f32[2,16,680]{2,1,0:T(8,128)}, u32[]{:S(2)}) copy-start(f32[2,16,680]{2,1,0:T(8,128)} %coeffs_ref.1) | copy-start | bytes 261124
  40.2 53.2 %copy-start.12 = (s32[96]{0:T(128)S(1)}, s32[96]{0:T(128)}, u32[]{:S(2)}) copy-start(s32[96]{0:T(128)} %get-tuple-element.14.place_ref) | copy-start | bytes 1156
  41.0 11.2 %all-to-all-start.1 = ((f32[4,256,128]{2,1,0:T(8,128)}), f32[4,256,128]{2,1,0:T(8,128)S(1)}, u32[]{:S(2)}, u32[]{:S(2)}) async-start(f32[4,256,128]{2,1,0:T(8,128)} %broadcast_in_dim.20), calls=%async_computation.1 | async-start | bytes 1048576 | tf_op jit(solution)/shard_map/all_to_all | solution.py:362
  94.9 8.5 %all-to-all-start.3 = ((bf16[4,2,16,768]{3,2,1,0:T(8,128)(2,1)}), bf16[4,2,16,768]{3,2,1,0:T(8,128)(2,1)S(1)}, u32[]{:S(2)}, u32[]{:S(2)}) async-start(bf16[4,2,16,768]{3,2,1,0:T(8,128)(2,1)} %get-tuple-element.17), calls=%async_computation.3 | async-start | bytes 393216 | tf_op jit(solution)/shard_map/all_to_all | solution.py:394
  98.2 1.6 %copy-start = (f32[768,680]{0,1:T(8,128)S(1)}, f32[768,680]{0,1:T(8,128)}, u32[]{:S(2)}) copy-start(f32[768,680]{0,1:T(8,128)} %param.18) | copy-start | bytes 6266884
  99.8 3.5 %copy-start.3 = (bf16[680,152]{0,1:T(8,128)(2,1)S(1)}, bf16[680,152]{0,1:T(8,128)(2,1)}, u32[]{:S(2)}) copy-start(bf16[680,152]{0,1:T(8,128)(2,1)} %param.23) | copy-start | bytes 620164
  99.8 3.5 %copy-start.5 = (s32[2048,16]{0,1:T(8,128)S(1)}, s32[2048,16]{0,1:T(8,128)}, u32[]{:S(2)}) copy-start(s32[2048,16]{0,1:T(8,128)} %param.20) | copy-start | bytes 393220
  99.8 3.5 %copy-start.6 = (s32[2048,16]{0,1:T(8,128)S(1)}, s32[2048,16]{0,1:T(8,128)}, u32[]{:S(2)}) copy-start(s32[2048,16]{0,1:T(8,128)} %param.21) | copy-start | bytes 393220
  99.8 3.5 %copy-start.8 = (s32[2048,8]{0,1:T(8,128)S(1)}, s32[2048,8]{0,1:T(8,128)}, u32[]{:S(2)}) copy-start(s32[2048,8]{0,1:T(8,128)} %param.24) | copy-start | bytes 196612
  99.8 3.6 %copy-start.9 = (s32[2048]{0:T(1024)S(1)}, s32[2048]{0:T(1024)}, u32[]{:S(2)}) copy-start(s32[2048]{0:T(1024)} %param.19) | copy-start | bytes 24580
  99.8 3.6 %copy-start.11 = (f32[8,8]{1,0:T(8,128)S(1)}, f32[8,8]{1,0:T(8,128)}, u32[]{:S(2)}) copy-start(f32[8,8]{1,0:T(8,128)} %reaction_ref.1) | copy-start | bytes 772
  103.4 47.2 %copy-start.1 = (bf16[2,680,680]{2,1,0:T(8,128)(2,1)S(1)}, bf16[2,680,680]{2,1,0:T(8,128)(2,1)}, u32[]{:S(2)}) copy-start(bf16[2,680,680]{2,1,0:T(8,128)(2,1)} %near_mat_ref.1) | copy-start | bytes 5548804
  103.4 47.2 %copy-start.2 = (bf16[8,152,152]{2,1,0:T(8,128)(2,1)S(1)}, bf16[8,152,152]{2,1,0:T(8,128)(2,1)}, u32[]{:S(2)}) copy-start(bf16[8,152,152]{2,1,0:T(8,128)(2,1)} %trans_ref.1) | copy-start | bytes 1108996
  103.4 47.2 %copy-start.4 = (bf16[152,680]{1,0:T(8,128)(2,1)S(1)}, bf16[152,680]{1,0:T(8,128)(2,1)}, u32[]{:S(2)}) copy-start(bf16[152,680]{1,0:T(8,128)(2,1)} %down_ref.1) | copy-start | bytes 620164
  133.3 17.3 %collective-permute-start.2 = (bf16[1024,384]{1,0:T(8,128)(2,1)S(1)}, bf16[1024,384]{1,0:T(8,128)(2,1)S(1)}, u32[]{:S(2)}, u32[]{:S(2)}) collective-permute-start(bf16[1024,384]{1,0:T(8,128)(2,1)S(1)} %all_gather.3.mine_ref), channel_id=1, source_target_pairs={{0,4},{4,0},{1,5},{5,1},{2,6},{6,2},{3,7},{7,3},{8,12},{12,8},{9,1... | collective-permute-start | bytes 2359304 | tf_op jit(solution)/shard_map/ppermute | solution.py:423
  142.7 4.7 %collective-permute-start = (bf16[2,8,680]{2,1,0:T(8,128)(2,1)S(1)}, bf16[2,8,680]{2,1,0:T(8,128)(2,1)S(1)}, u32[]{:S(2)}, u32[]{:S(2)}) collective-permute-start(bf16[2,8,680]{2,1,0:T(8,128)(2,1)S(1)} %get-tuple-element.18), channel_id=1, source_target_pairs={{0,4},{4,8},{8,12},{12,16},{16,20},{20,24},{24,28},{28,32},{32,36}... | collective-permute-start | bytes 65288 | tf_op jit(solution)/shard_map/ppermute | solution.py:419
  145.5 5.1 %collective-permute-start.1 = (bf16[2,8,680]{2,1,0:T(8,128)(2,1)S(1)}, bf16[2,8,680]{2,1,0:T(8,128)(2,1)S(1)}, u32[]{:S(2)}, u32[]{:S(2)}) collective-permute-start(bf16[2,8,680]{2,1,0:T(8,128)(2,1)S(1)} %get-tuple-element.20), channel_id=1, source_target_pairs={{4,0},{8,4},{12,8},{16,12},{20,16},{24,20},{28,24},{32,28},{36,32}... | collective-permute-start | bytes 65288 | tf_op jit(solution)/shard_map/ppermute | solution.py:420
